TPU v7x, 256 devices: a 4x2x16 block of a 4x16x16 slice. The times are simulated.
256 devices in a mesh: groups: 2 (over y), dp: 16 (over z), tensor: 4 (over x), seq: 2 (over core).
Axes of the slice: x: 4, y: 2, z: 16, core: 2. Of those that a mesh axis runs over, the one named last changes fastest.
The devices are a block of a 4x16x16 slice.
Arguments:
- hidden: bfloat16 [1024, 64, 8192], P(('groups', 'dp', 'seq'), None, 'tensor'), parts along dimension 0, may hold values from -6 to 6
- lengths: int32 [1024], P(('groups', 'dp', 'seq')), parts along dimension 0, may hold values from 2 to 64
- answers: int32 [1024], P(('groups', 'dp', 'seq')), parts along dimension 0, may hold values from 0 to 63
- prompt_of: int32 [1024], P(('groups', 'dp', 'seq')), parts along dimension 0, may hold values from 0 to 31, as said below
- query_weight: bfloat16 [8192, 4096], P(('tensor', 'dp'))
- key_weight: bfloat16 [8192, 512], P('tensor')
- value_weight: bfloat16 [8192, 512], P('tensor'), may hold values from -0.0625 to 0.0625
- score_vec: float32 [4096], replicated, may hold values from -0.75 to 0.75
Outputs:
- vote_share: float32 [64, 64], P(('groups', 'dp')), parts along dimension 0
There are 2 independent parts, one for each index of `groups`. A program takes and returns all parts, laid end to end along the dimension named above; an argument that names none is the same for every part. Nothing has to cross between parts.
Inputs may be any that keep to these rules, and one draw needn't show every extreme that they name: `prompt_of`: every prompt has exactly 16 samples. In every aligned block of 16 samples, exactly one sample belongs to each pair of prompts 2k and 2k + 1.
All inputs are finite; a program needn't handle non-finite values.
Results may differ from a plain program's by a relative error of at most 0.003.
Values may be sent and summed in bfloat16 or wider, within the bound.
No kernel may reach another device: no remote copies, remote signals or barrier semaphores. Data moves between devices by JAX's collectives and lax.ppermute only.
A program may use at most 64 MiB of HBM per device.

v0:
```python
import math

import jax
import jax.numpy as jnp
from jax import lax
from jax.sharding import PartitionSpec as P

HEAD_SIZE = 128
QUERY_HEADS = 32
KEY_VALUE_HEADS = 4
ANSWERS = 64
PROMPT_DEV = 2


rope_base = 500000.0


def from_everyone(shard, axis):
    count = lax.axis_size(axis)
    return lax.all_to_all(
        jnp.broadcast_to(shard[None], (count, *shard.shape)), axis, 0, 0, tiled=True
    )


def of_everyone(shard, axis):
    everything = from_everyone(shard, axis)
    return jnp.sum(everything, axis=0)


def cut_along(shard, dim, count):
    lengths = shard.shape
    tiles = shard.reshape(*lengths[:dim], count, lengths[dim] // count, *lengths[dim + 1 :])
    return jnp.moveaxis(tiles, dim, 0)


def summed_on_arrival(shard, axis, dim):
    tiles = cut_along(shard, dim, lax.axis_size(axis))
    arrived = lax.all_to_all(tiles, axis, split_axis=0, concat_axis=0, tiled=True)
    return arrived.sum(axis=0)


def all_in_one(shard, axis):
    leaves = jax.tree.leaves(shard)
    order = sorted(range(len(leaves)), key=lambda k: -leaves[k].size)
    width = (1, *leaves[order[0]].shape)[-1]
    lines = [
        jnp.pad(leaves[k].reshape(-1), (0, -leaves[k].size % width)).reshape(-1, width)
        for k in order
    ]
    both, at, found = (from_everyone(jnp.concatenate(lines), axis), 0, {})
    for k, line in zip(order, lines):
        slab = both[:, at : at + len(line)].reshape(len(both), -1)
        found[k] = slab[:, : leaves[k].size].reshape(-1, *leaves[k].shape)
        at += len(line)
    numbers = iter(range(len(leaves)))
    return jax.tree.map(lambda _: found[next(numbers)], shard)


def joined_by_halves(pieces, combine):
    while len(jax.tree.leaves(pieces)[0]) > 1:
        pieces = jax.vmap(combine)(
            *(jax.tree.map(lambda part: part[side::2], pieces) for side in (0, 1))
        )
    return jax.tree.map(lambda part: part[0], pieces)


def combined_all(shard, axis, combine):
    pieces = all_in_one(shard, axis)
    return joined_by_halves(pieces, combine)


def gathered_total(shard, axis):
    tiles = lax.all_gather(shard, axis)
    return tiles.sum(axis=0)


def rotate(vectors, positions):
    halves = vectors.shape[-1] // 2
    frequency = rope_base ** (-jnp.arange(halves, dtype=jnp.float32) * 2.0 / vectors.shape[-1])
    angles = positions[..., None] * frequency
    cosine = jnp.cos(angles)
    sine_part = jnp.sin(angles)
    first_half = vectors[..., :halves]
    second_half = vectors[..., halves:]
    return jnp.concatenate(
        [
            first_half * cosine - second_half * sine_part,
            second_half * cosine + first_half * sine_part,
        ],
        -1,
    )


def combine_soft(earlier, later):
    row_maximum = jnp.maximum(earlier[0], later[0])
    scale_one = jnp.exp(earlier[0] - row_maximum)
    scale_two = jnp.exp(later[0] - row_maximum)
    softmax_sum = earlier[1] * scale_one + later[1] * scale_two
    weighted_values = earlier[2] * scale_one[..., None] + later[2] * scale_two[..., None]
    return (row_maximum, softmax_sum, weighted_values)


def shards(hidden, lengths, answers, prompt_of, query_weight, key_weight, value_weight, score_vec):
    local_samples, total_length, features = hidden.shape
    tensor_number = lax.axis_size("tensor")
    heads_local = KEY_VALUE_HEADS // tensor_number
    group_width = QUERY_HEADS // KEY_VALUE_HEADS
    tensor_index = lax.axis_index("tensor")
    last_pos = lengths - 1
    position_ids = jnp.arange(total_length, dtype=jnp.int32)
    onehot = (position_ids[None, :] == last_pos[:, None]).astype(jnp.bfloat16)
    final_row = jnp.einsum("bp,bpd->bd", onehot, hidden, preferred_element_type=jnp.float32).astype(
        jnp.bfloat16
    )
    moved_rows = lax.all_to_all(final_row, "dp", split_axis=1, concat_axis=0, tiled=True)
    query_partial = lax.psum_scatter(
        jnp.dot(moved_rows, query_weight, preferred_element_type=jnp.float32),
        "dp",
        scatter_dimension=0,
        tiled=True,
    )
    query_complete = of_everyone(query_partial, "tensor")
    grouped_query = query_complete.reshape(local_samples, KEY_VALUE_HEADS, group_width, HEAD_SIZE)
    query_heads = lax.dynamic_slice_in_dim(
        grouped_query, tensor_index * heads_local, heads_local, 1
    )
    query_heads = rotate(query_heads, last_pos.astype(jnp.float32)[:, None, None]).astype(
        jnp.bfloat16
    )
    flat_scores = hidden.reshape(local_samples * total_length, features)
    key_cols = key_weight.reshape(features, heads_local * lax.axis_size("tensor"), HEAD_SIZE)
    value_cols = value_weight.reshape(features, heads_local * lax.axis_size("tensor"), HEAD_SIZE)
    key_part = jnp.einsum("nd,dhe->hne", flat_scores, key_cols, preferred_element_type=jnp.float32)
    value_part = jnp.einsum(
        "nd,dhe->hne", flat_scores, value_cols, preferred_element_type=jnp.float32
    )
    key_values = summed_on_arrival(jnp.concatenate([key_part, value_part], 2), "tensor", 0)
    key_positions = position_ids.astype(jnp.float32)
    local_keys = key_values[:, :, :HEAD_SIZE].reshape(
        heads_local, local_samples, total_length, HEAD_SIZE
    )
    local_keys = rotate(local_keys, key_positions[None, None, :]).astype(jnp.bfloat16)
    local_values = (
        key_values[:, :, HEAD_SIZE:]
        .reshape(heads_local, local_samples, total_length, HEAD_SIZE)
        .astype(jnp.bfloat16)
    )
    scores = jnp.einsum(
        "bgjd,gbpd->bgjp", query_heads, local_keys, preferred_element_type=jnp.float32
    ) / math.sqrt(HEAD_SIZE)
    visible = (position_ids[None, :] < lengths[:, None])[:, None, None, :]
    masked = jnp.where(visible, scores, -1e30)
    row_maximum = jnp.max(masked, axis=-1)
    weights_soft = jnp.where(visible, jnp.exp(masked - row_maximum[..., None]), 0.0)
    softmax_sum = jnp.sum(weights_soft, axis=-1)
    weighted_values = jnp.einsum(
        "bgjp,gbpd->bgjd",
        weights_soft,
        local_values.astype(jnp.float32),
        precision=lax.Precision.HIGHEST,
    )
    head_offset = tensor_index * heads_local
    maxima_all = lax.dynamic_update_slice_in_dim(
        jnp.full((local_samples, KEY_VALUE_HEADS, group_width), -1e30, jnp.float32),
        row_maximum,
        head_offset,
        1,
    )
    totals_all = lax.dynamic_update_slice_in_dim(
        jnp.zeros((local_samples, KEY_VALUE_HEADS, group_width), jnp.float32),
        softmax_sum,
        head_offset,
        1,
    )
    weighted_all = lax.dynamic_update_slice_in_dim(
        jnp.zeros((local_samples, KEY_VALUE_HEADS, group_width, HEAD_SIZE), jnp.float32),
        weighted_values,
        head_offset,
        1,
    )
    merged = combined_all((maxima_all, totals_all, weighted_all), "tensor", combine_soft)
    attention = (
        (merged[2] / merged[1][..., None])
        .astype(jnp.bfloat16)
        .reshape(local_samples, QUERY_HEADS * HEAD_SIZE)
    )
    rating = jnp.dot(attention.astype(jnp.float32), score_vec, precision=lax.Precision.HIGHEST)
    reward = jax.nn.sigmoid(rating)
    onehot_answer = (answers[:, None] == jnp.arange(ANSWERS, dtype=jnp.int32)[None, :]).astype(
        jnp.float32
    )
    reward_table = reward[:, None] * onehot_answer
    prompt_total = PROMPT_DEV * lax.axis_size("dp")
    onehot_prompt = (
        prompt_of[:, None] == jnp.arange(prompt_total, dtype=jnp.int32)[None, :]
    ).astype(jnp.float32)
    tally_partial = jnp.dot(onehot_prompt.T, reward_table, precision=lax.Precision.HIGHEST)
    half_tallies = summed_on_arrival(tally_partial, "dp", 0)
    tallies = gathered_total(half_tallies, "seq")
    return tallies / jnp.sum(tallies, axis=1, keepdims=True)


def solution(mesh):
    placed = (
        P(("groups", "dp", "seq"), None, "tensor"),
        P(("groups", "dp", "seq")),
        P(("groups", "dp", "seq")),
        P(("groups", "dp", "seq")),
        P(("tensor", "dp"), None),
        P("tensor", None),
        P("tensor", None),
        P(),
    )
    return jax.shard_map(
        shards, mesh=mesh, in_specs=placed, out_specs=P(("groups", "dp"), None), check_vma=False
    )
```

profile of v0, /device:TPU:33, one launch (start us, length us, event | category | flops | bytes accessed | tf_op | source)
XLA Modules:
  0.0 191.7 jit_solution(6659080232287992275)
XLA Ops:
  6.6 0.7 fusion.40
  7.4 2.8 %fusion.27 = bf16[16,1,2048]{2,1,0:T(2,128)(2,1)S(1)} fusion(bf16[16,64,2048]{2,1,0:T(8,128)(2,1)} %param.8, pred[16,64,1]{1,0,2:T(8,128)(4,1)S(1)} %fusion.32), kind=kOutput, calls=%fused_computation.58 | convolution fusion | flops 4194304 | bytes 4260864 | tf_op jit(solution)/shard_map/bp,bpd->bd/dot_general | solution.py:112
  10.3 35.7 %all_to_all.39 = bf16[16,16,128]{2,0,1:T(8,128)(2,1)S(1)} all-to-all(bf16[16,16,128]{2,0,1:T(8,128)(2,1)S(1)} %copy_bitcast_fusion), channel_id=1, replica_groups=mesh['groups'=2,'dp'=16,'tensor'=4,'seq'=2] {'dp'}, dimensions={1} | all-to-all | bytes 131072 | tf_op jit(solution)/shard_map/all_to_all | solution.py:115
  46.0 2.6 %fusion.46 = f32[256,4096]{1,0:T(8,128)} fusion(bf16[256,128]{1,0:T(8,128)(2,1)S(1)} %bitcast.129, bf16[128,4096]{1,0:T(8,128)(2,1)S(1)} %copy-done), kind=kOutput, calls=%fused_computation.87 | convolution fusion | flops 268435456 | bytes 5308416 | tf_op jit(solution)/shard_map/dot_general | solution.py:117
  48.6 1.5 copy-done.2
  50.2 2.5 %copy.56 = bf16[2048,512]{0,1:T(8,128)(2,1)} copy(bf16[2048,512]{1,0:T(8,128)(2,1)S(1)} %copy-done.2) | data formatting | bytes 4194304 | tf_op jit(solution)/shard_map/reshape | solution.py:132
  52.7 2.9 %copy.55 = bf16[2048,512]{0,1:T(8,128)(2,1)S(1)} copy(bf16[2048,512]{1,0:T(8,128)(2,1)} %param.13) | data formatting | bytes 4194304 | tf_op jit(solution)/shard_map/reshape | solution.py:131
  55.6 5.4 %convolution_bitcast_fusion = f32[4,1024,128]{1,2,0:T(8,128)S(1)} fusion(bf16[2048,4,128]{0,2,1:T(8,128)(2,1)} %bitcast.123, bf16[1024,2048,1]{1,0,2:T(8,128)(2,1)} %bitcast.117), kind=kOutput, calls=%fused_computation.2 | convolution fusion | flops 2147483648 | bytes 8388608 | tf_op jit(solution)/shard_map/nd,dhe->hne/dot_general | solution.py:134
  61.0 2.4 %convolution_bitcast_fusion.1 = f32[4,1024,128]{1,2,0:T(8,128)S(1)} fusion(bf16[2048,4,128]{0,2,1:T(8,128)(2,1)S(1)} %bitcast.122, bf16[1024,2048,1]{1,0,2:T(8,128)(2,1)S(1)} %bitcast.118), kind=kOutput, calls=%fused_computation.3 | convolution fusion | flops 2147483648 | bytes 8388608 | tf_op jit(solution)/shard_map/nd,dhe->hne/dot_general | solution.py:133
  63.4 2.5 %maximum_bitcast_fusion = f32[4,1,1024,256]{2,3,1,0:T(8,128)} fusion(f32[4,1024,128]{1,2,0:T(8,128)S(1)} %convolution_bitcast_fusion, f32[4,1024,128]{1,2,0:T(8,128)S(1)} %convolution_bitcast_fusion.1), kind=kLoop, calls=%fused_computation | loop fusion | flops 1048576 | bytes 8388608 | tf_op jit(solution)/shard_map/reshape | solution.py:32
  65.9 5.1 %all-to-all-start.2 = ((f32[4,1,1024,256]{2,3,1,0:T(8,128)}), f32[4,1,1024,256]{2,3,1,0:T(8,128)}, u32[]{:S(2)}, u32[]{:S(2)}) async-start(f32[4,1,1024,256]{2,3,1,0:T(8,128)} %maximum_bitcast_fusion), calls=%async_computation.3 | async-start | bytes 8388608 | tf_op jit(solution)/shard_map/all_to_all | solution.py:38
  71.2 46.6 %all-to-all-done.2 = f32[4,1,1024,256]{2,3,1,0:T(8,128)} async-done(((f32[4,1,1024,256]{2,3,1,0:T(8,128)}), f32[4,1,1024,256]{2,3,1,0:T(8,128)}, u32[]{:S(2)}, u32[]{:S(2)}) %all-to-all-start.2) | async-done | bytes 4194336 | tf_op jit(solution)/shard_map/all_to_all | solution.py:38
  117.9 2.0 %broadcast_in_dim.30 = f32[4,16,4096]{2,1,0:T(8,128)} broadcast(f32[16,4096]{1,0:T(8,128)} %reduce-scatter.2.cloned.1.call-done), dimensions={1,2} | broadcast | bytes 1310720 | tf_op jit(solution)/shard_map/broadcast_in_dim | solution.py:21
  119.9 3.6 %all-to-all-start.1 = ((f32[4,16,4096]{2,1,0:T(8,128)}), f32[4,16,4096]{2,1,0:T(8,128)S(1)}, u32[]{:S(2)}, u32[]{:S(2)}) async-start(f32[4,16,4096]{2,1,0:T(8,128)} %broadcast_in_dim.30), calls=%async_computation.2 | async-start | bytes 2097152 | tf_op jit(solution)/shard_map/all_to_all | solution.py:20
  123.7 2.8 %bitcast_reduce_fusion = f32[1024,256]{0,1:T(8,128)S(1)} fusion(f32[4,1,1024,256]{2,3,1,0:T(8,128)} %all-to-all-done.2), kind=kLoop, calls=%fused_computation.1 | loop fusion | flops 786432 | bytes 5242880 | tf_op jit(solution)/shard_map/reduce_sum | solution.py:39
  127.2 5.9 %all-to-all-done.1 = f32[4,16,4096]{2,1,0:T(8,128)S(1)} async-done(((f32[4,16,4096]{2,1,0:T(8,128)}), f32[4,16,4096]{2,1,0:T(8,128)S(1)}, u32[]{:S(2)}, u32[]{:S(2)}) %all-to-all-start.1) | async-done | bytes 1048608 | tf_op jit(solution)/shard_map/all_to_all | solution.py:20
  133.4 0.4 fusion.45
  134.3 0.4 fusion
  134.8 12.3 %all_to_all.40 = f32[4,520,128]{2,1,0:T(8,128)S(1)} all-to-all(f32[4,520,128]{2,1,0:T(8,128)S(1)} %broadcast_in_dim.35), channel_id=1, replica_groups=mesh['groups'=2,'dp'=16,'tensor'=4,'seq'=2] {'tensor'}, dimensions={0} | all-to-all | bytes 2129920 | tf_op jit(solution)/shard_map/all_to_all | solution.py:20
  149.2 17.6 %all_to_all.41 = f32[16,1,128]{2,1,0:T(1,128)S(1)} all-to-all(f32[16,1,128]{2,1,0:T(1,128)S(1)} %reshape.284), channel_id=1, replica_groups=mesh['groups'=2,'dp'=16,'tensor'=4,'seq'=2] {'dp'}, dimensions={0} | all-to-all | bytes 16384 | tf_op jit(solution)/shard_map/all_to_all | solution.py:38
  166.8 0.5 broadcast.142
  167.3 0.7 reduce.12
  168.1 16.0 %all-gather.1 = f32[2,2,64]{2,1,0:T(2,128)S(1)} all-gather(f32[1,2,64]{2,1,0:T(2,128)S(1)} %bitcast.133), channel_id=2, replica_groups=mesh['groups'=2,'dp'=16,'tensor'=4,'seq'=2] {'seq'}, dimensions={0}, use_global_device_ids=true | all-gather | bytes 1536 | tf_op jit(solution)/shard_map/all_gather | solution.py:73
  184.2 0.6 broadcast_divide_fusion
  (57 shorter events, 4.4 us)
Async XLA Ops:
  6.5 39.4 %copy-start = (bf16[128,4096]{1,0:T(8,128)(2,1)S(1)}, bf16[128,4096]{1,0:T(8,128)(2,1)}, u32[]{:S(2)}) copy-start(bf16[128,4096]{1,0:T(8,128)(2,1)} %param.12) | copy-start | bytes 3145732
  6.6 111.3 %reduce-scatter.2.cloned.1.call-start = ((), (), s32[]{:S(2)}) async-start(), calls=%async_computation.6 | async-start | bytes 4456448 | tf_op jit(solution)/shard_map/reduce_scatter | solution.py:116
  48.6 1.6 copy-start.2
  55.6 5.4 %copy-start.1 = (bf16[16,64,2048]{2,1,0:T(8,128)(2,1)S(1)}, bf16[16,64,2048]{2,1,0:T(8,128)(2,1)}, u32[]{:S(2)}) copy-start(bf16[16,64,2048]{2,1,0:T(8,128)(2,1)} %param.8) | copy-start | bytes 12582916
  65.9 5.1 %copy-start.3 = (s32[16]{0:T(128)S(1)}, s32[16]{0:T(128)}, u32[]{:S(2)}) copy-start(s32[16]{0:T(128)} %param.9) | copy-start | bytes 196
  65.9 51.9 %all-to-all-start.2 = ((f32[4,1,1024,256]{2,3,1,0:T(8,128)}), f32[4,1,1024,256]{2,3,1,0:T(8,128)}, u32[]{:S(2)}, u32[]{:S(2)}) async-start(f32[4,1,1024,256]{2,3,1,0:T(8,128)} %maximum_bitcast_fusion), calls=%async_computation.3 | async-start | bytes 8388608 | tf_op jit(solution)/shard_map/all_to_all | solution.py:38
  119.9 13.3 %all-to-all-start.1 = ((f32[4,16,4096]{2,1,0:T(8,128)}), f32[4,16,4096]{2,1,0:T(8,128)S(1)}, u32[]{:S(2)}, u32[]{:S(2)}) async-start(f32[4,16,4096]{2,1,0:T(8,128)} %broadcast_in_dim.30), calls=%async_computation.2 | async-start | bytes 2097152 | tf_op jit(solution)/shard_map/all_to_all | solution.py:20
  147.7 0.8 copy-start.4
  147.7 1.2 copy-start.5
  147.7 1.2 copy-start.6
Sparse Core Ops, SparseCore 0:
  48.8 63.9 reduce-scatter.1
where the time goes:
time: 192 us
  blocking collectives  81.5 us (42%)
  waiting for transfers between devices  52.6 us (27%)
  matrix products  14.7 us (8%)
  between operations  13.8 us (7%)
  local copies, waits for them, and re-layouts  11.3 us (6%)
  other arithmetic  9.2 us (5%)
  starting transfers between devices  8.68 us (5%)
    all_to_all x1, waiting for transfers between devices, summed_on_arrival(): lax.all_to_all(tiles, axis, split_axis=0, concat_axis=0, tiled=True)  46.6 us
    all_to_all x1, blocking collectives, shards(): lax.all_to_all(final_row, 'dp', split_axis=1, concat_axis=0, tiled=True)  35.7 us
    all_to_all x1, blocking collectives, summed_on_arrival(): lax.all_to_all(tiles, axis, split_axis=0, concat_axis=0, tiled=True)  17.6 us
    all_gather x1, blocking collectives, gathered_total(): tiles = lax.all_gather(shard, axis)  16 us
    all_to_all x1, blocking collectives, from_everyone(): lax.all_to_all(jnp.broadcast_to(shard[None], (count, *shard.shape)), axis...  12.3 us
    all_to_all x1, waiting for transfers between devices, from_everyone(): lax.all_to_all(jnp.broadcast_to(shard[None], (count, *shard.shape)), axis...  5.94 us
    dot_general x1, matrix products, shards(): jnp.einsum('nd,dhe->hne', flat_scores, value_cols, preferred_element_type...  5.41 us
    all_to_all x1, starting transfers between devices, summed_on_arrival(): lax.all_to_all(tiles, axis, split_axis=0, concat_axis=0, tiled=True)  5.07 us
  transfers between devices with their start and end apart: 3, of which 2 were waited for; matrix products, arithmetic and copies ran while one was open for 10% of the time, Pallas kernels for 0%

commit v1 on v0

v1 whole, which is shorter than its diff:
```python
import functools
import math

import jax
import jax.numpy as jnp
from jax import lax
from jax.experimental import pallas as pl
from jax.experimental.pallas import tpu as pltpu
from jax.sharding import PartitionSpec as P

HEAD_SIZE = 128
QUERY_HEADS = 32
KEY_VALUE_HEADS = 4
GROUP = QUERY_HEADS // KEY_VALUE_HEADS
ANSWERS = 64
PROMPT_DEV = 2
ROPE_BASE = 500000.0
BF = jnp.bfloat16
F32 = jnp.float32

VMEM = pl.BlockSpec(memory_space=pltpu.VMEM)
SMEM = pl.BlockSpec(memory_space=pltpu.SMEM)
ANY = pl.BlockSpec(memory_space=pl.ANY)


def cost(flops, bytes_accessed):
    return pl.CostEstimate(flops=flops, bytes_accessed=bytes_accessed, transcendentals=0)


def rope_tables(positions):
    halves = HEAD_SIZE // 2
    frequency = ROPE_BASE ** (-jnp.arange(halves, dtype=F32) * 2.0 / HEAD_SIZE)
    angles = positions[:, None] * frequency
    cosine, sine = jnp.cos(angles), jnp.sin(angles)
    return jnp.concatenate([cosine, cosine], -1), jnp.concatenate([-sine, sine], -1)


def rows_kernel(n_dp, lengths_ref, wide_ref, hidden_ref, out_ref, tiles, sems):
    samples, block = tiles.shape[0], tiles.shape[1]
    copies = []
    for i in range(samples):
        at = pl.multiple_of(((lengths_ref[i] - 1) // block) * block, block)
        copy = pltpu.make_async_copy(
            hidden_ref.at[i, pl.ds(at, block), :], tiles.at[i], sems.at[i]
        )
        copy.start()
        copies.append(copy)
    lane = lax.broadcasted_iota(jnp.int32, (samples, samples * block), 1)
    row = lax.broadcasted_iota(jnp.int32, (samples, samples * block), 0)
    inside = (wide_ref[:, : 1] - 1) % block
    pick = jnp.where(lane == row * block + inside, 1.0, 0.0).astype(BF)
    for copy in copies:
        copy.wait()
    stacked = tiles[...].reshape(samples * block, tiles.shape[2])
    rows = jnp.dot(pick, stacked, preferred_element_type=F32).astype(BF)
    width = rows.shape[1] // n_dp
    for d in range(n_dp):
        for side, source in enumerate((d, d ^ 1)):
            out_ref[d, :, side * width : (side + 1) * width] = rows[
                :, source * width : (source + 1) * width
            ]


def scoring_rows(lengths, wide, hidden, n_dp):
    samples, _, features = hidden.shape
    width = 2 * features // n_dp
    return pl.pallas_call(
        functools.partial(rows_kernel, n_dp),
        out_shape=jax.ShapeDtypeStruct((n_dp, samples, width), BF),
        in_specs=[SMEM, VMEM, ANY],
        out_specs=VMEM,
        scratch_shapes=[
            pltpu.VMEM((samples, 16, features), BF),
            pltpu.SemaphoreType.DMA((samples,)),
        ],
        cost_estimate=cost(2 * samples * 256 * features, samples * 16 * features * 2),
        name="scoring_rows",
    )(lengths, wide, hidden)


def cut_kernel(n_tensor, place_ref, weight_ref, *out_refs):
    t, parity = place_ref[0], place_ref[1]
    part = out_refs[0].shape[1]
    for side in range(2):
        for s in range(n_tensor):
            column = 2 * ((t + s) % n_tensor) + (parity ^ side)
            at = pl.multiple_of(column * part, part)
            out_refs[side * n_tensor + s][...] = weight_ref[:, pl.ds(at, part)]


def cut_weight(place, weight, n_tensor):
    rows, columns = weight.shape
    part = columns // (2 * n_tensor)
    count = 2 * n_tensor
    return pl.pallas_call(
        functools.partial(cut_kernel, n_tensor),
        out_shape=[jax.ShapeDtypeStruct((rows, part), BF)] * count,
        in_specs=[SMEM, VMEM],
        out_specs=[VMEM] * count,
        cost_estimate=cost(1000, 2 * rows * columns * 2),
        name="cut_weight",
    )(place, weight)


def kv_kernel(n_tensor, t_ref, x_ref, *refs):
    wk_refs = refs[:n_tensor]
    wv_ref, s_ref, cos_ref, sin_ref = refs[n_tensor : n_tensor + 4]
    out_refs = refs[n_tensor + 4 : 2 * n_tensor + 4]
    z_ref, w_ref = refs[2 * n_tensor + 4 :]
    step = pl.program_id(0)
    heads = QUERY_HEADS

    @pl.when(step == 0)
    def _():
        t = t_ref[0]
        head = lax.broadcasted_iota(jnp.int32, (heads, KEY_VALUE_HEADS * HEAD_SIZE), 0)
        column = lax.broadcasted_iota(jnp.int32, (heads, KEY_VALUE_HEADS * HEAD_SIZE), 1)
        spread = jnp.concatenate([s_ref[...]] * KEY_VALUE_HEADS, axis=1)
        full = jnp.where(head // GROUP == column // HEAD_SIZE, spread, 0.0)
        high = full.astype(BF)
        low = (full - high.astype(F32)).astype(BF)
        both = jnp.concatenate([high, low], axis=0)
        z = lax.dot_general(
            both, wv_ref[...], (((1,), (1,)), ((), ())), preferred_element_type=F32
        )
        z = z[:heads] + z[heads:]
        z_high = z.astype(BF)
        z_ref[:heads, :] = z_high
        z_ref[heads:, :] = (z - z_high.astype(F32)).astype(BF)
        for s in range(n_tensor):
            w_ref[:, s * HEAD_SIZE : (s + 1) * HEAD_SIZE] = wk_refs[s][...]

    x = x_ref[...]
    rows = x.shape[0]
    keys = jnp.dot(x, w_ref[...], preferred_element_type=F32)
    cosine = jnp.concatenate([cos_ref[...]] * (rows // cos_ref.shape[0]), axis=0)
    sine = jnp.concatenate([sin_ref[...]] * (rows // sin_ref.shape[0]), axis=0)
    at = pl.multiple_of(step * rows, rows)
    for s in range(n_tensor):
        k = keys[:, s * HEAD_SIZE : (s + 1) * HEAD_SIZE]
        rotated = k * cosine + pltpu.roll(k, HEAD_SIZE // 2, 1) * sine
        out_refs[s][pl.ds(at, rows), :] = rotated.astype(BF)
    u = lax.dot_general(
        z_ref[...], x, (((1,), (1,)), ((), ())), preferred_element_type=F32
    )
    u = u[:heads] + u[heads:]
    u_high = u.astype(BF)
    u_low = (u - u_high.astype(F32)).astype(BF)
    total = pl.num_programs(0) * rows
    for g in range(n_tensor):
        slot = (g - t_ref[0] + n_tensor) % n_tensor
        mine = jnp.concatenate(
            [u_high[g * GROUP : (g + 1) * GROUP], u_low[g * GROUP : (g + 1) * GROUP]], axis=0
        )
        for s in range(n_tensor):

            @pl.when(slot == s)
            def _():
                for c in range(rows // HEAD_SIZE):
                    base = total + (step * (rows // HEAD_SIZE) + c) * 2 * GROUP
                    out_refs[s][pl.ds(pl.multiple_of(base, 2 * GROUP), 2 * GROUP), :] = mine[
                        :, c * HEAD_SIZE : (c + 1) * HEAD_SIZE
                    ]


def keys_and_values(place, flat, key_weight, value_weight, score_rows, cosine, sine, n_tensor):
    total, features = flat.shape
    rows = 256
    packed = total + (total // HEAD_SIZE) * 2 * GROUP

    def whole(*dims):
        return pl.BlockSpec(dims, lambda i, p: (0,) * len(dims))

    def key_block(s):
        return pl.BlockSpec((features, HEAD_SIZE), lambda i, p: (0, (p[0] + s) % n_tensor))

    return pl.pallas_call(
        functools.partial(kv_kernel, n_tensor),
        grid_spec=pltpu.PrefetchScalarGridSpec(
            num_scalar_prefetch=1,
            grid=(total // rows,),
            in_specs=[pl.BlockSpec((rows, features), lambda i, p: (i, 0))]
            + [key_block(s) for s in range(n_tensor)]
            + [
                whole(*value_weight.shape),
                whole(*score_rows.shape),
                whole(*cosine.shape),
                whole(*sine.shape),
            ],
            out_specs=[whole(packed, HEAD_SIZE)] * n_tensor,
            scratch_shapes=[
                pltpu.VMEM((2 * QUERY_HEADS, features), BF),
                pltpu.VMEM((features, n_tensor * HEAD_SIZE), BF),
            ],
        ),
        out_shape=[jax.ShapeDtypeStruct((packed, HEAD_SIZE), BF)] * n_tensor,
        cost_estimate=cost(2 * total * features * 640, 9 * 2**20),
        name="keys_and_values",
    )(place, flat, *[key_weight] * n_tensor, value_weight, score_rows, cosine, sine)


def query_kernel(n_tensor, *refs):
    x_refs = refs[:n_tensor]
    w_refs = refs[n_tensor : 3 * n_tensor]
    out_ref = refs[3 * n_tensor]
    n_dp, heads, samples, _ = out_ref.shape
    x = jnp.concatenate(
        [x_refs[s][...].reshape(n_dp * samples, -1) for s in range(n_tensor)], axis=1
    )
    w = jnp.concatenate(
        [w_refs[side * n_tensor + s][...] for s in range(n_tensor) for side in range(2)], axis=0
    )
    q = jnp.dot(x, w, preferred_element_type=F32).astype(BF)
    for h in range(heads):
        out_ref[:, h, :, :] = q[:, h * HEAD_SIZE : (h + 1) * HEAD_SIZE].reshape(
            n_dp, samples, HEAD_SIZE
        )


def partial_queries(pieces, weights):
    n_dp, samples, width = pieces[0].shape
    heads = weights[0].shape[1] // HEAD_SIZE
    return pl.pallas_call(
        functools.partial(query_kernel, len(pieces)),
        out_shape=jax.ShapeDtypeStruct((n_dp, heads, samples, HEAD_SIZE), BF),
        in_specs=[VMEM] * (len(pieces) + len(weights)),
        out_specs=VMEM,
        cost_estimate=cost(2 * n_dp * samples * width * 4 * heads * HEAD_SIZE, 2 * 2**20),
        name="partial_queries",
    )(*pieces, *weights)


def attention_kernel(n_tensor, q_ref, *refs):
    kv_refs = refs[:n_tensor]
    wide_ref, cos_ref, sin_ref, prompt_ref, answer_ref, out_ref = refs[n_tensor:]
    n_dp, half, samples, _ = q_ref.shape
    q = jnp.zeros((2 * half * samples, HEAD_SIZE), F32)
    for pair in range(n_dp // 2):
        block = q_ref[2 * pair : 2 * pair + 2].reshape(2 * half * samples, HEAD_SIZE)
        q = q + block.astype(F32)
    heads = 2 * half
    cosine = jnp.concatenate([cos_ref[...]] * heads, axis=0)
    sine = jnp.concatenate([sin_ref[...]] * heads, axis=0)
    q = (q * cosine + pltpu.roll(q, HEAD_SIZE // 2, 1) * sine).astype(BF)
    total = samples * 64
    chunks = total // HEAD_SIZE
    lengths = jnp.concatenate([wide_ref[...]] * heads, axis=0)
    lane = lax.broadcasted_iota(jnp.int32, (heads * samples, HEAD_SIZE), 1)
    row = lax.broadcasted_iota(jnp.int32, (heads * samples, HEAD_SIZE), 0)
    start = (row % samples) * 64
    scores, values = [], []
    for c in range(chunks):
        k = kv_refs[0][c * HEAD_SIZE : (c + 1) * HEAD_SIZE].astype(F32)
        base = total + c * 2 * GROUP
        u = kv_refs[0][base : base + 2 * GROUP].astype(F32)
        for s in range(1, n_tensor):
            k = k + kv_refs[s][c * HEAD_SIZE : (c + 1) * HEAD_SIZE].astype(F32)
            u = u + kv_refs[s][base : base + 2 * GROUP].astype(F32)
        u = u[:GROUP] + u[GROUP:]
        score = lax.dot_general(
            q, k.astype(BF), (((1,), (1,)), ((), ())), preferred_element_type=F32
        ) / math.sqrt(HEAD_SIZE)
        position = lane + c * HEAD_SIZE - start
        scores.append(jnp.where((position >= 0) & (position < lengths), score, -1e30))
        values.append(
            jnp.broadcast_to(u[:, None, :], (heads, samples, HEAD_SIZE)).reshape(
                heads * samples, HEAD_SIZE
            )
        )
    top = scores[0]
    for c in range(1, chunks):
        top = jnp.maximum(top, scores[c])
    top = jnp.max(top, axis=1, keepdims=True)
    below = jnp.zeros_like(scores[0])
    above = jnp.zeros_like(scores[0])
    for c in range(chunks):
        weight = jnp.exp(scores[c] - top)
        below = below + weight
        above = above + weight * values[c]
    part = jnp.sum(above, axis=1, keepdims=True) / jnp.sum(below, axis=1, keepdims=True)
    rating = jnp.sum(part.reshape(heads, samples, 1), axis=0)
    out_rows = out_ref.shape[0]
    owner = lax.broadcasted_iota(jnp.int32, (out_rows, HEAD_SIZE), 0) // n_tensor
    column = lax.broadcasted_iota(jnp.int32, (out_rows, HEAD_SIZE), 1)
    out = jnp.zeros((out_rows, HEAD_SIZE), F32)
    for i in range(samples):
        prompt = prompt_ref[i]
        place = ((prompt % PROMPT_DEV) * ANSWERS + answer_ref[i]).astype(F32)
        value = jnp.broadcast_to(rating[i : i + 1, :], (out_rows, HEAD_SIZE))
        entry = jnp.where(column == 0, value, jnp.where(column == 1, place, 0.0))
        out = jnp.where(owner == prompt // PROMPT_DEV, entry, out)
    out_ref[...] = out


def partial_ratings(queries, kv, wide, cosine, sine, prompt_of, answers):
    n_tensor = len(kv)
    n_dp = queries.shape[0]
    return pl.pallas_call(
        functools.partial(attention_kernel, n_tensor),
        out_shape=jax.ShapeDtypeStruct((n_dp * n_tensor, HEAD_SIZE), F32),
        in_specs=[VMEM] * (n_tensor + 4) + [SMEM, SMEM],
        out_specs=VMEM,
        cost_estimate=cost(2 * 128 * 128 * 1024, 2 * 2**20),
        name="partial_ratings",
    )(queries, *kv, wide, cosine, sine, prompt_of, answers)


def tally_kernel(n_tensor, rows_ref, out_ref):
    rows = rows_ref[...]
    summed = rows.reshape(rows.shape[0] // n_tensor, n_tensor, HEAD_SIZE)
    rating = jnp.sum(summed[:, :, 0:1], axis=1)
    place = summed[:, 0, 1:2].astype(jnp.int32)
    reward = 1.0 / (1.0 + jnp.exp(-rating))
    lane = lax.broadcasted_iota(jnp.int32, (rating.shape[0], HEAD_SIZE), 1)
    out_ref[...] = jnp.sum(jnp.where(lane == place, reward, 0.0), axis=0, keepdims=True)


def half_tallies(rows, n_tensor):
    return pl.pallas_call(
        functools.partial(tally_kernel, n_tensor),
        out_shape=jax.ShapeDtypeStruct((1, HEAD_SIZE), F32),
        in_specs=[VMEM],
        out_specs=VMEM,
        name="half_tallies",
    )(rows)


def share_kernel(here_ref, there_ref, out_ref):
    total = here_ref[...] + there_ref[...]
    for q in range(PROMPT_DEV):
        tally = total[:, q * ANSWERS : (q + 1) * ANSWERS]
        out_ref[q : q + 1, :] = tally / jnp.sum(tally, axis=1, keepdims=True)


def shares(here, there):
    return pl.pallas_call(
        share_kernel,
        out_shape=jax.ShapeDtypeStruct((PROMPT_DEV, ANSWERS), F32),
        in_specs=[VMEM, VMEM],
        out_specs=VMEM,
        name="shares",
    )(here, there)


def shards(hidden, lengths, answers, prompt_of, query_weight, key_weight, value_weight, score_vec):
    samples, positions, features = hidden.shape
    n_dp, n_tensor, n_seq = (lax.axis_size(a) for a in ("dp", "tensor", "seq"))
    t = lax.axis_index("tensor").astype(jnp.int32)
    parity = lax.axis_index("dp").astype(jnp.int32) % 2
    place = jnp.stack([t, parity])
    wide = jnp.broadcast_to(lengths[:, None], (samples, HEAD_SIZE))

    def over_tensor(value, s):
        return lax.ppermute(value, "tensor", [(i, (i + s) % n_tensor) for i in range(n_tensor)])

    def weight_piece(value, side, s):
        if side == 0 and s == 0:
            return value
        pairs = [
            (d * n_tensor + i, (d ^ side) * n_tensor + (i + s) % n_tensor)
            for d in range(n_dp)
            for i in range(n_tensor)
        ]
        return lax.ppermute(value, ("dp", "tensor"), pairs)

    rows = scoring_rows(lengths, wide, hidden, n_dp)
    moved = lax.all_to_all(rows, "dp", 0, 0, tiled=True)

    cut = cut_weight(place, query_weight, n_tensor)
    weights = [weight_piece(cut[k], k // n_tensor, k % n_tensor) for k in range(2 * n_tensor)]

    key_cos, key_sin = rope_tables(jnp.arange(positions, dtype=F32))
    kv = keys_and_values(
        place,
        hidden.reshape(samples * positions, features),
        key_weight,
        value_weight,
        score_vec.reshape(QUERY_HEADS, HEAD_SIZE),
        key_cos,
        key_sin,
        n_tensor,
    )
    pieces = [moved] + [over_tensor(moved, s) for s in range(1, n_tensor)]
    queries = partial_queries(pieces, weights)
    arrived = lax.all_to_all(queries, "dp", 0, 0, tiled=True)
    kv = [kv[0]] + [over_tensor(kv[s], s) for s in range(1, n_tensor)]
    query_cos, query_sin = rope_tables((lengths - 1).astype(F32))
    rated = partial_ratings(arrived, kv, wide, query_cos, query_sin, prompt_of, answers)
    gathered = lax.all_to_all(rated, ("dp", "tensor"), 0, 0, tiled=True)
    here = half_tallies(gathered, n_tensor)
    there = lax.ppermute(here, "seq", [(i, (i + 1) % n_seq) for i in range(n_seq)])
    return shares(here, there)


def solution(mesh):
    placed = (
        P(("groups", "dp", "seq"), None, "tensor"),
        P(("groups", "dp", "seq")),
        P(("groups", "dp", "seq")),
        P(("groups", "dp", "seq")),
        P(("tensor", "dp"), None),
        P("tensor", None),
        P("tensor", None),
        P(),
    )
    return jax.shard_map(
        shards, mesh=mesh, in_specs=placed, out_specs=P(("groups", "dp"), None), check_vma=False
    )
```

time: 192 us -> 136 us (0.71)
  blocking collectives: 81.5 us -> 29.9 us
  starting transfers between devices: 8.68 us -> 58 us
  waiting for transfers between devices: 52.6 us -> 17.9 us
  Pallas kernels: 0 us -> 23.6 us
  matrix products: 14.7 us -> 0 us
  between operations: 13.8 us -> 0.15 us
  local copies, waits for them, and re-layouts: 11.3 us -> 3.43 us
  other arithmetic: 9.2 us -> 2.28 us
    all_to_all x2, waiting for transfers between devices: 52.6 us -> 0.01 us  [the longest x1 0.01 us: shards(): arrived = lax.all_to_all(queries, 'dp', 0, 0, tiled=True)]
    all_to_all x3 -> x1, blocking collectives: 65.5 us -> 29.9 us  [shards(): gathered = lax.all_to_all(rated, ('dp', 'tensor'), 0, 0, tiled=True)]
    ppermute x0 -> x14, starting transfers between devices: none -> 25.1 us  [the longest x6 9.88 us: over_tensor(): lax.ppermute(value, 'tensor', [(i, (i + s) % n_tensor) for i in range(n_t...]
    all_to_all x2, starting transfers between devices: 8.68 us -> 32.9 us  [the longest x1 24.5 us: shards(): moved = lax.all_to_all(rows, 'dp', 0, 0, tiled=True)]
    pallas_call x0 -> x7, Pallas kernels: none -> 23.6 us  [the longest x1 10.2 us: keys_and_values(): pl.pallas_call(functools.partial(kv_kernel, n_tensor), grid_spec=pltpu.Pr...]
    ppermute x0 -> x14, waiting for transfers between devices: none -> 17.9 us  [the longest x6 12 us: over_tensor(): lax.ppermute(value, 'tensor', [(i, (i + s) % n_tensor) for i in range(n_t...]
    all_gather x1 -> x0, blocking collectives: 16 us -> none  [gathered_total(): tiles = lax.all_gather(shard, axis)]
    dot_general x8 -> x0, matrix products: 14.7 us -> none  [the longest x1 5.41 us: shards(): jnp.einsum('nd,dhe->hne', flat_scores, value_cols, preferred_element_type...]
  transfers between devices with their start and end apart: 3 -> 16, of which waited for: 2 -> 8; matrix products, arithmetic and copies ran while one was open for 10% -> 2% of each run, Pallas kernels for 0% -> 9%
where the time goes in v1:
time: 136 us; the launch traced here: 135 us
  starting transfers between devices  58 us (43%)
  blocking collectives  29.9 us (22%)
  Pallas kernels  23.6 us (17%)
  waiting for transfers between devices  17.9 us (13%)
  local copies, waits for them, and re-layouts  3.43 us (3%)
  other arithmetic  2.28 us (2%)
    all_to_all x1, blocking collectives, shards(): gathered = lax.all_to_all(rated, ('dp', 'tensor'), 0, 0, tiled=True)  29.9 us
    all_to_all x1, starting transfers between devices, shards(): moved = lax.all_to_all(rows, 'dp', 0, 0, tiled=True)  24.5 us
    ppermute x6, waiting for transfers between devices, over_tensor(): lax.ppermute(value, 'tensor', [(i, (i + s) % n_tensor) for i in range(n_t...  12 us
    pallas_call x1, Pallas kernels, keys_and_values(): pl.pallas_call(functools.partial(kv_kernel, n_tensor), grid_spec=pltpu.Pr...  10.2 us
    ppermute x6, starting transfers between devices, over_tensor(): lax.ppermute(value, 'tensor', [(i, (i + s) % n_tensor) for i in range(n_t...  9.88 us
    ppermute x7, starting transfers between devices, weight_piece(): return lax.ppermute(value, ('dp', 'tensor'), pairs)  8.64 us
    all_to_all x1, starting transfers between devices, shards(): arrived = lax.all_to_all(queries, 'dp', 0, 0, tiled=True)  8.42 us
    ppermute x1, starting transfers between devices, shards(): lax.ppermute(here, 'seq', [(i, (i + 1) % n_seq) for i in range(n_seq)])  6.54 us
  transfers between devices with their start and end apart: 16, of which 8 were waited for; matrix products, arithmetic and copies ran while one was open for 2% of the time, Pallas kernels for 9%

profile of v1, /device:TPU:33, one launch (start us, length us, event | category | flops | bytes accessed | tf_op | source)
XLA Modules:
  0.0 135.2 jit_solution(2541520158650253260)
XLA Ops:
  0.0 1.3 broadcast_in_dim.2.wide_ref.refs_4_
  1.3 3.0 %scoring_rows.1 = bf16[16,16,256]{2,1,0:T(8,128)(2,1)} custom-call(s32[16]{0:T(128)} %lengths_ref.1, s32[16,128]{1,0:T(8,128)} %broadcast_in_dim.2.wide_ref.refs_4_, bf16[16,64,2048]{2,1,0:T(8,128)(2,1)} %hidden_ref.1), custom_call_target="tpu_custom_call" | custom-call | flops 16777216 | bytes 1048576 | tf_op jit(solution)/shard_map/scoring_rows/pallas_call | solution.py:67
  4.3 24.5 %all-to-all-start = ((bf16[16,16,256]{2,1,0:T(8,128)(2,1)}), bf16[16,16,256]{2,1,0:T(8,128)(2,1)S(1)}, u32[]{:S(2)}, u32[]{:S(2)}) async-start(bf16[16,16,256]{2,1,0:T(8,128)(2,1)} %scoring_rows.1), calls=%async_computation | async-start | bytes 262144 | tf_op jit(solution)/shard_map/all_to_all | solution.py:367
  29.5 2.3 %cut_weight.1 = (bf16[128,512]{1,0:T(8,128)(2,1)}, bf16[128,512]{1,0:T(8,128)(2,1)}, bf16[128,512]{1,0:T(8,128)(2,1)}, bf16[128,512]{1,0:T(8,128)(2,1)}, bf16[12...) custom-call(s32[2]{0:T(128)} %pad_add_fusion.place_ref.t_ref, ...), custom_call_target="tpu_custom_call" | custom-call | flops 1000 | bytes 2097152 | tf_op jit(solution)/shard_map/cut_weight/pallas_call | solution.py:95
  31.8 1.3 collective-permute-start.3
  33.2 2.7 %collective-permute-start.4 = (bf16[128,512]{1,0:T(8,128)(2,1)}, bf16[128,512]{1,0:T(8,128)(2,1)S(1)}, u32[]{:S(2)}, u32[]{:S(2)}) collective-permute-start(bf16[128,512]{1,0:T(8,128)(2,1)} %get-tuple-element.19), channel_id=1, source_target_pairs={{0,4},{2,6},{4,0},{6,2},{8,12},{10,14},{12,8},{14,10},{16,20},{18,... | collective-permute-start | bytes 393224 | tf_op jit(solution)/shard_map/ppermute | solution.py:364
  38.6 1.6 %collective-permute-start.8 = (bf16[128,512]{1,0:T(8,128)(2,1)}, bf16[128,512]{1,0:T(8,128)(2,1)S(1)}, u32[]{:S(2)}, u32[]{:S(2)}) collective-permute-start(bf16[128,512]{1,0:T(8,128)(2,1)} %get-tuple-element.23), channel_id=1, source_target_pairs={{0,12},{2,14},{4,8},{6,10},{8,4},{10,6},{12,0},{14,2},{16,28},{18,... | collective-permute-start | bytes 393224 | tf_op jit(solution)/shard_map/ppermute | solution.py:364
  40.2 1.5 %collective-permute-done.4.refs_6_ = bf16[128,512]{1,0:T(8,128)(2,1)S(1)} collective-permute-done((bf16[128,512]{1,0:T(8,128)(2,1)}, bf16[128,512]{1,0:T(8,128)(2,1)S(1)}, u32[]{:S(2)}, u32[]{:S(2)}) %collective-permute-start.4) | collective-permute-done | bytes 131104 | tf_op jit(solution)/shard_map/ppermute | solution.py:364
  42.0 1.8 %collective-permute-start = (bf16[16,16,256]{2,1,0:T(8,128)(2,1)S(1)}, bf16[16,16,256]{2,1,0:T(8,128)(2,1)S(1)}, u32[]{:S(2)}, u32[]{:S(2)}) collective-permute-start(bf16[16,16,256]{2,1,0:T(8,128)(2,1)S(1)} %all-to-all-done.refs_0_), channel_id=1, source_target_pairs={{0,2},{2,4},{4,6},{6,0},{1,3},{3,5},{5,7},{7,1},{8,10},{10,12},{12... | collective-permute-start | bytes 393224 | tf_op jit(solution)/shard_map/ppermute | solution.py:354
  43.8 1.4 %collective-permute-start.1 = (bf16[16,16,256]{2,1,0:T(8,128)(2,1)S(1)}, bf16[16,16,256]{2,1,0:T(8,128)(2,1)S(1)}, u32[]{:S(2)}, u32[]{:S(2)}) collective-permute-start(bf16[16,16,256]{2,1,0:T(8,128)(2,1)S(1)} %all-to-all-done.refs_0_), channel_id=1, source_target_pairs={{0,4},{2,6},{4,0},{6,2},{1,5},{3,7},{5,1},{7,3},{8,12},{10,14},{12... | collective-permute-start | bytes 393224 | tf_op jit(solution)/shard_map/ppermute | solution.py:354
  46.4 2.4 %collective-permute-done.8.refs_10_ = bf16[128,512]{1,0:T(8,128)(2,1)S(1)} collective-permute-done((bf16[128,512]{1,0:T(8,128)(2,1)}, bf16[128,512]{1,0:T(8,128)(2,1)S(1)}, u32[]{:S(2)}, u32[]{:S(2)}) %collective-permute-start.8) | collective-permute-done | bytes 131104 | tf_op jit(solution)/shard_map/ppermute | solution.py:364
  49.8 5.7 %collective-permute-done.refs_1_ = bf16[16,16,256]{2,1,0:T(8,128)(2,1)S(1)} collective-permute-done((bf16[16,16,256]{2,1,0:T(8,128)(2,1)S(1)}, bf16[16,16,256]{2,1,0:T(8,128)(2,1)S(1)}, u32[]{:S(2)}, u32[]{:S(2)}) %collective-permute-start) | collective-permute-done | bytes 131104 | tf_op jit(solution)/shard_map/ppermute | solution.py:354
  56.5 2.6 %partial_queries.1 = bf16[16,4,16,128]{3,2,1,0:T(8,128)(2,1)} custom-call(bf16[16,16,256]{2,1,0:T(8,128)(2,1)} %copy-done.1, bf16[16,16,256]{2,1,0:T(8,128)(2,1)} %copy-done.12, bf16[16,16,256]{2,1,0:T(8,128)(2,1)} %copy-done.13, bf16[16,16,256]{2,1,0:T(8,128)(2,1)} %copy-done.14, bf16[128,512]{1,0:T(8,128)(2,1)} %get-tuple-element.17.refs_4_, ...), custom_call_target="tpu_custom_call" | custom-call | flops 268435456 | bytes 2097152 | tf_op jit(solution)/shard_map/partial_queries/pallas_call | solution.py:223
  59.1 8.4 %all-to-all-start.1 = ((bf16[16,4,16,128]{3,2,1,0:T(8,128)(2,1)}), bf16[16,4,16,128]{3,2,1,0:T(8,128)(2,1)S(1)}, u32[]{:S(2)}, u32[]{:S(2)}) async-start(bf16[16,4,16,128]{3,2,1,0:T(8,128)(2,1)} %partial_queries.1), calls=%async_computation.1 | async-start | bytes 524288 | tf_op jit(solution)/shard_map/all_to_all | solution.py:385
  68.4 10.2 %keys_and_values.1 = (bf16[1152,128]{1,0:T(8,128)(2,1)}, bf16[1152,128]{1,0:T(8,128)(2,1)}, bf16[1152,128]{1,0:T(8,128)(2,1)}, bf16[1152,128]{1,0:T(8,128)(2,1)}) custom-call(s32[2]{0:T(128)} %pad_add_fusion.place_ref.t_ref, bf16[1024,2048]{1,0:T(8,128)(2,1)} %bitcast.8, bf16[2048,512]{1,0:T(8,128)(2,1)} %refs_3_.1, bf16[2048,512]{1,0:T(8,128)(2,1)} %refs_3_.1, ...), custom_call_target="tpu_custom_call" | custom-call | flops 2684354560 | bytes 9437184 | tf_op jit(solution)/shard_map/keys_and_values/pallas_call | solution.py:177
  78.6 1.6 %collective-permute-start.10 = (bf16[1152,128]{1,0:T(8,128)(2,1)}, bf16[1152,128]{1,0:T(8,128)(2,1)S(1)}, u32[]{:S(2)}, u32[]{:S(2)}) collective-permute-start(bf16[1152,128]{1,0:T(8,128)(2,1)} %get-tuple-element.26), channel_id=1, source_target_pairs={{0,2},{2,4},{4,6},{6,0},{1,3},{3,5},{5,7},{7,1},{8,10},{10,12},{12... | collective-permute-start | bytes 884744 | tf_op jit(solution)/shard_map/ppermute | solution.py:354
  80.2 2.1 %collective-permute-start.11 = (bf16[1152,128]{1,0:T(8,128)(2,1)}, bf16[1152,128]{1,0:T(8,128)(2,1)S(1)}, u32[]{:S(2)}, u32[]{:S(2)}) collective-permute-start(bf16[1152,128]{1,0:T(8,128)(2,1)} %get-tuple-element.27), channel_id=1, source_target_pairs={{0,4},{2,6},{4,0},{6,2},{1,5},{3,7},{5,1},{7,3},{8,12},{10,14},{12... | collective-permute-start | bytes 884744 | tf_op jit(solution)/shard_map/ppermute | solution.py:354
  82.3 1.8 %collective-permute-start.12 = (bf16[1152,128]{1,0:T(8,128)(2,1)}, bf16[1152,128]{1,0:T(8,128)(2,1)S(1)}, u32[]{:S(2)}, u32[]{:S(2)}) collective-permute-start(bf16[1152,128]{1,0:T(8,128)(2,1)} %get-tuple-element.28), channel_id=1, source_target_pairs={{0,6},{2,0},{4,2},{6,4},{1,7},{3,1},{5,3},{7,5},{8,14},{10,8},{12,... | collective-permute-start | bytes 884744 | tf_op jit(solution)/shard_map/ppermute | solution.py:354
  85.9 4.9 %collective-permute-done.11.refs_2_ = bf16[1152,128]{1,0:T(8,128)(2,1)S(1)} collective-permute-done((bf16[1152,128]{1,0:T(8,128)(2,1)}, bf16[1152,128]{1,0:T(8,128)(2,1)S(1)}, u32[]{:S(2)}, u32[]{:S(2)}) %collective-permute-start.11) | collective-permute-done | bytes 294944 | tf_op jit(solution)/shard_map/ppermute | solution.py:354
  91.7 2.6 %partial_ratings.1 = f32[64,128]{1,0:T(8,128)} custom-call(bf16[16,4,16,128]{3,2,1,0:T(8,128)(2,1)} %copy-done, bf16[1152,128]{1,0:T(8,128)(2,1)} %get-tuple-element.25.refs_0_, bf16[1152,128]{1,0:T(8,128)(2,1)} %copy-done.2, bf16[1152,128]{1,0:T(8,128)(2,1)} %copy-done.3, bf16[1152,128]{1,0:T(8,128)(2,1)} %copy-done.4, ...), custom_call_target="tpu_custom_call" | custom-call | flops 33554432 | bytes 2097152 | tf_op jit(solution)/shard_map/partial_ratings/pallas_call | solution.py:298
  94.4 29.9 %all_to_all.21 = f32[64,1,128]{2,1,0:T(1,128)} all-to-all(f32[64,1,128]{2,1,0:T(1,128)} %bitcast.9), channel_id=1, replica_groups=mesh['groups'=2,'dp'=16,'tensor'=4,'seq'=2] {'dp','tensor'}, dimensions={0} | all-to-all | bytes 65536 | tf_op jit(solution)/shard_map/all_to_all | solution.py:389
  124.3 1.4 %half_tallies.1.here_ref = f32[1,128]{1,0:T(1,128)} custom-call(f32[64,128]{1,0:T(8,128)} %bitcast.10), custom_call_target="tpu_custom_call" | custom-call | tf_op jit(solution)/shard_map/half_tallies/pallas_call | solution.py:319
  125.7 6.5 %collective-permute-start.13 = (f32[1,128]{1,0:T(1,128)}, f32[1,128]{1,0:T(1,128)S(1)}, u32[]{:S(2)}, u32[]{:S(2)}) collective-permute-start(f32[1,128]{1,0:T(1,128)} %half_tallies.1.here_ref), channel_id=1, source_target_pairs={{0,1},{1,0},{2,3},{3,2},{4,5},{5,4},{6,7},{7,6},{8,9},{9,8},{10,11... | collective-permute-start | bytes 1544 | tf_op jit(solution)/shard_map/ppermute | solution.py:391
  133.8 1.4 %shares.1 = f32[2,64]{1,0:T(2,128)} custom-call(f32[1,128]{1,0:T(1,128)} %half_tallies.1.here_ref, f32[1,128]{1,0:T(1,128)} %copy-done.16), custom_call_target="tpu_custom_call" | custom-call | tf_op jit(solution)/shard_map/shares/pallas_call | solution.py:336
  (58 shorter events, 12.0 us)
Async XLA Ops:
  4.3 37.6 %all-to-all-start = ((bf16[16,16,256]{2,1,0:T(8,128)(2,1)}), bf16[16,16,256]{2,1,0:T(8,128)(2,1)S(1)}, u32[]{:S(2)}, u32[]{:S(2)}) async-start(bf16[16,16,256]{2,1,0:T(8,128)(2,1)} %scoring_rows.1), calls=%async_computation | async-start | bytes 262144 | tf_op jit(solution)/shard_map/all_to_all | solution.py:367
  31.8 6.7 %collective-permute-start.3 = (bf16[128,512]{1,0:T(8,128)(2,1)}, bf16[128,512]{1,0:T(8,128)(2,1)S(1)}, u32[]{:S(2)}, u32[]{:S(2)}) collective-permute-start(bf16[128,512]{1,0:T(8,128)(2,1)} %get-tuple-element.18), channel_id=1, source_target_pairs={{0,2},{2,4},{4,6},{6,0},{8,10},{10,12},{12,14},{14,8},{16,18},{18,... | collective-permute-start | bytes 393224 | tf_op jit(solution)/shard_map/ppermute | solution.py:364
  33.2 8.4 %collective-permute-start.4 = (bf16[128,512]{1,0:T(8,128)(2,1)}, bf16[128,512]{1,0:T(8,128)(2,1)S(1)}, u32[]{:S(2)}, u32[]{:S(2)}) collective-permute-start(bf16[128,512]{1,0:T(8,128)(2,1)} %get-tuple-element.19), channel_id=1, source_target_pairs={{0,4},{2,6},{4,0},{6,2},{8,12},{10,14},{12,8},{14,10},{16,20},{18,... | collective-permute-start | bytes 393224 | tf_op jit(solution)/shard_map/ppermute | solution.py:364
  35.9 6.0 %collective-permute-start.5 = (bf16[128,512]{1,0:T(8,128)(2,1)}, bf16[128,512]{1,0:T(8,128)(2,1)S(1)}, u32[]{:S(2)}, u32[]{:S(2)}) collective-permute-start(bf16[128,512]{1,0:T(8,128)(2,1)} %get-tuple-element.20), channel_id=1, source_target_pairs={{0,6},{2,0},{4,2},{6,4},{8,14},{10,8},{12,10},{14,12},{16,22},{18,... | collective-permute-start | bytes 393224 | tf_op jit(solution)/shard_map/ppermute | solution.py:364
  36.9 6.9 %collective-permute-start.6 = (bf16[128,512]{1,0:T(8,128)(2,1)}, bf16[128,512]{1,0:T(8,128)(2,1)S(1)}, u32[]{:S(2)}, u32[]{:S(2)}) collective-permute-start(bf16[128,512]{1,0:T(8,128)(2,1)} %get-tuple-element.21), channel_id=1, source_target_pairs={{0,8},{2,10},{4,12},{6,14},{8,0},{10,2},{12,4},{14,6},{16,24},{18,... | collective-permute-start | bytes 393224 | tf_op jit(solution)/shard_map/ppermute | solution.py:364
  38.1 7.1 %collective-permute-start.7 = (bf16[128,512]{1,0:T(8,128)(2,1)}, bf16[128,512]{1,0:T(8,128)(2,1)S(1)}, u32[]{:S(2)}, u32[]{:S(2)}) collective-permute-start(bf16[128,512]{1,0:T(8,128)(2,1)} %get-tuple-element.22), channel_id=1, source_target_pairs={{0,10},{2,12},{4,14},{6,8},{8,2},{10,4},{12,6},{14,0},{16,26},{18,... | collective-permute-start | bytes 393224 | tf_op jit(solution)/shard_map/ppermute | solution.py:364
  38.6 17.3 %copy-start.5 = (bf16[128,512]{1,0:T(8,128)(2,1)}, bf16[128,512]{1,0:T(8,128)(2,1)S(1)}, u32[]{:S(2)}) copy-start(bf16[128,512]{1,0:T(8,128)(2,1)S(1)} %collective-permute-done.3.refs_5_) | copy-start | bytes 393220
  38.6 10.2 %collective-permute-start.8 = (bf16[128,512]{1,0:T(8,128)(2,1)}, bf16[128,512]{1,0:T(8,128)(2,1)S(1)}, u32[]{:S(2)}, u32[]{:S(2)}) collective-permute-start(bf16[128,512]{1,0:T(8,128)(2,1)} %get-tuple-element.23), channel_id=1, source_target_pairs={{0,12},{2,14},{4,8},{6,10},{8,4},{10,6},{12,0},{14,2},{16,28},{18,... | collective-permute-start | bytes 393224 | tf_op jit(solution)/shard_map/ppermute | solution.py:364
  41.6 14.2 %copy-start.6 = (bf16[128,512]{1,0:T(8,128)(2,1)}, bf16[128,512]{1,0:T(8,128)(2,1)S(1)}, u32[]{:S(2)}) copy-start(bf16[128,512]{1,0:T(8,128)(2,1)S(1)} %collective-permute-done.4.refs_6_) | copy-start | bytes 393220
  41.6 8.1 %collective-permute-start.9 = (bf16[128,512]{1,0:T(8,128)(2,1)}, bf16[128,512]{1,0:T(8,128)(2,1)S(1)}, u32[]{:S(2)}, u32[]{:S(2)}) collective-permute-start(bf16[128,512]{1,0:T(8,128)(2,1)} %get-tuple-element.24), channel_id=1, source_target_pairs={{0,14},{2,8},{4,10},{6,12},{8,6},{10,0},{12,2},{14,4},{16,30},{18,... | collective-permute-start | bytes 393224 | tf_op jit(solution)/shard_map/ppermute | solution.py:364
  41.9 13.9 %copy-start.7 = (bf16[128,512]{1,0:T(8,128)(2,1)}, bf16[128,512]{1,0:T(8,128)(2,1)S(1)}, u32[]{:S(2)}) copy-start(bf16[128,512]{1,0:T(8,128)(2,1)S(1)} %collective-permute-done.5.refs_7_) | copy-start | bytes 393220
  42.0 13.9 %copy-start.1 = (bf16[16,16,256]{2,1,0:T(8,128)(2,1)}, bf16[16,16,256]{2,1,0:T(8,128)(2,1)S(1)}, u32[]{:S(2)}) copy-start(bf16[16,16,256]{2,1,0:T(8,128)(2,1)S(1)} %all-to-all-done.refs_0_) | copy-start | bytes 393220
  42.0 13.5 %collective-permute-start = (bf16[16,16,256]{2,1,0:T(8,128)(2,1)S(1)}, bf16[16,16,256]{2,1,0:T(8,128)(2,1)S(1)}, u32[]{:S(2)}, u32[]{:S(2)}) collective-permute-start(bf16[16,16,256]{2,1,0:T(8,128)(2,1)S(1)} %all-to-all-done.refs_0_), channel_id=1, source_target_pairs={{0,2},{2,4},{4,6},{6,0},{1,3},{3,5},{5,7},{7,1},{8,10},{10,12},{12... | collective-permute-start | bytes 393224 | tf_op jit(solution)/shard_map/ppermute | solution.py:354
  43.8 12.1 %copy-start.8 = (bf16[128,512]{1,0:T(8,128)(2,1)}, bf16[128,512]{1,0:T(8,128)(2,1)S(1)}, u32[]{:S(2)}) copy-start(bf16[128,512]{1,0:T(8,128)(2,1)S(1)} %collective-permute-done.6.refs_8_) | copy-start | bytes 393220
  43.8 11.7 %collective-permute-start.1 = (bf16[16,16,256]{2,1,0:T(8,128)(2,1)S(1)}, bf16[16,16,256]{2,1,0:T(8,128)(2,1)S(1)}, u32[]{:S(2)}, u32[]{:S(2)}) collective-permute-start(bf16[16,16,256]{2,1,0:T(8,128)(2,1)S(1)} %all-to-all-done.refs_0_), channel_id=1, source_target_pairs={{0,4},{2,6},{4,0},{6,2},{1,5},{3,7},{5,1},{7,3},{8,12},{10,14},{12... | collective-permute-start | bytes 393224 | tf_op jit(solution)/shard_map/ppermute | solution.py:354
  45.2 10.7 %copy-start.9 = (bf16[128,512]{1,0:T(8,128)(2,1)}, bf16[128,512]{1,0:T(8,128)(2,1)S(1)}, u32[]{:S(2)}) copy-start(bf16[128,512]{1,0:T(8,128)(2,1)S(1)} %collective-permute-done.7.refs_9_) | copy-start | bytes 393220
  45.2 10.7 %collective-permute-start.2 = (bf16[16,16,256]{2,1,0:T(8,128)(2,1)S(1)}, bf16[16,16,256]{2,1,0:T(8,128)(2,1)S(1)}, u32[]{:S(2)}, u32[]{:S(2)}) collective-permute-start(bf16[16,16,256]{2,1,0:T(8,128)(2,1)S(1)} %all-to-all-done.refs_0_), channel_id=1, source_target_pairs={{0,6},{2,0},{4,2},{6,4},{1,7},{3,1},{5,3},{7,5},{8,14},{10,8},{12,... | collective-permute-start | bytes 393224 | tf_op jit(solution)/shard_map/ppermute | solution.py:354
  48.7 7.2 %copy-start.10 = (bf16[128,512]{1,0:T(8,128)(2,1)}, bf16[128,512]{1,0:T(8,128)(2,1)S(1)}, u32[]{:S(2)}) copy-start(bf16[128,512]{1,0:T(8,128)(2,1)S(1)} %collective-permute-done.8.refs_10_) | copy-start | bytes 393220
  59.1 31.7 %all-to-all-start.1 = ((bf16[16,4,16,128]{3,2,1,0:T(8,128)(2,1)}), bf16[16,4,16,128]{3,2,1,0:T(8,128)(2,1)S(1)}, u32[]{:S(2)}, u32[]{:S(2)}) async-start(bf16[16,4,16,128]{3,2,1,0:T(8,128)(2,1)} %partial_queries.1), calls=%async_computation.1 | async-start | bytes 524288 | tf_op jit(solution)/shard_map/all_to_all | solution.py:385
  68.4 15.7 %copy-start.15 = (s32[16]{0:T(128)S(1)}, s32[16]{0:T(128)}, u32[]{:S(2)}) copy-start(s32[16]{0:T(128)} %lengths_ref.1) | copy-start | bytes 196
  78.6 7.3 %collective-permute-start.10 = (bf16[1152,128]{1,0:T(8,128)(2,1)}, bf16[1152,128]{1,0:T(8,128)(2,1)S(1)}, u32[]{:S(2)}, u32[]{:S(2)}) collective-permute-start(bf16[1152,128]{1,0:T(8,128)(2,1)} %get-tuple-element.26), channel_id=1, source_target_pairs={{0,2},{2,4},{4,6},{6,0},{1,3},{3,5},{5,7},{7,1},{8,10},{10,12},{12... | collective-permute-start | bytes 884744 | tf_op jit(solution)/shard_map/ppermute | solution.py:354
  80.2 10.6 %collective-permute-start.11 = (bf16[1152,128]{1,0:T(8,128)(2,1)}, bf16[1152,128]{1,0:T(8,128)(2,1)S(1)}, u32[]{:S(2)}, u32[]{:S(2)}) collective-permute-start(bf16[1152,128]{1,0:T(8,128)(2,1)} %get-tuple-element.27), channel_id=1, source_target_pairs={{0,4},{2,6},{4,0},{6,2},{1,5},{3,7},{5,1},{7,3},{8,12},{10,14},{12... | collective-permute-start | bytes 884744 | tf_op jit(solution)/shard_map/ppermute | solution.py:354
  82.3 8.5 %collective-permute-start.12 = (bf16[1152,128]{1,0:T(8,128)(2,1)}, bf16[1152,128]{1,0:T(8,128)(2,1)S(1)}, u32[]{:S(2)}, u32[]{:S(2)}) collective-permute-start(bf16[1152,128]{1,0:T(8,128)(2,1)} %get-tuple-element.28), channel_id=1, source_target_pairs={{0,6},{2,0},{4,2},{6,4},{1,7},{3,1},{5,3},{7,5},{8,14},{10,8},{12,... | collective-permute-start | bytes 884744 | tf_op jit(solution)/shard_map/ppermute | solution.py:354
  125.7 7.6 %collective-permute-start.13 = (f32[1,128]{1,0:T(1,128)}, f32[1,128]{1,0:T(1,128)S(1)}, u32[]{:S(2)}, u32[]{:S(2)}) collective-permute-start(f32[1,128]{1,0:T(1,128)} %half_tallies.1.here_ref), channel_id=1, source_target_pairs={{0,1},{1,0},{2,3},{3,2},{4,5},{5,4},{6,7},{7,6},{8,9},{9,8},{10,11... | collective-permute-start | bytes 1544 | tf_op jit(solution)/shard_map/ppermute | solution.py:391
  (9 other events, 16.2 us)

commit v2 on v1

v2 whole, which is shorter than its diff:
```python
import functools
import math

import jax
import jax.numpy as jnp
from jax import lax
from jax.experimental import pallas as pl
from jax.experimental.pallas import tpu as pltpu
from jax.sharding import PartitionSpec as P

HEAD_SIZE = 128
QUERY_HEADS = 32
KEY_VALUE_HEADS = 4
GROUP = QUERY_HEADS // KEY_VALUE_HEADS
ANSWERS = 64
PROMPT_DEV = 2
ROPE_BASE = 500000.0
BF = jnp.bfloat16
F32 = jnp.float32

VMEM = pl.BlockSpec(memory_space=pltpu.VMEM)
SMEM = pl.BlockSpec(memory_space=pltpu.SMEM)
ANY = pl.BlockSpec(memory_space=pl.ANY)
HBM = pl.BlockSpec(memory_space=pltpu.HBM)


def limit(mib):
    return pltpu.CompilerParams(vmem_limit_bytes=mib * 2**20)


def cost(flops, bytes_accessed):
    return pl.CostEstimate(flops=flops, bytes_accessed=bytes_accessed, transcendentals=0)


def rope_tables(positions):
    halves = HEAD_SIZE // 2
    frequency = ROPE_BASE ** (-jnp.arange(halves, dtype=F32) * 2.0 / HEAD_SIZE)
    angles = positions[:, None] * frequency
    cosine, sine = jnp.cos(angles), jnp.sin(angles)
    return jnp.concatenate([cosine, cosine], -1), jnp.concatenate([-sine, sine], -1)


def rows_kernel(n_dp, lengths_ref, hidden_ref, out_ref, tiles, sems):
    samples, block = tiles.shape[0], tiles.shape[1]
    copies = []
    for i in range(samples):
        at = pl.multiple_of(((lengths_ref[i] - 1) // block) * block, block)
        copy = pltpu.make_async_copy(
            hidden_ref.at[i, pl.ds(at, block), :], tiles.at[i], sems.at[i]
        )
        copy.start()
        copies.append(copy)
    lane = lax.broadcasted_iota(jnp.int32, (samples, samples * block), 1)
    row = lax.broadcasted_iota(jnp.int32, (samples, samples * block), 0)
    chosen = jnp.zeros(lane.shape, jnp.int32)
    for i in range(samples):
        chosen = jnp.where(row == i, i * block + (lengths_ref[i] - 1) % block, chosen)
    pick = jnp.where(lane == chosen, 1.0, 0.0).astype(BF)
    for copy in copies:
        copy.wait()
    stacked = tiles[...].reshape(samples * block, tiles.shape[2])
    rows = jnp.dot(pick, stacked, preferred_element_type=F32).astype(BF)
    width = rows.shape[1] // n_dp
    for d in range(n_dp):
        for side, source in enumerate((d, d ^ 1)):
            out_ref[d, :, side * width : (side + 1) * width] = rows[
                :, source * width : (source + 1) * width
            ]


def scoring_rows(lengths, hidden, n_dp):
    samples, _, features = hidden.shape
    width = 2 * features // n_dp
    return pl.pallas_call(
        functools.partial(rows_kernel, n_dp),
        out_shape=jax.ShapeDtypeStruct((n_dp, samples, width), BF),
        in_specs=[SMEM, HBM],
        out_specs=VMEM,
        scratch_shapes=[
            pltpu.VMEM((samples, 16, features), BF),
            pltpu.SemaphoreType.DMA((samples,)),
        ],
        cost_estimate=cost(2 * samples * 256 * features, samples * 16 * features * 2),
        compiler_params=limit(62),
        name="scoring_rows",
    )(lengths, hidden)


def cut_kernel(n_tensor, weight_ref, *out_refs):
    t, parity = lax.axis_index("tensor"), lax.axis_index("dp") % 2
    part = out_refs[0].shape[1]
    for side in range(2):
        for s in range(n_tensor):
            column = 2 * ((t + s) % n_tensor) + (parity ^ side)
            at = pl.multiple_of(column * part, part)
            out_refs[side * n_tensor + s][...] = weight_ref[:, pl.ds(at, part)]


def cut_weight(weight, n_tensor):
    rows, columns = weight.shape
    part = columns // (2 * n_tensor)
    count = 2 * n_tensor
    return pl.pallas_call(
        functools.partial(cut_kernel, n_tensor),
        out_shape=[jax.ShapeDtypeStruct((rows, part), BF)] * count,
        in_specs=[VMEM],
        out_specs=[VMEM] * count,
        cost_estimate=cost(1000, 2 * rows * columns * 2),
        compiler_params=limit(4),
        name="cut_weight",
    )(weight)


def kv_kernel(
    n_tensor, h_ref, k_ref, v_ref, s_ref, cos_ref, sin_ref, after_ref, *refs
):
    out_refs = refs[:n_tensor]
    x_ref, wv_ref, w_ref, x_sems, w_sems = refs[n_tensor:]
    steps, rows, _ = x_ref.shape
    heads = QUERY_HEADS
    t = lax.axis_index("tensor")
    copies = [pltpu.make_async_copy(h_ref.at[pl.ds(0, rows), :], x_ref.at[0], x_sems.at[0])]
    for s in range(n_tensor):
        at = pl.multiple_of(((t + s) % n_tensor) * HEAD_SIZE, HEAD_SIZE)
        copies.append(
            pltpu.make_async_copy(
                k_ref.at[:, pl.ds(at, HEAD_SIZE)],
                w_ref.at[:, s * HEAD_SIZE : (s + 1) * HEAD_SIZE],
                w_sems.at[s],
            )
        )
    value_copy = pltpu.make_async_copy(v_ref, wv_ref, w_sems.at[n_tensor])
    copies.append(value_copy)
    for i in range(1, steps):
        copies.append(
            pltpu.make_async_copy(
                h_ref.at[pl.ds(i * rows, rows), :], x_ref.at[i], x_sems.at[i]
            )
        )
    for copy in copies:
        copy.start()

    head = lax.broadcasted_iota(jnp.int32, (heads, KEY_VALUE_HEADS * HEAD_SIZE), 0)
    column = lax.broadcasted_iota(jnp.int32, (heads, KEY_VALUE_HEADS * HEAD_SIZE), 1)
    spread = jnp.concatenate([s_ref[...]] * KEY_VALUE_HEADS, axis=1)
    full = jnp.where(head // GROUP == column // HEAD_SIZE, spread, 0.0)
    high = full.astype(BF)
    low = (full - high.astype(F32)).astype(BF)
    both = jnp.concatenate([high, low], axis=0)
    cosine = jnp.concatenate([cos_ref[...]] * (rows // cos_ref.shape[0]), axis=0)
    sine = jnp.concatenate([sin_ref[...]] * (rows // sin_ref.shape[0]), axis=0)

    for i in range(steps):
        copies[0 if i == 0 else n_tensor + 1 + i].wait()
        if i == 0:
            for s in range(n_tensor):
                copies[1 + s].wait()
        x = x_ref[i]
        keys = jnp.dot(x, w_ref[...], preferred_element_type=F32)
        for s in range(n_tensor):
            k = keys[:, s * HEAD_SIZE : (s + 1) * HEAD_SIZE]
            rotated = k * cosine + pltpu.roll(k, HEAD_SIZE // 2, 1) * sine
            out_refs[s][i * rows : (i + 1) * rows, :] = rotated.astype(BF)
        if i == 0:
            value_copy.wait()
            z = lax.dot_general(
                both, wv_ref[...], (((1,), (1,)), ((), ())), preferred_element_type=F32
            )
            z = z[:heads] + z[heads:]
            z_high = z.astype(BF)
            z_low = (z - z_high.astype(F32)).astype(BF)
            z = jnp.concatenate([z_high, z_low], axis=0)
        u = lax.dot_general(z, x, (((1,), (1,)), ((), ())), preferred_element_type=F32)
        u = u[:heads] + u[heads:]
        u_high = u.astype(BF)
        u_low = (u - u_high.astype(F32)).astype(BF)
        for g in range(n_tensor):
            slot = (g - t + n_tensor) % n_tensor
            mine = jnp.concatenate(
                [u_high[g * GROUP : (g + 1) * GROUP], u_low[g * GROUP : (g + 1) * GROUP]], axis=0
            )
            for s in range(n_tensor):

                @pl.when(slot == s)
                def _():
                    for c in range(rows // HEAD_SIZE):
                        base = steps * rows + (i * (rows // HEAD_SIZE) + c) * 2 * GROUP
                        out_refs[s][base : base + 2 * GROUP, :] = mine[
                            :, c * HEAD_SIZE : (c + 1) * HEAD_SIZE
                        ]


def keys_and_values(flat, key_weight, value_weight, score_rows, cosine, sine, after, n_tensor):
    total, features = flat.shape
    rows = 256
    packed = total + (total // HEAD_SIZE) * 2 * GROUP
    return pl.pallas_call(
        functools.partial(kv_kernel, n_tensor),
        in_specs=[HBM, HBM, HBM, VMEM, VMEM, VMEM, ANY],
        out_specs=[VMEM] * n_tensor,
        scratch_shapes=[
            pltpu.VMEM((total // rows, rows, features), BF),
            pltpu.VMEM(value_weight.shape, BF),
            pltpu.VMEM(key_weight.shape, BF),
            pltpu.SemaphoreType.DMA((total // rows,)),
            pltpu.SemaphoreType.DMA((n_tensor + 1,)),
        ],
        out_shape=[jax.ShapeDtypeStruct((packed, HEAD_SIZE), BF)] * n_tensor,
        cost_estimate=cost(2 * total * features * 640, 9 * 2**20),
        compiler_params=limit(52),
        name="keys_and_values",
    )(flat, key_weight, value_weight, score_rows, cosine, sine, after)


def query_kernel(n_tensor, *refs):
    x_refs = refs[:n_tensor]
    w_refs = refs[n_tensor : 3 * n_tensor]
    out_ref = refs[3 * n_tensor + 1]
    n_dp, heads, samples, _ = out_ref.shape
    x = jnp.concatenate(
        [x_refs[s][...].reshape(n_dp * samples, -1) for s in range(n_tensor)], axis=1
    )
    w = jnp.concatenate(
        [w_refs[side * n_tensor + s][...] for s in range(n_tensor) for side in range(2)], axis=0
    )
    q = jnp.dot(x, w, preferred_element_type=F32).astype(BF)
    for h in range(heads):
        out_ref[:, h, :, :] = q[:, h * HEAD_SIZE : (h + 1) * HEAD_SIZE].reshape(
            n_dp, samples, HEAD_SIZE
        )


def partial_queries(pieces, weights, after):
    n_dp, samples, width = pieces[0].shape
    heads = weights[0].shape[1] // HEAD_SIZE
    return pl.pallas_call(
        functools.partial(query_kernel, len(pieces)),
        out_shape=jax.ShapeDtypeStruct((n_dp, heads, samples, HEAD_SIZE), BF),
        in_specs=[VMEM] * (len(pieces) + len(weights)) + [ANY],
        out_specs=VMEM,
        cost_estimate=cost(2 * n_dp * samples * width * 4 * heads * HEAD_SIZE, 2 * 2**20),
        compiler_params=limit(8),
        name="partial_queries",
    )(*pieces, *weights, after)


def attention_kernel(n_tensor, q_ref, *refs):
    kv_refs = refs[:n_tensor]
    cos_ref, sin_ref, lengths_ref, prompt_ref, answer_ref, out_ref = refs[n_tensor:]
    n_dp, half, samples, _ = q_ref.shape
    q = jnp.zeros((2 * half * samples, HEAD_SIZE), F32)
    for pair in range(n_dp // 2):
        block = q_ref[2 * pair : 2 * pair + 2].reshape(2 * half * samples, HEAD_SIZE)
        q = q + block.astype(F32)
    heads = 2 * half
    cosine = jnp.concatenate([cos_ref[...]] * heads, axis=0)
    sine = jnp.concatenate([sin_ref[...]] * heads, axis=0)
    q = (q * cosine + pltpu.roll(q, HEAD_SIZE // 2, 1) * sine).astype(BF)
    total = samples * 64
    chunks = total // HEAD_SIZE
    own = lax.broadcasted_iota(jnp.int32, (samples, HEAD_SIZE), 0)
    lengths = jnp.zeros((samples, HEAD_SIZE), jnp.int32)
    for i in range(samples):
        lengths = jnp.where(own == i, lengths_ref[i], lengths)
    lengths = jnp.concatenate([lengths] * heads, axis=0)
    lane = lax.broadcasted_iota(jnp.int32, (heads * samples, HEAD_SIZE), 1)
    row = lax.broadcasted_iota(jnp.int32, (heads * samples, HEAD_SIZE), 0)
    start = (row % samples) * 64
    scores, values = [], []
    for c in range(chunks):
        k = kv_refs[0][c * HEAD_SIZE : (c + 1) * HEAD_SIZE].astype(F32)
        base = total + c * 2 * GROUP
        u = kv_refs[0][base : base + 2 * GROUP].astype(F32)
        for s in range(1, n_tensor):
            k = k + kv_refs[s][c * HEAD_SIZE : (c + 1) * HEAD_SIZE].astype(F32)
            u = u + kv_refs[s][base : base + 2 * GROUP].astype(F32)
        u = u[:GROUP] + u[GROUP:]
        score = lax.dot_general(
            q, k.astype(BF), (((1,), (1,)), ((), ())), preferred_element_type=F32
        ) / math.sqrt(HEAD_SIZE)
        position = lane + c * HEAD_SIZE - start
        scores.append(jnp.where((position >= 0) & (position < lengths), score, -1e30))
        values.append(
            jnp.broadcast_to(u[:, None, :], (heads, samples, HEAD_SIZE)).reshape(
                heads * samples, HEAD_SIZE
            )
        )
    top = scores[0]
    for c in range(1, chunks):
        top = jnp.maximum(top, scores[c])
    top = jnp.max(top, axis=1, keepdims=True)
    below = jnp.zeros_like(scores[0])
    above = jnp.zeros_like(scores[0])
    for c in range(chunks):
        weight = jnp.exp(scores[c] - top)
        below = below + weight
        above = above + weight * values[c]
    part = jnp.sum(above, axis=1, keepdims=True) / jnp.sum(below, axis=1, keepdims=True)
    rating = jnp.sum(part.reshape(heads, samples, 1), axis=0)
    out_rows = out_ref.shape[0]
    owner = lax.broadcasted_iota(jnp.int32, (out_rows, HEAD_SIZE), 0) // n_tensor
    column = lax.broadcasted_iota(jnp.int32, (out_rows, HEAD_SIZE), 1)
    out = jnp.zeros((out_rows, HEAD_SIZE), F32)
    for i in range(samples):
        prompt = prompt_ref[i]
        place = ((prompt % PROMPT_DEV) * ANSWERS + answer_ref[i]).astype(F32)
        value = jnp.broadcast_to(rating[i : i + 1, :], (out_rows, HEAD_SIZE))
        entry = jnp.where(column == 0, value, jnp.where(column == 1, place, 0.0))
        out = jnp.where(owner == prompt // PROMPT_DEV, entry, out)
    out_ref[...] = out


def partial_ratings(queries, kv, cosine, sine, lengths, prompt_of, answers):
    n_tensor = len(kv)
    n_dp = queries.shape[0]
    return pl.pallas_call(
        functools.partial(attention_kernel, n_tensor),
        out_shape=jax.ShapeDtypeStruct((n_dp * n_tensor, HEAD_SIZE), F32),
        in_specs=[VMEM] * (n_tensor + 3) + [SMEM] * 3,
        out_specs=VMEM,
        cost_estimate=cost(2 * 128 * 128 * 1024, 2 * 2**20),
        compiler_params=limit(12),
        name="partial_ratings",
    )(queries, *kv, cosine, sine, lengths, prompt_of, answers)


def tally_kernel(n_tensor, rows_ref, out_ref):
    rows = rows_ref[...]
    summed = rows.reshape(rows.shape[0] // n_tensor, n_tensor, HEAD_SIZE)
    rating = jnp.sum(summed[:, :, 0:1], axis=1)
    place = summed[:, 0, 1:2].astype(jnp.int32)
    reward = 1.0 / (1.0 + jnp.exp(-rating))
    lane = lax.broadcasted_iota(jnp.int32, (rating.shape[0], HEAD_SIZE), 1)
    out_ref[...] = jnp.sum(jnp.where(lane == place, reward, 0.0), axis=0, keepdims=True)


def half_tallies(rows, n_tensor):
    return pl.pallas_call(
        functools.partial(tally_kernel, n_tensor),
        out_shape=jax.ShapeDtypeStruct((1, HEAD_SIZE), F32),
        in_specs=[VMEM],
        out_specs=VMEM,
        compiler_params=limit(2),
        name="half_tallies",
    )(rows)


def share_kernel(here_ref, there_ref, out_ref):
    total = here_ref[...] + there_ref[...]
    for q in range(PROMPT_DEV):
        tally = total[:, q * ANSWERS : (q + 1) * ANSWERS]
        out_ref[q : q + 1, :] = tally / jnp.sum(tally, axis=1, keepdims=True)


def shares(here, there):
    return pl.pallas_call(
        share_kernel,
        out_shape=jax.ShapeDtypeStruct((PROMPT_DEV, ANSWERS), F32),
        in_specs=[VMEM, VMEM],
        out_specs=VMEM,
        compiler_params=limit(2),
        name="shares",
    )(here, there)


def shards(hidden, lengths, answers, prompt_of, query_weight, key_weight, value_weight, score_vec):
    samples, positions, features = hidden.shape
    n_dp, n_tensor, n_seq = (lax.axis_size(a) for a in ("dp", "tensor", "seq"))

    def over_tensor(value, s):
        return lax.ppermute(value, "tensor", [(i, (i + s) % n_tensor) for i in range(n_tensor)])

    def weight_piece(value, side, s):
        if side == 0 and s == 0:
            return value
        pairs = [
            (d * n_tensor + i, (d ^ side) * n_tensor + (i + s) % n_tensor)
            for d in range(n_dp)
            for i in range(n_tensor)
        ]
        return lax.ppermute(value, ("dp", "tensor"), pairs)

    rows = scoring_rows(lengths, hidden, n_dp)
    moved = lax.all_to_all(rows, "dp", 0, 0, tiled=True)

    cut = cut_weight(query_weight, n_tensor)
    weights = [weight_piece(cut[k], k // n_tensor, k % n_tensor) for k in range(2 * n_tensor)]

    key_cos, key_sin = rope_tables(jnp.arange(positions, dtype=F32))
    kv = keys_and_values(
        hidden.reshape(samples * positions, features),
        key_weight,
        value_weight,
        score_vec.reshape(QUERY_HEADS, HEAD_SIZE),
        key_cos,
        key_sin,
        moved,
        n_tensor,
    )
    pieces = [moved] + [over_tensor(moved, s) for s in range(1, n_tensor)]
    queries = partial_queries(pieces, weights, kv[0])
    queries, *kv = lax.optimization_barrier((queries, *kv))
    arrived = lax.all_to_all(queries, "dp", 0, 0, tiled=True)
    kv = [kv[0]] + [over_tensor(kv[s], s) for s in range(1, n_tensor)]
    query_cos, query_sin = rope_tables((lengths - 1).astype(F32))
    rated = partial_ratings(arrived, kv, query_cos, query_sin, lengths, prompt_of, answers)
    gathered = lax.all_to_all(rated, ("dp", "tensor"), 0, 0, tiled=True)
    here = half_tallies(gathered, n_tensor)
    there = lax.ppermute(here, "seq", [(i, (i + 1) % n_seq) for i in range(n_seq)])
    return shares(here, there)


def solution(mesh):
    placed = (
        P(("groups", "dp", "seq"), None, "tensor"),
        P(("groups", "dp", "seq")),
        P(("groups", "dp", "seq")),
        P(("groups", "dp", "seq")),
        P(("tensor", "dp"), None),
        P("tensor", None),
        P("tensor", None),
        P(),
    )
    return jax.shard_map(
        shards, mesh=mesh, in_specs=placed, out_specs=P(("groups", "dp"), None), check_vma=False
    )
```

time: 136 us -> 117 us (0.86)
  Pallas kernels: 23.6 us -> 15.2 us
  local copies, waits for them, and re-layouts: 3.43 us -> 0.03 us
  waiting for transfers between devices: 17.9 us -> 14.5 us
  other arithmetic: 2.28 us -> 0.43 us
    ppermute x7, waiting for transfers between devices: 4.84 us -> 1.28 us  [weight_piece(): return lax.ppermute(value, ('dp', 'tensor'), pairs)]
    ppermute x1, starting transfers between devices: 6.54 us -> 3.82 us  [shards(): lax.ppermute(here, 'seq', [(i, (i + 1) % n_seq) for i in range(n_seq)])]
    pallas_call x1, Pallas kernels: 2.33 us -> 0.09 us  [cut_weight(): pl.pallas_call(functools.partial(cut_kernel, n_tensor), out_shape=[jax.Sh...]
    unnamed x34 -> x10, local copies, waits for them, and re-layouts: 2.11 us -> 0.03 us
    pallas_call x1, Pallas kernels: 10.2 us -> 8.68 us  [keys_and_values(): pl.pallas_call(functools.partial(kv_kernel, n_tensor), in_specs=[HBM, HBM...]
    pallas_call x1, Pallas kernels: 2.58 us -> 1.15 us  [partial_queries(): pl.pallas_call(functools.partial(query_kernel, len(pieces)), out_shape=ja...]
    pallas_call x1, Pallas kernels: 2.65 us -> 1.24 us  [partial_ratings(): pl.pallas_call(functools.partial(attention_kernel, n_tensor), out_shape=j...]
  transfers between devices with their start and end apart: 16 -> 16, of which waited for: 8 -> 7; matrix products, arithmetic and copies ran while one was open for 2% -> 0% of each run, Pallas kernels for 9% -> 8%
where the time goes in v2:
time: 117 us; the launch traced here: 116 us
  starting transfers between devices  57.4 us (49%)
  blocking collectives  28.6 us (24%)
  Pallas kernels  15.2 us (13%)
  waiting for transfers between devices  14.5 us (12%)
    all_to_all x1, blocking collectives, shards(): gathered = lax.all_to_all(rated, ('dp', 'tensor'), 0, 0, tiled=True)  28.6 us
    all_to_all x1, starting transfers between devices, shards(): moved = lax.all_to_all(rows, 'dp', 0, 0, tiled=True)  24.5 us
    ppermute x6, waiting for transfers between devices, over_tensor(): lax.ppermute(value, 'tensor', [(i, (i + s) % n_tensor) for i in range(n_t...  11.2 us
    ppermute x6, starting transfers between devices, over_tensor(): lax.ppermute(value, 'tensor', [(i, (i + s) % n_tensor) for i in range(n_t...  10.3 us
    all_to_all x1, starting transfers between devices, shards(): arrived = lax.all_to_all(queries, 'dp', 0, 0, tiled=True)  9.38 us
    ppermute x7, starting transfers between devices, weight_piece(): return lax.ppermute(value, ('dp', 'tensor'), pairs)  9.36 us
    pallas_call x1, Pallas kernels, keys_and_values(): pl.pallas_call(functools.partial(kv_kernel, n_tensor), in_specs=[HBM, HBM...  8.68 us
    ppermute x1, starting transfers between devices, shards(): lax.ppermute(here, 'seq', [(i, (i + 1) % n_seq) for i in range(n_seq)])  3.82 us
  transfers between devices with their start and end apart: 16, of which 7 were waited for; matrix products, arithmetic and copies ran while one was open for 0% of the time, Pallas kernels for 8%

profile of v2, /device:TPU:33, one launch (start us, length us, event | category | flops | bytes accessed | tf_op | source)
XLA Modules:
  0.0 116.3 jit_solution(7383599371924609146)
XLA Ops:
  0.0 3.1 %scoring_rows.1 = bf16[16,16,256]{2,1,0:T(8,128)(2,1)} custom-call(s32[16]{0:T(128)} %refs_6_.1, bf16[16,64,2048]{2,1,0:T(8,128)(2,1)} %hidden_ref.1), custom_call_target="tpu_custom_call" | custom-call | flops 16777216 | bytes 1048576 | tf_op jit(solution)/shard_map/scoring_rows/pallas_call | solution.py:74
  3.1 24.5 %all-to-all-start = ((bf16[16,16,256]{2,1,0:T(8,128)(2,1)}), bf16[16,16,256]{2,1,0:T(8,128)(2,1)S(1)}, u32[]{:S(2)}, u32[]{:S(2)}) async-start(bf16[16,16,256]{2,1,0:T(8,128)(2,1)} %scoring_rows.1), calls=%async_computation | async-start | bytes 262144 | tf_op jit(solution)/shard_map/all_to_all | solution.py:384
  27.8 1.5 %collective-permute-start.3 = (bf16[128,512]{1,0:T(8,128)(2,1)S(1)}, bf16[128,512]{1,0:T(8,128)(2,1)S(1)}, u32[]{:S(2)}, u32[]{:S(2)}) collective-permute-start(bf16[128,512]{1,0:T(8,128)(2,1)S(1)} %get-tuple-element.23), channel_id=1, source_target_pairs={{0,2},{2,4},{4,6},{6,0},{8,10},{10,12},{12,14},{14,8},{16,18},{18,... | collective-permute-start | bytes 393224 | tf_op jit(solution)/shard_map/ppermute | solution.py:381
  29.2 2.7 %collective-permute-start.4 = (bf16[128,512]{1,0:T(8,128)(2,1)S(1)}, bf16[128,512]{1,0:T(8,128)(2,1)S(1)}, u32[]{:S(2)}, u32[]{:S(2)}) collective-permute-start(bf16[128,512]{1,0:T(8,128)(2,1)S(1)} %get-tuple-element.24), channel_id=1, source_target_pairs={{0,4},{2,6},{4,0},{6,2},{8,12},{10,14},{12,8},{14,10},{16,20},{18,... | collective-permute-start | bytes 393224 | tf_op jit(solution)/shard_map/ppermute | solution.py:381
  32.0 1.0 collective-permute-start.5
  33.0 1.2 collective-permute-start.6
  34.9 1.7 %collective-permute-start.8 = (bf16[128,512]{1,0:T(8,128)(2,1)S(1)}, bf16[128,512]{1,0:T(8,128)(2,1)S(1)}, u32[]{:S(2)}, u32[]{:S(2)}) collective-permute-start(bf16[128,512]{1,0:T(8,128)(2,1)S(1)} %get-tuple-element.28), channel_id=1, source_target_pairs={{0,12},{2,14},{4,8},{6,10},{8,4},{10,6},{12,0},{14,2},{16,28},{18,... | collective-permute-start | bytes 393224 | tf_op jit(solution)/shard_map/ppermute | solution.py:381
  36.6 0.9 collective-permute-done.4.refs_6_
  38.3 1.2 %all-to-all-done.after_ref.refs_0_ = bf16[16,16,256]{2,1,0:T(8,128)(2,1)S(1)} async-done(((bf16[16,16,256]{2,1,0:T(8,128)(2,1)}), bf16[16,16,256]{2,1,0:T(8,128)(2,1)S(1)}, u32[]{:S(2)}, u32[]{:S(2)}) %all-to-all-start) | async-done | bytes 131104 | tf_op jit(solution)/shard_map/all_to_all | solution.py:384
  39.4 1.4 %collective-permute-start = (bf16[16,16,256]{2,1,0:T(8,128)(2,1)S(1)}, bf16[16,16,256]{2,1,0:T(8,128)(2,1)S(1)}, u32[]{:S(2)}, u32[]{:S(2)}) collective-permute-start(bf16[16,16,256]{2,1,0:T(8,128)(2,1)S(1)} %all-to-all-done.after_ref.refs_0_), channel_id=1, source_target_pairs={{0,2},{2,4},{4,6},{6,0},{1,3},{3,5},{5,7},{7,1},{8,10},{10,12},{12... | collective-permute-start | bytes 393224 | tf_op jit(solution)/shard_map/ppermute | solution.py:371
  40.8 2.7 %collective-permute-start.1 = (bf16[16,16,256]{2,1,0:T(8,128)(2,1)S(1)}, bf16[16,16,256]{2,1,0:T(8,128)(2,1)S(1)}, u32[]{:S(2)}, u32[]{:S(2)}) collective-permute-start(bf16[16,16,256]{2,1,0:T(8,128)(2,1)S(1)} %all-to-all-done.after_ref.refs_0_), channel_id=1, source_target_pairs={{0,4},{2,6},{4,0},{6,2},{1,5},{3,7},{5,1},{7,3},{8,12},{10,14},{12... | collective-permute-start | bytes 393224 | tf_op jit(solution)/shard_map/ppermute | solution.py:371
  44.6 8.7 %keys_and_values.1 = (bf16[1152,128]{1,0:T(8,128)(2,1)S(1)}, bf16[1152,128]{1,0:T(8,128)(2,1)S(1)}, bf16[1152,128]{1,0:T(8,128)(2,1)S(1)}, bf16[1152,128]{1,0:T(8,128)(2,1)S(1)}) custom-call(bf16[1024,2048]{1,0:T(8,128)(2,1)} %bitcast.9, bf16[2048,512]{1,0:T(8,128)(2,1)} %k_ref.1, bf16[2048,512]{1,0:T(8,128)(2,1)} %v_ref.1, f32[32,128]{1,0:T(8,128)S(1)} %bitcast.8, ...), custom_call_target="tpu_custom_call" | custom-call | flops 2684354560 | bytes 9437184 | tf_op jit(solution)/shard_map/keys_and_values/pallas_call | solution.py:197
  53.3 0.9 collective-permute-done.2.refs_3_
  54.3 1.2 partial_queries.1
  55.4 9.4 %all-to-all-start.1 = ((bf16[16,4,16,128]{3,2,1,0:T(8,128)(2,1)}), bf16[16,4,16,128]{3,2,1,0:T(8,128)(2,1)S(1)}, u32[]{:S(2)}, u32[]{:S(2)}) async-start(bf16[16,4,16,128]{3,2,1,0:T(8,128)(2,1)} %partial_queries.1), calls=%async_computation.1 | async-start | bytes 524288 | tf_op jit(solution)/shard_map/all_to_all | solution.py:403
  64.8 2.5 %collective-permute-start.10 = (bf16[1152,128]{1,0:T(8,128)(2,1)S(1)}, bf16[1152,128]{1,0:T(8,128)(2,1)S(1)}, u32[]{:S(2)}, u32[]{:S(2)}) collective-permute-start(bf16[1152,128]{1,0:T(8,128)(2,1)S(1)} %get-tuple-element.36), channel_id=1, source_target_pairs={{0,2},{2,4},{4,6},{6,0},{1,3},{3,5},{5,7},{7,1},{8,10},{10,12},{12... | collective-permute-start | bytes 884744 | tf_op jit(solution)/shard_map/ppermute | solution.py:371
  67.3 1.2 %collective-permute-start.11 = (bf16[1152,128]{1,0:T(8,128)(2,1)S(1)}, bf16[1152,128]{1,0:T(8,128)(2,1)S(1)}, u32[]{:S(2)}, u32[]{:S(2)}) collective-permute-start(bf16[1152,128]{1,0:T(8,128)(2,1)S(1)} %get-tuple-element.37), channel_id=1, source_target_pairs={{0,4},{2,6},{4,0},{6,2},{1,5},{3,7},{5,1},{7,3},{8,12},{10,14},{12... | collective-permute-start | bytes 884744 | tf_op jit(solution)/shard_map/ppermute | solution.py:371
  68.5 1.9 %collective-permute-start.12 = (bf16[1152,128]{1,0:T(8,128)(2,1)S(1)}, bf16[1152,128]{1,0:T(8,128)(2,1)S(1)}, u32[]{:S(2)}, u32[]{:S(2)}) collective-permute-start(bf16[1152,128]{1,0:T(8,128)(2,1)S(1)} %get-tuple-element.38), channel_id=1, source_target_pairs={{0,6},{2,0},{4,2},{6,4},{1,7},{3,1},{5,3},{7,5},{8,14},{10,8},{12,... | collective-permute-start | bytes 884744 | tf_op jit(solution)/shard_map/ppermute | solution.py:371
  70.6 2.1 %collective-permute-done.10.refs_1_ = bf16[1152,128]{1,0:T(8,128)(2,1)S(1)} collective-permute-done((bf16[1152,128]{1,0:T(8,128)(2,1)S(1)}, bf16[1152,128]{1,0:T(8,128)(2,1)S(1)}, u32[]{:S(2)}, u32[]{:S(2)}) %collective-permute-start.10) | collective-permute-done | bytes 294944 | tf_op jit(solution)/shard_map/ppermute | solution.py:371
  72.8 8.1 %collective-permute-done.11.refs_2_ = bf16[1152,128]{1,0:T(8,128)(2,1)S(1)} collective-permute-done((bf16[1152,128]{1,0:T(8,128)(2,1)S(1)}, bf16[1152,128]{1,0:T(8,128)(2,1)S(1)}, u32[]{:S(2)}, u32[]{:S(2)}) %collective-permute-start.11) | collective-permute-done | bytes 294944 | tf_op jit(solution)/shard_map/ppermute | solution.py:371
  80.9 1.2 %partial_ratings.1 = f32[64,128]{1,0:T(8,128)S(1)} custom-call(bf16[16,4,16,128]{3,2,1,0:T(8,128)(2,1)S(1)} %all-to-all-done.1.q_ref, bf16[1152,128]{1,0:T(8,128)(2,1)S(1)} %get-tuple-element.35.refs_12_.refs_0_, bf16[1152,128]{1,0:T(8,128)(2,1)S(1)} %collective-permute-done.10.refs_1_, bf16[1152,128]{1,0:T(8,128)(2,1)S(1)} %collective-permute-done.11.refs_2_, ...), custom_call_target="tpu_custom_call" | custom-call | flops 33554432 | bytes 2097152 | tf_op jit(solution)/shard_map/partial_ratings/pallas_call | solution.py:316
  82.2 28.6 %all_to_all.21 = f32[64,1,128]{2,1,0:T(1,128)S(1)} all-to-all(f32[64,1,128]{2,1,0:T(1,128)S(1)} %bitcast.6), channel_id=1, replica_groups=mesh['groups'=2,'dp'=16,'tensor'=4,'seq'=2] {'dp','tensor'}, dimensions={0} | all-to-all | bytes 65536 | tf_op jit(solution)/shard_map/all_to_all | solution.py:407
  110.9 3.8 %collective-permute-start.13 = (f32[1,128]{1,0:T(1,128)S(1)}, f32[1,128]{1,0:T(1,128)S(1)}, u32[]{:S(2)}, u32[]{:S(2)}) collective-permute-start(f32[1,128]{1,0:T(1,128)S(1)} %half_tallies.1.here_ref), channel_id=1, source_target_pairs={{0,1},{1,0},{2,3},{3,2},{4,5},{5,4},{6,7},{7,6},{8,9},{9,8},{10,11... | collective-permute-start | bytes 1544 | tf_op jit(solution)/shard_map/ppermute | solution.py:409
  114.7 0.8 collective-permute-done.13.there_ref
  (32 shorter events, 3.8 us)
Async XLA Ops:
  0.0 27.7 %copy-start = (bf16[128,4096]{1,0:T(8,128)(2,1)S(1)}, bf16[128,4096]{1,0:T(8,128)(2,1)}, u32[]{:S(2)}) copy-start(bf16[128,4096]{1,0:T(8,128)(2,1)} %weight_ref.1) | copy-start | bytes 3145732
  0.0 44.5 %copy-start.4 = (f32[4096]{0:T(1024)S(1)}, f32[4096]{0:T(1024)}, u32[]{:S(2)}) copy-start(f32[4096]{0:T(1024)} %param.15) | copy-start | bytes 49156
  3.1 36.3 %all-to-all-start = ((bf16[16,16,256]{2,1,0:T(8,128)(2,1)}), bf16[16,16,256]{2,1,0:T(8,128)(2,1)S(1)}, u32[]{:S(2)}, u32[]{:S(2)}) async-start(bf16[16,16,256]{2,1,0:T(8,128)(2,1)} %scoring_rows.1), calls=%async_computation | async-start | bytes 262144 | tf_op jit(solution)/shard_map/all_to_all | solution.py:384
  27.8 7.1 %collective-permute-start.3 = (bf16[128,512]{1,0:T(8,128)(2,1)S(1)}, bf16[128,512]{1,0:T(8,128)(2,1)S(1)}, u32[]{:S(2)}, u32[]{:S(2)}) collective-permute-start(bf16[128,512]{1,0:T(8,128)(2,1)S(1)} %get-tuple-element.23), channel_id=1, source_target_pairs={{0,2},{2,4},{4,6},{6,0},{8,10},{10,12},{12,14},{14,8},{16,18},{18,... | collective-permute-start | bytes 393224 | tf_op jit(solution)/shard_map/ppermute | solution.py:381
  29.2 8.2 %collective-permute-start.4 = (bf16[128,512]{1,0:T(8,128)(2,1)S(1)}, bf16[128,512]{1,0:T(8,128)(2,1)S(1)}, u32[]{:S(2)}, u32[]{:S(2)}) collective-permute-start(bf16[128,512]{1,0:T(8,128)(2,1)S(1)} %get-tuple-element.24), channel_id=1, source_target_pairs={{0,4},{2,6},{4,0},{6,2},{8,12},{10,14},{12,8},{14,10},{16,20},{18,... | collective-permute-start | bytes 393224 | tf_op jit(solution)/shard_map/ppermute | solution.py:381
  32.0 6.3 %collective-permute-start.5 = (bf16[128,512]{1,0:T(8,128)(2,1)S(1)}, bf16[128,512]{1,0:T(8,128)(2,1)S(1)}, u32[]{:S(2)}, u32[]{:S(2)}) collective-permute-start(bf16[128,512]{1,0:T(8,128)(2,1)S(1)} %get-tuple-element.25), channel_id=1, source_target_pairs={{0,6},{2,0},{4,2},{6,4},{8,14},{10,8},{12,10},{14,12},{16,22},{18,... | collective-permute-start | bytes 393224 | tf_op jit(solution)/shard_map/ppermute | solution.py:381
  33.0 7.8 %collective-permute-start.6 = (bf16[128,512]{1,0:T(8,128)(2,1)S(1)}, bf16[128,512]{1,0:T(8,128)(2,1)S(1)}, u32[]{:S(2)}, u32[]{:S(2)}) collective-permute-start(bf16[128,512]{1,0:T(8,128)(2,1)S(1)} %get-tuple-element.26), channel_id=1, source_target_pairs={{0,8},{2,10},{4,12},{6,14},{8,0},{10,2},{12,4},{14,6},{16,24},{18,... | collective-permute-start | bytes 393224 | tf_op jit(solution)/shard_map/ppermute | solution.py:381
  34.1 9.8 %collective-permute-start.7 = (bf16[128,512]{1,0:T(8,128)(2,1)S(1)}, bf16[128,512]{1,0:T(8,128)(2,1)S(1)}, u32[]{:S(2)}, u32[]{:S(2)}) collective-permute-start(bf16[128,512]{1,0:T(8,128)(2,1)S(1)} %get-tuple-element.27), channel_id=1, source_target_pairs={{0,10},{2,12},{4,14},{6,8},{8,2},{10,4},{12,6},{14,0},{16,26},{18,... | collective-permute-start | bytes 393224 | tf_op jit(solution)/shard_map/ppermute | solution.py:381
  34.9 18.4 %collective-permute-start.8 = (bf16[128,512]{1,0:T(8,128)(2,1)S(1)}, bf16[128,512]{1,0:T(8,128)(2,1)S(1)}, u32[]{:S(2)}, u32[]{:S(2)}) collective-permute-start(bf16[128,512]{1,0:T(8,128)(2,1)S(1)} %get-tuple-element.28), channel_id=1, source_target_pairs={{0,12},{2,14},{4,8},{6,10},{8,4},{10,6},{12,0},{14,2},{16,28},{18,... | collective-permute-start | bytes 393224 | tf_op jit(solution)/shard_map/ppermute | solution.py:381
  37.5 15.8 %collective-permute-start.9 = (bf16[128,512]{1,0:T(8,128)(2,1)S(1)}, bf16[128,512]{1,0:T(8,128)(2,1)S(1)}, u32[]{:S(2)}, u32[]{:S(2)}) collective-permute-start(bf16[128,512]{1,0:T(8,128)(2,1)S(1)} %get-tuple-element.29), channel_id=1, source_target_pairs={{0,14},{2,8},{4,10},{6,12},{8,6},{10,0},{12,2},{14,4},{16,30},{18,... | collective-permute-start | bytes 393224 | tf_op jit(solution)/shard_map/ppermute | solution.py:381
  39.4 13.9 %collective-permute-start = (bf16[16,16,256]{2,1,0:T(8,128)(2,1)S(1)}, bf16[16,16,256]{2,1,0:T(8,128)(2,1)S(1)}, u32[]{:S(2)}, u32[]{:S(2)}) collective-permute-start(bf16[16,16,256]{2,1,0:T(8,128)(2,1)S(1)} %all-to-all-done.after_ref.refs_0_), channel_id=1, source_target_pairs={{0,2},{2,4},{4,6},{6,0},{1,3},{3,5},{5,7},{7,1},{8,10},{10,12},{12... | collective-permute-start | bytes 393224 | tf_op jit(solution)/shard_map/ppermute | solution.py:371
  40.8 12.5 %collective-permute-start.1 = (bf16[16,16,256]{2,1,0:T(8,128)(2,1)S(1)}, bf16[16,16,256]{2,1,0:T(8,128)(2,1)S(1)}, u32[]{:S(2)}, u32[]{:S(2)}) collective-permute-start(bf16[16,16,256]{2,1,0:T(8,128)(2,1)S(1)} %all-to-all-done.after_ref.refs_0_), channel_id=1, source_target_pairs={{0,4},{2,6},{4,0},{6,2},{1,5},{3,7},{5,1},{7,3},{8,12},{10,14},{12... | collective-permute-start | bytes 393224 | tf_op jit(solution)/shard_map/ppermute | solution.py:371
  43.9 10.3 %collective-permute-start.2 = (bf16[16,16,256]{2,1,0:T(8,128)(2,1)S(1)}, bf16[16,16,256]{2,1,0:T(8,128)(2,1)S(1)}, u32[]{:S(2)}, u32[]{:S(2)}) collective-permute-start(bf16[16,16,256]{2,1,0:T(8,128)(2,1)S(1)} %all-to-all-done.after_ref.refs_0_), channel_id=1, source_target_pairs={{0,6},{2,0},{4,2},{6,4},{1,7},{3,1},{5,3},{7,5},{8,14},{10,8},{12,... | collective-permute-start | bytes 393224 | tf_op jit(solution)/shard_map/ppermute | solution.py:371
  53.2 11.5 %copy-start.1 = (s32[16]{0:T(128)S(1)}, s32[16]{0:T(128)}, u32[]{:S(2)}) copy-start(s32[16]{0:T(128)} %refs_6_.1) | copy-start | bytes 196
  53.3 27.6 %copy-start.2 = (s32[16]{0:T(128)S(1)}, s32[16]{0:T(128)}, u32[]{:S(2)}) copy-start(s32[16]{0:T(128)} %refs_7_.1) | copy-start | bytes 196
  53.3 27.6 %copy-start.3 = (s32[16]{0:T(128)S(1)}, s32[16]{0:T(128)}, u32[]{:S(2)}) copy-start(s32[16]{0:T(128)} %refs_8_.1) | copy-start | bytes 196
  55.4 25.5 %all-to-all-start.1 = ((bf16[16,4,16,128]{3,2,1,0:T(8,128)(2,1)}), bf16[16,4,16,128]{3,2,1,0:T(8,128)(2,1)S(1)}, u32[]{:S(2)}, u32[]{:S(2)}) async-start(bf16[16,4,16,128]{3,2,1,0:T(8,128)(2,1)} %partial_queries.1), calls=%async_computation.1 | async-start | bytes 524288 | tf_op jit(solution)/shard_map/all_to_all | solution.py:403
  64.8 7.9 %collective-permute-start.10 = (bf16[1152,128]{1,0:T(8,128)(2,1)S(1)}, bf16[1152,128]{1,0:T(8,128)(2,1)S(1)}, u32[]{:S(2)}, u32[]{:S(2)}) collective-permute-start(bf16[1152,128]{1,0:T(8,128)(2,1)S(1)} %get-tuple-element.36), channel_id=1, source_target_pairs={{0,2},{2,4},{4,6},{6,0},{1,3},{3,5},{5,7},{7,1},{8,10},{10,12},{12... | collective-permute-start | bytes 884744 | tf_op jit(solution)/shard_map/ppermute | solution.py:371
  67.3 13.5 %collective-permute-start.11 = (bf16[1152,128]{1,0:T(8,128)(2,1)S(1)}, bf16[1152,128]{1,0:T(8,128)(2,1)S(1)}, u32[]{:S(2)}, u32[]{:S(2)}) collective-permute-start(bf16[1152,128]{1,0:T(8,128)(2,1)S(1)} %get-tuple-element.37), channel_id=1, source_target_pairs={{0,4},{2,6},{4,0},{6,2},{1,5},{3,7},{5,1},{7,3},{8,12},{10,14},{12... | collective-permute-start | bytes 884744 | tf_op jit(solution)/shard_map/ppermute | solution.py:371
  68.5 12.4 %collective-permute-start.12 = (bf16[1152,128]{1,0:T(8,128)(2,1)S(1)}, bf16[1152,128]{1,0:T(8,128)(2,1)S(1)}, u32[]{:S(2)}, u32[]{:S(2)}) collective-permute-start(bf16[1152,128]{1,0:T(8,128)(2,1)S(1)} %get-tuple-element.38), channel_id=1, source_target_pairs={{0,6},{2,0},{4,2},{6,4},{1,7},{3,1},{5,3},{7,5},{8,14},{10,8},{12,... | collective-permute-start | bytes 884744 | tf_op jit(solution)/shard_map/ppermute | solution.py:371
  110.9 4.6 %collective-permute-start.13 = (f32[1,128]{1,0:T(1,128)S(1)}, f32[1,128]{1,0:T(1,128)S(1)}, u32[]{:S(2)}, u32[]{:S(2)}) collective-permute-start(f32[1,128]{1,0:T(1,128)S(1)} %half_tallies.1.here_ref), channel_id=1, source_target_pairs={{0,1},{1,0},{2,3},{3,2},{4,5},{5,4},{6,7},{7,6},{8,9},{9,8},{10,11... | collective-permute-start | bytes 1544 | tf_op jit(solution)/shard_map/ppermute | solution.py:409

commit v3 on v2

--- a/solution.py
+++ b/solution.py
@@ -7,6 +7,7 @@
 from jax.experimental import pallas as pl
 from jax.experimental.pallas import tpu as pltpu
 from jax.sharding import PartitionSpec as P
+
 
 HEAD_SIZE = 128
 QUERY_HEADS = 32
@@ -87,28 +88,46 @@
 
 
 def cut_kernel(n_tensor, weight_ref, *out_refs):
-    t, parity = lax.axis_index("tensor"), lax.axis_index("dp") % 2
+    t, side = lax.axis_index("tensor"), lax.axis_index("dp") % 2
+    side = (side + lax.axis_index("seq")) % 2
     part = out_refs[0].shape[1]
-    for side in range(2):
-        for s in range(n_tensor):
-            column = 2 * ((t + s) % n_tensor) + (parity ^ side)
-            at = pl.multiple_of(column * part, part)
-            out_refs[side * n_tensor + s][...] = weight_ref[:, pl.ds(at, part)]
+    for s in range(n_tensor):
+        at = pl.multiple_of((2 * ((t + s) % n_tensor) + side) * part, part)
+        out_refs[s][...] = weight_ref[:, pl.ds(at, part)]
 
 
 def cut_weight(weight, n_tensor):
     rows, columns = weight.shape
     part = columns // (2 * n_tensor)
-    count = 2 * n_tensor
     return pl.pallas_call(
         functools.partial(cut_kernel, n_tensor),
-        out_shape=[jax.ShapeDtypeStruct((rows, part), BF)] * count,
+        out_shape=[jax.ShapeDtypeStruct((rows, part), BF)] * n_tensor,
         in_specs=[VMEM],
-        out_specs=[VMEM] * count,
+        out_specs=[VMEM] * n_tensor,
         cost_estimate=cost(1000, 2 * rows * columns * 2),
         compiler_params=limit(4),
         name="cut_weight",
     )(weight)
+
+
+def stack_kernel(own_ref, *refs):
+    out_ref = refs[-1]
+    first = lax.axis_index("seq") == 0
+    out_ref[0] = jnp.where(first, own_ref[...].astype(F32), refs[0][...].astype(F32)).astype(BF)
+    for s in range(1, len(refs) - 1):
+        out_ref[s] = refs[s][...]
+
+
+def stacked_weight(own, arrived):
+    return pl.pallas_call(
+        stack_kernel,
+        out_shape=jax.ShapeDtypeStruct((len(arrived), *own.shape), BF),
+        in_specs=[VMEM] * (1 + len(arrived)),
+        out_specs=VMEM,
+        cost_estimate=cost(1000, 2**20),
+        compiler_params=limit(4),
+        name="stacked_weight",
+    )(own, *arrived)
 
 
 def kv_kernel(
@@ -214,15 +233,18 @@
 
 def query_kernel(n_tensor, *refs):
     x_refs = refs[:n_tensor]
-    w_refs = refs[n_tensor : 3 * n_tensor]
-    out_ref = refs[3 * n_tensor + 1]
+    here_ref, there_ref, _, out_ref = refs[n_tensor:]
     n_dp, heads, samples, _ = out_ref.shape
-    x = jnp.concatenate(
-        [x_refs[s][...].reshape(n_dp * samples, -1) for s in range(n_tensor)], axis=1
-    )
-    w = jnp.concatenate(
-        [w_refs[side * n_tensor + s][...] for s in range(n_tensor) for side in range(2)], axis=0
-    )
+    depth = here_ref.shape[1]
+    seq = lax.axis_index("seq")
+    columns, weights = [], []
+    for s in range(n_tensor):
+        for side, w_ref in ((seq, here_ref), (1 - seq, there_ref)):
+            at = pl.multiple_of(side * depth, depth)
+            columns.append(x_refs[s][:, :, pl.ds(at, depth)].reshape(n_dp * samples, depth))
+            weights.append(w_ref[s])
+    x = jnp.concatenate(columns, axis=1)
+    w = jnp.concatenate(weights, axis=0)
     q = jnp.dot(x, w, preferred_element_type=F32).astype(BF)
     for h in range(heads):
         out_ref[:, h, :, :] = q[:, h * HEAD_SIZE : (h + 1) * HEAD_SIZE].reshape(
@@ -230,21 +252,21 @@
         )
 
 
-def partial_queries(pieces, weights, after):
+def partial_queries(pieces, here, there, after):
     n_dp, samples, width = pieces[0].shape
-    heads = weights[0].shape[1] // HEAD_SIZE
+    heads = here.shape[2] // HEAD_SIZE
     return pl.pallas_call(
         functools.partial(query_kernel, len(pieces)),
         out_shape=jax.ShapeDtypeStruct((n_dp, heads, samples, HEAD_SIZE), BF),
-        in_specs=[VMEM] * (len(pieces) + len(weights)) + [ANY],
+        in_specs=[VMEM] * (len(pieces) + 2) + [ANY],
         out_specs=VMEM,
         cost_estimate=cost(2 * n_dp * samples * width * 4 * heads * HEAD_SIZE, 2 * 2**20),
         compiler_params=limit(8),
         name="partial_queries",
-    )(*pieces, *weights, after)
-
-
-def attention_kernel(n_tensor, q_ref, *refs):
+    )(*pieces, here, there, after)
+
+
+def attention_kernel(n_tensor, copies, q_ref, *refs):
     kv_refs = refs[:n_tensor]
     cos_ref, sin_ref, lengths_ref, prompt_ref, answer_ref, out_ref = refs[n_tensor:]
     n_dp, half, samples, _ = q_ref.shape
@@ -298,7 +320,7 @@
     part = jnp.sum(above, axis=1, keepdims=True) / jnp.sum(below, axis=1, keepdims=True)
     rating = jnp.sum(part.reshape(heads, samples, 1), axis=0)
     out_rows = out_ref.shape[0]
-    owner = lax.broadcasted_iota(jnp.int32, (out_rows, HEAD_SIZE), 0) // n_tensor
+    owner = lax.broadcasted_iota(jnp.int32, (out_rows, HEAD_SIZE), 0) // copies
     column = lax.broadcasted_iota(jnp.int32, (out_rows, HEAD_SIZE), 1)
     out = jnp.zeros((out_rows, HEAD_SIZE), F32)
     for i in range(samples):
@@ -310,12 +332,12 @@
     out_ref[...] = out
 
 
-def partial_ratings(queries, kv, cosine, sine, lengths, prompt_of, answers):
+def partial_ratings(queries, kv, cosine, sine, lengths, prompt_of, answers, copies):
     n_tensor = len(kv)
     n_dp = queries.shape[0]
     return pl.pallas_call(
-        functools.partial(attention_kernel, n_tensor),
-        out_shape=jax.ShapeDtypeStruct((n_dp * n_tensor, HEAD_SIZE), F32),
+        functools.partial(attention_kernel, n_tensor, copies),
+        out_shape=jax.ShapeDtypeStruct((n_dp * copies, HEAD_SIZE), F32),
         in_specs=[VMEM] * (n_tensor + 3) + [SMEM] * 3,
         out_specs=VMEM,
         cost_estimate=cost(2 * 128 * 128 * 1024, 2 * 2**20),
@@ -324,43 +346,31 @@
     )(queries, *kv, cosine, sine, lengths, prompt_of, answers)
 
 
-def tally_kernel(n_tensor, rows_ref, out_ref):
-    rows = rows_ref[...]
-    summed = rows.reshape(rows.shape[0] // n_tensor, n_tensor, HEAD_SIZE)
-    rating = jnp.sum(summed[:, :, 0:1], axis=1)
-    place = summed[:, 0, 1:2].astype(jnp.int32)
-    reward = 1.0 / (1.0 + jnp.exp(-rating))
-    lane = lax.broadcasted_iota(jnp.int32, (rating.shape[0], HEAD_SIZE), 1)
-    out_ref[...] = jnp.sum(jnp.where(lane == place, reward, 0.0), axis=0, keepdims=True)
-
-
-def half_tallies(rows, n_tensor):
-    return pl.pallas_call(
-        functools.partial(tally_kernel, n_tensor),
-        out_shape=jax.ShapeDtypeStruct((1, HEAD_SIZE), F32),
+def share_kernel(n_tensor, rows_ref, out_ref):
+    rows = rows_ref[...].reshape(-1, n_tensor, 2, HEAD_SIZE)
+    total = jnp.zeros((1, HEAD_SIZE), F32)
+    for seq in range(2):
+        rating = rows[:, 0, seq, 0:1]
+        for s in range(1, n_tensor):
+            rating = rating + rows[:, s, seq, 0:1]
+        place = rows[:, 0, seq, 1:2].astype(jnp.int32)
+        reward = 1.0 / (1.0 + jnp.exp(-rating))
+        lane = lax.broadcasted_iota(jnp.int32, (rating.shape[0], HEAD_SIZE), 1)
+        total = total + jnp.sum(jnp.where(lane == place, reward, 0.0), axis=0, keepdims=True)
+    for q in range(PROMPT_DEV):
+        tally = total[:, q * ANSWERS : (q + 1) * ANSWERS]
+        out_ref[q : q + 1, :] = tally / jnp.sum(tally, axis=1, keepdims=True)
+
+
+def shares(rows, n_tensor):
+    return pl.pallas_call(
+        functools.partial(share_kernel, n_tensor),
+        out_shape=jax.ShapeDtypeStruct((PROMPT_DEV, ANSWERS), F32),
         in_specs=[VMEM],
         out_specs=VMEM,
         compiler_params=limit(2),
-        name="half_tallies",
+        name="shares",
     )(rows)
-
-
-def share_kernel(here_ref, there_ref, out_ref):
-    total = here_ref[...] + there_ref[...]
-    for q in range(PROMPT_DEV):
-        tally = total[:, q * ANSWERS : (q + 1) * ANSWERS]
-        out_ref[q : q + 1, :] = tally / jnp.sum(tally, axis=1, keepdims=True)
-
-
-def shares(here, there):
-    return pl.pallas_call(
-        share_kernel,
-        out_shape=jax.ShapeDtypeStruct((PROMPT_DEV, ANSWERS), F32),
-        in_specs=[VMEM, VMEM],
-        out_specs=VMEM,
-        compiler_params=limit(2),
-        name="shares",
-    )(here, there)
 
 
 def shards(hidden, lengths, answers, prompt_of, query_weight, key_weight, value_weight, score_vec):
@@ -370,21 +380,24 @@
     def over_tensor(value, s):
         return lax.ppermute(value, "tensor", [(i, (i + s) % n_tensor) for i in range(n_tensor)])
 
-    def weight_piece(value, side, s):
-        if side == 0 and s == 0:
-            return value
+    def weight_piece(value, s):
         pairs = [
-            (d * n_tensor + i, (d ^ side) * n_tensor + (i + s) % n_tensor)
+            (
+                (d * n_tensor + i) * n_seq + c,
+                ((d ^ c) * n_tensor + (i + s) % n_tensor) * n_seq + c,
+            )
             for d in range(n_dp)
             for i in range(n_tensor)
+            for c in range(n_seq)
+            if s or c
         ]
-        return lax.ppermute(value, ("dp", "tensor"), pairs)
+        return lax.ppermute(value, ("dp", "tensor", "seq"), pairs)
 
     rows = scoring_rows(lengths, hidden, n_dp)
     moved = lax.all_to_all(rows, "dp", 0, 0, tiled=True)
 
     cut = cut_weight(query_weight, n_tensor)
-    weights = [weight_piece(cut[k], k // n_tensor, k % n_tensor) for k in range(2 * n_tensor)]
+    arrived_weight = [weight_piece(cut[s], s) for s in range(n_tensor)]
 
     key_cos, key_sin = rope_tables(jnp.arange(positions, dtype=F32))
     kv = keys_and_values(
@@ -394,20 +407,22 @@
         score_vec.reshape(QUERY_HEADS, HEAD_SIZE),
         key_cos,
         key_sin,
-        moved,
+        cut[0],
         n_tensor,
     )
+    moved, *kv = lax.optimization_barrier((moved, *kv))
     pieces = [moved] + [over_tensor(moved, s) for s in range(1, n_tensor)]
-    queries = partial_queries(pieces, weights, kv[0])
-    queries, *kv = lax.optimization_barrier((queries, *kv))
+    here = stacked_weight(cut[0], arrived_weight)
+    there = lax.ppermute(here, "seq", [(i, (i + 1) % n_seq) for i in range(n_seq)])
+    queries = partial_queries(pieces, here, there, kv[0])
+    kv = [kv[0]] + [over_tensor(kv[s], s) for s in range(1, n_tensor)]
     arrived = lax.all_to_all(queries, "dp", 0, 0, tiled=True)
-    kv = [kv[0]] + [over_tensor(kv[s], s) for s in range(1, n_tensor)]
     query_cos, query_sin = rope_tables((lengths - 1).astype(F32))
-    rated = partial_ratings(arrived, kv, query_cos, query_sin, lengths, prompt_of, answers)
-    gathered = lax.all_to_all(rated, ("dp", "tensor"), 0, 0, tiled=True)
-    here = half_tallies(gathered, n_tensor)
-    there = lax.ppermute(here, "seq", [(i, (i + 1) % n_seq) for i in range(n_seq)])
-    return shares(here, there)
+    rated = partial_ratings(
+        arrived, kv, query_cos, query_sin, lengths, prompt_of, answers, n_tensor * n_seq
+    )
+    gathered = lax.all_to_all(rated, ("dp", "tensor", "seq"), 0, 0, tiled=True)
+    return shares(gathered, n_tensor)
 
 
 def solution(mesh):
@@ -421,6 +436,7 @@
         P("tensor", None),
         P(),
     )
+
     return jax.shard_map(
         shards, mesh=mesh, in_specs=placed, out_specs=P(("groups", "dp"), None), check_vma=False
     )

time: 117 us -> 120 us (1.026)
  waiting for transfers between devices: 14.5 us -> 22.5 us
  starting transfers between devices: 57.4 us -> 49.5 us
  blocking collectives: 28.6 us -> 31.2 us
  local copies, waits for them, and re-layouts: 0.03 us -> 1.25 us
    ppermute x6, waiting for transfers between devices: 11.2 us -> 18.2 us  [over_tensor(): lax.ppermute(value, 'tensor', [(i, (i + s) % n_tensor) for i in range(n_t...]
    ppermute x1, starting transfers between devices: 3.82 us -> 0.14 us  [shards(): lax.ppermute(here, 'seq', [(i, (i + 1) % n_seq) for i in range(n_seq)])]
    all_to_all x1, waiting for transfers between devices: 1.18 us -> 4.33 us  [shards(): moved = lax.all_to_all(rows, 'dp', 0, 0, tiled=True)]
    all_to_all x1, blocking collectives: 28.6 us -> 31.2 us  [shards(): gathered = lax.all_to_all(rated, ('dp', 'tensor', 'seq'), 0, 0, tiled=True)]
    ppermute x6, starting transfers between devices: 10.3 us -> 7.87 us  [over_tensor(): lax.ppermute(value, 'tensor', [(i, (i + s) % n_tensor) for i in range(n_t...]
    all_to_all x1, starting transfers between devices: 24.5 us -> 22.7 us  [shards(): moved = lax.all_to_all(rows, 'dp', 0, 0, tiled=True)]
    ppermute x7 -> x4, starting transfers between devices: 9.36 us -> 11.1 us  [weight_piece(): return lax.ppermute(value, ('dp', 'tensor', 'seq'), pairs)]
    all_to_all x1, starting transfers between devices: 9.38 us -> 7.74 us  [shards(): arrived = lax.all_to_all(queries, 'dp', 0, 0, tiled=True)]
  transfers between devices with their start and end apart: 16 -> 13, of which waited for: 7 -> 5; matrix products, arithmetic and copies ran while one was open for 0% -> 0% of each run, Pallas kernels for 8% -> 10%
where the time goes in v3:
time: 120 us
  starting transfers between devices  49.5 us (41%)
  blocking collectives  31.2 us (26%)
  waiting for transfers between devices  22.5 us (19%)
  Pallas kernels  14.9 us (12%)
  local copies, waits for them, and re-layouts  1.25 us (1%)
    all_to_all x1, blocking collectives, shards(): gathered = lax.all_to_all(rated, ('dp', 'tensor', 'seq'), 0, 0, tiled=True)  31.2 us
    all_to_all x1, starting transfers between devices, shards(): moved = lax.all_to_all(rows, 'dp', 0, 0, tiled=True)  22.7 us
    ppermute x6, waiting for transfers between devices, over_tensor(): lax.ppermute(value, 'tensor', [(i, (i + s) % n_tensor) for i in range(n_t...  18.2 us
    ppermute x4, starting transfers between devices, weight_piece(): return lax.ppermute(value, ('dp', 'tensor', 'seq'), pairs)  11.1 us
    pallas_call x1, Pallas kernels, keys_and_values(): pl.pallas_call(functools.partial(kv_kernel, n_tensor), in_specs=[HBM, HBM...  8.51 us
    ppermute x6, starting transfers between devices, over_tensor(): lax.ppermute(value, 'tensor', [(i, (i + s) % n_tensor) for i in range(n_t...  7.87 us
    all_to_all x1, starting transfers between devices, shards(): arrived = lax.all_to_all(queries, 'dp', 0, 0, tiled=True)  7.74 us
    all_to_all x1, waiting for transfers between devices, shards(): moved = lax.all_to_all(rows, 'dp', 0, 0, tiled=True)  4.33 us
  transfers between devices with their start and end apart: 13, of which 5 were waited for; matrix products, arithmetic and copies ran while one was open for 0% of the time, Pallas kernels for 10%

profile of v3, /device:TPU:33, one launch (start us, length us, event | category | flops | bytes accessed | tf_op | source)
XLA Modules:
  0.0 120.0 jit_solution(16694256696113576252)
XLA Ops:
  0.0 1.2 %copy-done = bf16[128,4096]{1,0:T(8,128)(2,1)S(1)} copy-done((bf16[128,4096]{1,0:T(8,128)(2,1)S(1)}, bf16[128,4096]{1,0:T(8,128)(2,1)}, u32[]{:S(2)}) %copy-start) | copy-done | bytes 1048600
  1.3 5.3 %collective-permute-start.3 = (bf16[128,512]{1,0:T(8,128)(2,1)S(1)}, bf16[128,512]{1,0:T(8,128)(2,1)S(1)}, u32[]{:S(2)}, u32[]{:S(2)}) collective-permute-start(bf16[128,512]{1,0:T(8,128)(2,1)S(1)} %get-tuple-element.18.after_ref.own_ref), channel_id=1, source_target_pairs={{1,9},{3,11},{5,13},{7,15},{9,1},{11,3},{13,5},{15,7},{17,25},{19,... | collective-permute-start | bytes 393224 | tf_op jit(solution)/shard_map/ppermute | solution.py:394
  6.5 1.2 collective-permute-start.4
  7.7 3.9 %collective-permute-start.5 = (bf16[128,512]{1,0:T(8,128)(2,1)S(1)}, bf16[128,512]{1,0:T(8,128)(2,1)S(1)}, u32[]{:S(2)}, u32[]{:S(2)}) collective-permute-start(bf16[128,512]{1,0:T(8,128)(2,1)S(1)} %get-tuple-element.25), channel_id=1, source_target_pairs={{0,4},{1,13},{2,6},{3,15},{4,0},{5,9},{6,2},{7,11},{8,12},{9,5},{1... | collective-permute-start | bytes 393224 | tf_op jit(solution)/shard_map/ppermute | solution.py:394
  11.6 0.7 collective-permute-start.6
  12.4 3.0 %scoring_rows.1 = bf16[16,16,256]{2,1,0:T(8,128)(2,1)} custom-call(s32[16]{0:T(128)} %refs_6_.1, bf16[16,64,2048]{2,1,0:T(8,128)(2,1)} %hidden_ref.1), custom_call_target="tpu_custom_call" | custom-call | flops 16777216 | bytes 1048576 | tf_op jit(solution)/shard_map/scoring_rows/pallas_call | solution.py:75
  15.3 22.7 %all-to-all-start = ((bf16[16,16,256]{2,1,0:T(8,128)(2,1)}), bf16[16,16,256]{2,1,0:T(8,128)(2,1)S(1)}, u32[]{:S(2)}, u32[]{:S(2)}) async-start(bf16[16,16,256]{2,1,0:T(8,128)(2,1)} %scoring_rows.1), calls=%async_computation | async-start | bytes 262144 | tf_op jit(solution)/shard_map/all_to_all | solution.py:397
  38.1 0.1 collective-permute-start.7
  38.5 8.5 %keys_and_values.1 = (bf16[1152,128]{1,0:T(8,128)(2,1)S(1)}, bf16[1152,128]{1,0:T(8,128)(2,1)S(1)}, bf16[1152,128]{1,0:T(8,128)(2,1)S(1)}, bf16[1152,128]{1,0:T(8,128)(2,1)S(1)}) custom-call(bf16[1024,2048]{1,0:T(8,128)(2,1)} %bitcast.9, bf16[2048,512]{1,0:T(8,128)(2,1)} %k_ref.1, bf16[2048,512]{1,0:T(8,128)(2,1)} %v_ref.1, f32[32,128]{1,0:T(8,128)S(1)} %bitcast.8, ...), custom_call_target="tpu_custom_call" | custom-call | flops 2684354560 | bytes 9437184 | tf_op jit(solution)/shard_map/keys_and_values/pallas_call | solution.py:216
  47.1 4.3 %all-to-all-done.refs_0_ = bf16[16,16,256]{2,1,0:T(8,128)(2,1)S(1)} async-done(((bf16[16,16,256]{2,1,0:T(8,128)(2,1)}), bf16[16,16,256]{2,1,0:T(8,128)(2,1)S(1)}, u32[]{:S(2)}, u32[]{:S(2)}) %all-to-all-start) | async-done | bytes 131104 | tf_op jit(solution)/shard_map/all_to_all | solution.py:397
  51.4 0.4 collective-permute-start
  51.8 0.8 collective-permute-start.1
  52.7 1.6 %collective-permute-start.2 = (bf16[16,16,256]{2,1,0:T(8,128)(2,1)S(1)}, bf16[16,16,256]{2,1,0:T(8,128)(2,1)S(1)}, u32[]{:S(2)}, u32[]{:S(2)}) collective-permute-start(bf16[16,16,256]{2,1,0:T(8,128)(2,1)S(1)} %all-to-all-done.refs_0_), channel_id=1, source_target_pairs={{0,6},{2,0},{4,2},{6,4},{1,7},{3,1},{5,3},{7,5},{8,14},{10,8},{12,... | collective-permute-start | bytes 393224 | tf_op jit(solution)/shard_map/ppermute | solution.py:381
  54.2 4.8 %collective-permute-done.refs_1_ = bf16[16,16,256]{2,1,0:T(8,128)(2,1)S(1)} collective-permute-done((bf16[16,16,256]{2,1,0:T(8,128)(2,1)S(1)}, bf16[16,16,256]{2,1,0:T(8,128)(2,1)S(1)}, u32[]{:S(2)}, u32[]{:S(2)}) %collective-permute-start) | collective-permute-done | bytes 131104 | tf_op jit(solution)/shard_map/ppermute | solution.py:381
  59.0 0.9 collective-permute-done.2.refs_3_
  59.9 1.2 partial_queries.1
  61.1 7.7 %all-to-all-start.1 = ((bf16[16,4,16,128]{3,2,1,0:T(8,128)(2,1)}), bf16[16,4,16,128]{3,2,1,0:T(8,128)(2,1)S(1)}, u32[]{:S(2)}, u32[]{:S(2)}) async-start(bf16[16,4,16,128]{3,2,1,0:T(8,128)(2,1)} %partial_queries.1), calls=%async_computation.1 | async-start | bytes 524288 | tf_op jit(solution)/shard_map/all_to_all | solution.py:419
  68.8 3.5 %collective-permute-start.10 = (bf16[1152,128]{1,0:T(8,128)(2,1)S(1)}, bf16[1152,128]{1,0:T(8,128)(2,1)S(1)}, u32[]{:S(2)}, u32[]{:S(2)}) collective-permute-start(bf16[1152,128]{1,0:T(8,128)(2,1)S(1)} %get-tuple-element.30), channel_id=1, source_target_pairs={{0,6},{2,0},{4,2},{6,4},{1,7},{3,1},{5,3},{7,5},{8,14},{10,8},{12,... | collective-permute-start | bytes 884744 | tf_op jit(solution)/shard_map/ppermute | solution.py:381
  72.4 1.5 %collective-permute-start.9 = (bf16[1152,128]{1,0:T(8,128)(2,1)S(1)}, bf16[1152,128]{1,0:T(8,128)(2,1)S(1)}, u32[]{:S(2)}, u32[]{:S(2)}) collective-permute-start(bf16[1152,128]{1,0:T(8,128)(2,1)S(1)} %get-tuple-element.29), channel_id=1, source_target_pairs={{0,4},{2,6},{4,0},{6,2},{1,5},{3,7},{5,1},{7,3},{8,12},{10,14},{12... | collective-permute-start | bytes 884744 | tf_op jit(solution)/shard_map/ppermute | solution.py:381
  74.1 10.1 %collective-permute-done.10.refs_3_ = bf16[1152,128]{1,0:T(8,128)(2,1)S(1)} collective-permute-done((bf16[1152,128]{1,0:T(8,128)(2,1)S(1)}, bf16[1152,128]{1,0:T(8,128)(2,1)S(1)}, u32[]{:S(2)}, u32[]{:S(2)}) %collective-permute-start.10) | collective-permute-done | bytes 294944 | tf_op jit(solution)/shard_map/ppermute | solution.py:381
  84.1 2.4 %collective-permute-done.9.refs_2_ = bf16[1152,128]{1,0:T(8,128)(2,1)S(1)} collective-permute-done((bf16[1152,128]{1,0:T(8,128)(2,1)S(1)}, bf16[1152,128]{1,0:T(8,128)(2,1)S(1)}, u32[]{:S(2)}, u32[]{:S(2)}) %collective-permute-start.9) | collective-permute-done | bytes 294944 | tf_op jit(solution)/shard_map/ppermute | solution.py:381
  86.6 1.3 %partial_ratings.1 = f32[128,128]{1,0:T(8,128)S(1)} custom-call(bf16[16,4,16,128]{3,2,1,0:T(8,128)(2,1)S(1)} %all-to-all-done.1.q_ref, bf16[1152,128]{1,0:T(8,128)(2,1)S(1)} %get-tuple-element.27.refs_6_.refs_0_, bf16[1152,128]{1,0:T(8,128)(2,1)S(1)} %collective-permute-done.8.refs_1_, bf16[1152,128]{1,0:T(8,128)(2,1)S(1)} %collective-permute-done.9.refs_2_, ...), custom_call_target="tpu_custom_call" | custom-call | flops 33554432 | bytes 2097152 | tf_op jit(solution)/shard_map/partial_ratings/pallas_call | solution.py:338
  87.9 31.2 %all_to_all.21 = f32[128,1,128]{2,1,0:T(1,128)S(1)} all-to-all(f32[128,1,128]{2,1,0:T(1,128)S(1)} %bitcast.6), channel_id=1, replica_groups=mesh['groups'=2,'dp'=16,'tensor'=4,'seq'=2] {'dp','tensor','seq'}, dimensions={0} | all-to-all | bytes 131072 | tf_op jit(solution)/shard_map/all_to_all | solution.py:424
  119.1 0.9 shares.1
  (26 shorter events, 0.6 us)
Async XLA Ops:
  0.0 1.2 %copy-start = (bf16[128,4096]{1,0:T(8,128)(2,1)S(1)}, bf16[128,4096]{1,0:T(8,128)(2,1)}, u32[]{:S(2)}) copy-start(bf16[128,4096]{1,0:T(8,128)(2,1)} %weight_ref.1) | copy-start | bytes 3145732
  1.3 36.8 %collective-permute-start.3 = (bf16[128,512]{1,0:T(8,128)(2,1)S(1)}, bf16[128,512]{1,0:T(8,128)(2,1)S(1)}, u32[]{:S(2)}, u32[]{:S(2)}) collective-permute-start(bf16[128,512]{1,0:T(8,128)(2,1)S(1)} %get-tuple-element.18.after_ref.own_ref), channel_id=1, source_target_pairs={{1,9},{3,11},{5,13},{7,15},{9,1},{11,3},{13,5},{15,7},{17,25},{19,... | collective-permute-start | bytes 393224 | tf_op jit(solution)/shard_map/ppermute | solution.py:394
  6.5 31.5 %collective-permute-start.4 = (bf16[128,512]{1,0:T(8,128)(2,1)S(1)}, bf16[128,512]{1,0:T(8,128)(2,1)S(1)}, u32[]{:S(2)}, u32[]{:S(2)}) collective-permute-start(bf16[128,512]{1,0:T(8,128)(2,1)S(1)} %get-tuple-element.24), channel_id=1, source_target_pairs={{0,2},{1,11},{2,4},{3,13},{4,6},{5,15},{6,0},{7,9},{8,10},{9,3},{1... | collective-permute-start | bytes 393224 | tf_op jit(solution)/shard_map/ppermute | solution.py:394
  7.7 30.3 %collective-permute-start.5 = (bf16[128,512]{1,0:T(8,128)(2,1)S(1)}, bf16[128,512]{1,0:T(8,128)(2,1)S(1)}, u32[]{:S(2)}, u32[]{:S(2)}) collective-permute-start(bf16[128,512]{1,0:T(8,128)(2,1)S(1)} %get-tuple-element.25), channel_id=1, source_target_pairs={{0,4},{1,13},{2,6},{3,15},{4,0},{5,9},{6,2},{7,11},{8,12},{9,5},{1... | collective-permute-start | bytes 393224 | tf_op jit(solution)/shard_map/ppermute | solution.py:394
  11.6 26.9 %copy-start.4 = (f32[4096]{0:T(1024)S(1)}, f32[4096]{0:T(1024)}, u32[]{:S(2)}) copy-start(f32[4096]{0:T(1024)} %param.15) | copy-start | bytes 49156
  11.6 26.4 %collective-permute-start.6 = (bf16[128,512]{1,0:T(8,128)(2,1)S(1)}, bf16[128,512]{1,0:T(8,128)(2,1)S(1)}, u32[]{:S(2)}, u32[]{:S(2)}) collective-permute-start(bf16[128,512]{1,0:T(8,128)(2,1)S(1)} %get-tuple-element.26), channel_id=1, source_target_pairs={{0,6},{1,15},{2,0},{3,9},{4,2},{5,11},{6,4},{7,13},{8,14},{9,7},{1... | collective-permute-start | bytes 393224 | tf_op jit(solution)/shard_map/ppermute | solution.py:394
  15.3 36.1 %all-to-all-start = ((bf16[16,16,256]{2,1,0:T(8,128)(2,1)}), bf16[16,16,256]{2,1,0:T(8,128)(2,1)S(1)}, u32[]{:S(2)}, u32[]{:S(2)}) async-start(bf16[16,16,256]{2,1,0:T(8,128)(2,1)} %scoring_rows.1), calls=%async_computation | async-start | bytes 262144 | tf_op jit(solution)/shard_map/all_to_all | solution.py:397
  38.1 21.8 %collective-permute-start.7 = (bf16[4,128,512]{2,1,0:T(8,128)(2,1)S(1)}, bf16[4,128,512]{2,1,0:T(8,128)(2,1)S(1)}, u32[]{:S(2)}, u32[]{:S(2)}) collective-permute-start(bf16[4,128,512]{2,1,0:T(8,128)(2,1)S(1)} %stacked_weight.1.refs_4_), channel_id=1, source_target_pairs={{0,1},{1,0},{2,3},{3,2},{4,5},{5,4},{6,7},{7,6},{8,9},{9,8},{10,11... | collective-permute-start | bytes 1572872 | tf_op jit(solution)/shard_map/ppermute | solution.py:416
  47.0 21.8 %copy-start.1 = (s32[16]{0:T(128)S(1)}, s32[16]{0:T(128)}, u32[]{:S(2)}) copy-start(s32[16]{0:T(128)} %refs_6_.1) | copy-start | bytes 196
  47.0 39.5 %copy-start.2 = (s32[16]{0:T(128)S(1)}, s32[16]{0:T(128)}, u32[]{:S(2)}) copy-start(s32[16]{0:T(128)} %refs_7_.1) | copy-start | bytes 196
  47.0 39.5 %copy-start.3 = (s32[16]{0:T(128)S(1)}, s32[16]{0:T(128)}, u32[]{:S(2)}) copy-start(s32[16]{0:T(128)} %refs_8_.1) | copy-start | bytes 196
  51.4 7.6 %collective-permute-start = (bf16[16,16,256]{2,1,0:T(8,128)(2,1)S(1)}, bf16[16,16,256]{2,1,0:T(8,128)(2,1)S(1)}, u32[]{:S(2)}, u32[]{:S(2)}) collective-permute-start(bf16[16,16,256]{2,1,0:T(8,128)(2,1)S(1)} %all-to-all-done.refs_0_), channel_id=1, source_target_pairs={{0,2},{2,4},{4,6},{6,0},{1,3},{3,5},{5,7},{7,1},{8,10},{10,12},{12... | collective-permute-start | bytes 393224 | tf_op jit(solution)/shard_map/ppermute | solution.py:381
  51.8 7.2 %collective-permute-start.1 = (bf16[16,16,256]{2,1,0:T(8,128)(2,1)S(1)}, bf16[16,16,256]{2,1,0:T(8,128)(2,1)S(1)}, u32[]{:S(2)}, u32[]{:S(2)}) collective-permute-start(bf16[16,16,256]{2,1,0:T(8,128)(2,1)S(1)} %all-to-all-done.refs_0_), channel_id=1, source_target_pairs={{0,4},{2,6},{4,0},{6,2},{1,5},{3,7},{5,1},{7,3},{8,12},{10,14},{12... | collective-permute-start | bytes 393224 | tf_op jit(solution)/shard_map/ppermute | solution.py:381
  52.7 7.2 %collective-permute-start.2 = (bf16[16,16,256]{2,1,0:T(8,128)(2,1)S(1)}, bf16[16,16,256]{2,1,0:T(8,128)(2,1)S(1)}, u32[]{:S(2)}, u32[]{:S(2)}) collective-permute-start(bf16[16,16,256]{2,1,0:T(8,128)(2,1)S(1)} %all-to-all-done.refs_0_), channel_id=1, source_target_pairs={{0,6},{2,0},{4,2},{6,4},{1,7},{3,1},{5,3},{7,5},{8,14},{10,8},{12,... | collective-permute-start | bytes 393224 | tf_op jit(solution)/shard_map/ppermute | solution.py:381
  61.1 25.5 %all-to-all-start.1 = ((bf16[16,4,16,128]{3,2,1,0:T(8,128)(2,1)}), bf16[16,4,16,128]{3,2,1,0:T(8,128)(2,1)S(1)}, u32[]{:S(2)}, u32[]{:S(2)}) async-start(bf16[16,4,16,128]{3,2,1,0:T(8,128)(2,1)} %partial_queries.1), calls=%async_computation.1 | async-start | bytes 524288 | tf_op jit(solution)/shard_map/all_to_all | solution.py:419
  68.8 15.3 %collective-permute-start.10 = (bf16[1152,128]{1,0:T(8,128)(2,1)S(1)}, bf16[1152,128]{1,0:T(8,128)(2,1)S(1)}, u32[]{:S(2)}, u32[]{:S(2)}) collective-permute-start(bf16[1152,128]{1,0:T(8,128)(2,1)S(1)} %get-tuple-element.30), channel_id=1, source_target_pairs={{0,6},{2,0},{4,2},{6,4},{1,7},{3,1},{5,3},{7,5},{8,14},{10,8},{12,... | collective-permute-start | bytes 884744 | tf_op jit(solution)/shard_map/ppermute | solution.py:381
  72.4 11.8 %collective-permute-start.8 = (bf16[1152,128]{1,0:T(8,128)(2,1)S(1)}, bf16[1152,128]{1,0:T(8,128)(2,1)S(1)}, u32[]{:S(2)}, u32[]{:S(2)}) collective-permute-start(bf16[1152,128]{1,0:T(8,128)(2,1)S(1)} %get-tuple-element.28), channel_id=1, source_target_pairs={{0,2},{2,4},{4,6},{6,0},{1,3},{3,5},{5,7},{7,1},{8,10},{10,12},{12... | collective-permute-start | bytes 884744 | tf_op jit(solution)/shard_map/ppermute | solution.py:381
  72.4 14.2 %collective-permute-start.9 = (bf16[1152,128]{1,0:T(8,128)(2,1)S(1)}, bf16[1152,128]{1,0:T(8,128)(2,1)S(1)}, u32[]{:S(2)}, u32[]{:S(2)}) collective-permute-start(bf16[1152,128]{1,0:T(8,128)(2,1)S(1)} %get-tuple-element.29), channel_id=1, source_target_pairs={{0,4},{2,6},{4,0},{6,2},{1,5},{3,7},{5,1},{7,3},{8,12},{10,14},{12... | collective-permute-start | bytes 884744 | tf_op jit(solution)/shard_map/ppermute | solution.py:381

commit v4 on v3

--- a/solution.py
+++ b/solution.py
@@ -266,18 +266,36 @@
     )(*pieces, here, there, after)
 
 
+def sum_kernel(q_ref, cos_ref, sin_ref, out_ref):
+    n_dp, half, samples, _ = q_ref.shape
+    heads = 2 * half
+    q = jnp.zeros((heads * samples, HEAD_SIZE), F32)
+    for pair in range(n_dp // 2):
+        block = q_ref[2 * pair : 2 * pair + 2].reshape(heads * samples, HEAD_SIZE)
+        q = q + block.astype(F32)
+    cosine = jnp.concatenate([cos_ref[...]] * heads, axis=0)
+    sine = jnp.concatenate([sin_ref[...]] * heads, axis=0)
+    out_ref[...] = (q * cosine + pltpu.roll(q, HEAD_SIZE // 2, 1) * sine).astype(BF)
+
+
+def summed_queries(arrived, cosine, sine):
+    _, half, samples, _ = arrived.shape
+    return pl.pallas_call(
+        sum_kernel,
+        out_shape=jax.ShapeDtypeStruct((2 * half * samples, HEAD_SIZE), BF),
+        in_specs=[VMEM] * 3,
+        out_specs=VMEM,
+        compiler_params=limit(4),
+        name="summed_queries",
+    )(arrived, cosine, sine)
+
+
 def attention_kernel(n_tensor, copies, q_ref, *refs):
     kv_refs = refs[:n_tensor]
-    cos_ref, sin_ref, lengths_ref, prompt_ref, answer_ref, out_ref = refs[n_tensor:]
-    n_dp, half, samples, _ = q_ref.shape
-    q = jnp.zeros((2 * half * samples, HEAD_SIZE), F32)
-    for pair in range(n_dp // 2):
-        block = q_ref[2 * pair : 2 * pair + 2].reshape(2 * half * samples, HEAD_SIZE)
-        q = q + block.astype(F32)
-    heads = 2 * half
-    cosine = jnp.concatenate([cos_ref[...]] * heads, axis=0)
-    sine = jnp.concatenate([sin_ref[...]] * heads, axis=0)
-    q = (q * cosine + pltpu.roll(q, HEAD_SIZE // 2, 1) * sine).astype(BF)
+    lengths_ref, prompt_ref, answer_ref, out_ref = refs[n_tensor:]
+    samples = lengths_ref.shape[0]
+    heads = q_ref.shape[0] // samples
+    q = q_ref[...]
     total = samples * 64
     chunks = total // HEAD_SIZE
     own = lax.broadcasted_iota(jnp.int32, (samples, HEAD_SIZE), 0)
@@ -332,18 +350,17 @@
     out_ref[...] = out
 
 
-def partial_ratings(queries, kv, cosine, sine, lengths, prompt_of, answers, copies):
+def partial_ratings(queries, kv, lengths, prompt_of, answers, n_dp, copies):
     n_tensor = len(kv)
-    n_dp = queries.shape[0]
     return pl.pallas_call(
         functools.partial(attention_kernel, n_tensor, copies),
         out_shape=jax.ShapeDtypeStruct((n_dp * copies, HEAD_SIZE), F32),
-        in_specs=[VMEM] * (n_tensor + 3) + [SMEM] * 3,
+        in_specs=[VMEM] * (n_tensor + 1) + [SMEM] * 3,
         out_specs=VMEM,
         cost_estimate=cost(2 * 128 * 128 * 1024, 2 * 2**20),
         compiler_params=limit(12),
         name="partial_ratings",
-    )(queries, *kv, cosine, sine, lengths, prompt_of, answers)
+    )(queries, *kv, lengths, prompt_of, answers)
 
 
 def share_kernel(n_tensor, rows_ref, out_ref):
@@ -415,12 +432,12 @@
     here = stacked_weight(cut[0], arrived_weight)
     there = lax.ppermute(here, "seq", [(i, (i + 1) % n_seq) for i in range(n_seq)])
     queries = partial_queries(pieces, here, there, kv[0])
+    query_cos, query_sin = rope_tables((lengths - 1).astype(F32))
+    queries, query_cos, query_sin = lax.optimization_barrier((queries, query_cos, query_sin))
     kv = [kv[0]] + [over_tensor(kv[s], s) for s in range(1, n_tensor)]
     arrived = lax.all_to_all(queries, "dp", 0, 0, tiled=True)
-    query_cos, query_sin = rope_tables((lengths - 1).astype(F32))
-    rated = partial_ratings(
-        arrived, kv, query_cos, query_sin, lengths, prompt_of, answers, n_tensor * n_seq
-    )
+    summed = summed_queries(arrived, query_cos, query_sin)
+    rated = partial_ratings(summed, kv, lengths, prompt_of, answers, n_dp, n_tensor * n_seq)
     gathered = lax.all_to_all(rated, ("dp", "tensor", "seq"), 0, 0, tiled=True)
     return shares(gathered, n_tensor)
 

time: 120 us -> 119 us (level)
  waiting for transfers between devices: 22.5 us -> 18.4 us
  starting transfers between devices: 49.5 us -> 53.5 us
  local copies, waits for them, and re-layouts: 1.25 us -> 0.03 us
    all_to_all x1, waiting for transfers between devices: 0.01 us -> 7.49 us  [shards(): arrived = lax.all_to_all(queries, 'dp', 0, 0, tiled=True)]
    ppermute x6, waiting for transfers between devices: 18.2 us -> 10.9 us  [over_tensor(): lax.ppermute(value, 'tensor', [(i, (i + s) % n_tensor) for i in range(n_t...]
    all_to_all x1, waiting for transfers between devices: 4.33 us -> 0.01 us  [shards(): moved = lax.all_to_all(rows, 'dp', 0, 0, tiled=True)]
    all_to_all x1, starting transfers between devices: 7.74 us -> 11.5 us  [shards(): arrived = lax.all_to_all(queries, 'dp', 0, 0, tiled=True)]
    all_to_all x1, starting transfers between devices: 22.7 us -> 24.5 us  [shards(): moved = lax.all_to_all(rows, 'dp', 0, 0, tiled=True)]
    ppermute x4, starting transfers between devices: 11.1 us -> 9.22 us  [weight_piece(): return lax.ppermute(value, ('dp', 'tensor', 'seq'), pairs)]
    unnamed x10, local copies, waits for them, and re-layouts: 1.25 us -> 0.03 us
  transfers between devices with their start and end apart: 13 -> 13, of which waited for: 5 -> 5; matrix products, arithmetic and copies ran while one was open for 0% -> 0% of each run, Pallas kernels for 10% -> 7%
where the time goes in v4:
time: 119 us
  starting transfers between devices  53.5 us (45%)
  blocking collectives  31.1 us (26%)
  waiting for transfers between devices  18.4 us (15%)
  Pallas kernels  15.1 us (13%)
    all_to_all x1, blocking collectives, shards(): gathered = lax.all_to_all(rated, ('dp', 'tensor', 'seq'), 0, 0, tiled=True)  31.1 us
    all_to_all x1, starting transfers between devices, shards(): moved = lax.all_to_all(rows, 'dp', 0, 0, tiled=True)  24.5 us
    all_to_all x1, starting transfers between devices, shards(): arrived = lax.all_to_all(queries, 'dp', 0, 0, tiled=True)  11.5 us
    ppermute x6, waiting for transfers between devices, over_tensor(): lax.ppermute(value, 'tensor', [(i, (i + s) % n_tensor) for i in range(n_t...  10.9 us
    ppermute x4, starting transfers between devices, weight_piece(): return lax.ppermute(value, ('dp', 'tensor', 'seq'), pairs)  9.22 us
    pallas_call x1, Pallas kernels, keys_and_values(): pl.pallas_call(functools.partial(kv_kernel, n_tensor), in_specs=[HBM, HBM...  8.5 us
    ppermute x6, starting transfers between devices, over_tensor(): lax.ppermute(value, 'tensor', [(i, (i + s) % n_tensor) for i in range(n_t...  8.14 us
    all_to_all x1, waiting for transfers between devices, shards(): arrived = lax.all_to_all(queries, 'dp', 0, 0, tiled=True)  7.49 us
  transfers between devices with their start and end apart: 13, of which 5 were waited for; matrix products, arithmetic and copies ran while one was open for 0% of the time, Pallas kernels for 7%

profile of v4, /device:TPU:33, one launch (start us, length us, event | category | flops | bytes accessed | tf_op | source)
XLA Modules:
  0.0 118.8 jit_solution(17308477348200024294)
XLA Ops:
  0.0 3.1 %scoring_rows.1 = bf16[16,16,256]{2,1,0:T(8,128)(2,1)} custom-call(s32[16]{0:T(128)} %refs_4_.1, bf16[16,64,2048]{2,1,0:T(8,128)(2,1)} %hidden_ref.1), custom_call_target="tpu_custom_call" | custom-call | flops 16777216 | bytes 1048576 | tf_op jit(solution)/shard_map/scoring_rows/pallas_call | solution.py:75
  3.1 24.5 %all-to-all-start = ((bf16[16,16,256]{2,1,0:T(8,128)(2,1)}), bf16[16,16,256]{2,1,0:T(8,128)(2,1)S(1)}, u32[]{:S(2)}, u32[]{:S(2)}) async-start(bf16[16,16,256]{2,1,0:T(8,128)(2,1)} %scoring_rows.1), calls=%async_computation | async-start | bytes 262144 | tf_op jit(solution)/shard_map/all_to_all | solution.py:414
  27.7 3.1 %collective-permute-start.3 = (bf16[128,512]{1,0:T(8,128)(2,1)S(1)}, bf16[128,512]{1,0:T(8,128)(2,1)S(1)}, u32[]{:S(2)}, u32[]{:S(2)}) collective-permute-start(bf16[128,512]{1,0:T(8,128)(2,1)S(1)} %get-tuple-element.21.after_ref.own_ref), channel_id=1, source_target_pairs={{1,9},{3,11},{5,13},{7,15},{9,1},{11,3},{13,5},{15,7},{17,25},{19,... | collective-permute-start | bytes 393224 | tf_op jit(solution)/shard_map/ppermute | solution.py:411
  30.8 1.5 %collective-permute-start.4 = (bf16[128,512]{1,0:T(8,128)(2,1)S(1)}, bf16[128,512]{1,0:T(8,128)(2,1)S(1)}, u32[]{:S(2)}, u32[]{:S(2)}) collective-permute-start(bf16[128,512]{1,0:T(8,128)(2,1)S(1)} %get-tuple-element.27), channel_id=1, source_target_pairs={{0,2},{1,11},{2,4},{3,13},{4,6},{5,15},{6,0},{7,9},{8,10},{9,3},{1... | collective-permute-start | bytes 393224 | tf_op jit(solution)/shard_map/ppermute | solution.py:411
  32.3 3.6 %collective-permute-start.5 = (bf16[128,512]{1,0:T(8,128)(2,1)S(1)}, bf16[128,512]{1,0:T(8,128)(2,1)S(1)}, u32[]{:S(2)}, u32[]{:S(2)}) collective-permute-start(bf16[128,512]{1,0:T(8,128)(2,1)S(1)} %get-tuple-element.28), channel_id=1, source_target_pairs={{0,4},{1,13},{2,6},{3,15},{4,0},{5,9},{6,2},{7,11},{8,12},{9,5},{1... | collective-permute-start | bytes 393224 | tf_op jit(solution)/shard_map/ppermute | solution.py:411
  35.9 1.0 collective-permute-start.6
  37.0 0.1 fusion.2
  37.2 8.5 %keys_and_values.1 = (bf16[1152,128]{1,0:T(8,128)(2,1)S(1)}, bf16[1152,128]{1,0:T(8,128)(2,1)S(1)}, bf16[1152,128]{1,0:T(8,128)(2,1)S(1)}, bf16[1152,128]{1,0:T(8,128)(2,1)S(1)}) custom-call(bf16[1024,2048]{1,0:T(8,128)(2,1)} %bitcast.9, bf16[2048,512]{1,0:T(8,128)(2,1)} %k_ref.1, bf16[2048,512]{1,0:T(8,128)(2,1)} %v_ref.1, f32[32,128]{1,0:T(8,128)S(1)} %bitcast.8, ...), custom_call_target="tpu_custom_call" | custom-call | flops 2684354560 | bytes 9437184 | tf_op jit(solution)/shard_map/keys_and_values/pallas_call | solution.py:216
  45.9 0.1 collective-permute-start.7
  46.0 0.6 collective-permute-start
  46.6 0.7 collective-permute-start.1
  47.3 1.8 %collective-permute-start.2 = (bf16[16,16,256]{2,1,0:T(8,128)(2,1)S(1)}, bf16[16,16,256]{2,1,0:T(8,128)(2,1)S(1)}, u32[]{:S(2)}, u32[]{:S(2)}) collective-permute-start(bf16[16,16,256]{2,1,0:T(8,128)(2,1)S(1)} %all-to-all-done.refs_0_), channel_id=1, source_target_pairs={{0,6},{2,0},{4,2},{6,4},{1,7},{3,1},{5,3},{7,5},{8,14},{10,8},{12,... | collective-permute-start | bytes 393224 | tf_op jit(solution)/shard_map/ppermute | solution.py:398
  49.3 5.5 %collective-permute-done.refs_1_ = bf16[16,16,256]{2,1,0:T(8,128)(2,1)S(1)} collective-permute-done((bf16[16,16,256]{2,1,0:T(8,128)(2,1)S(1)}, bf16[16,16,256]{2,1,0:T(8,128)(2,1)S(1)}, u32[]{:S(2)}, u32[]{:S(2)}) %collective-permute-start) | collective-permute-done | bytes 131104 | tf_op jit(solution)/shard_map/ppermute | solution.py:398
  54.8 0.3 collective-permute-done.2.refs_3_
  55.1 1.1 partial_queries.1
  56.3 11.5 %all-to-all-start.1 = ((bf16[16,4,16,128]{3,2,1,0:T(8,128)(2,1)}), bf16[16,4,16,128]{3,2,1,0:T(8,128)(2,1)S(1)}, u32[]{:S(2)}, u32[]{:S(2)}) async-start(bf16[16,4,16,128]{3,2,1,0:T(8,128)(2,1)} %partial_queries.1), calls=%async_computation.1 | async-start | bytes 524288 | tf_op jit(solution)/shard_map/all_to_all | solution.py:438
  67.8 3.5 %collective-permute-start.10 = (bf16[1152,128]{1,0:T(8,128)(2,1)S(1)}, bf16[1152,128]{1,0:T(8,128)(2,1)S(1)}, u32[]{:S(2)}, u32[]{:S(2)}) collective-permute-start(bf16[1152,128]{1,0:T(8,128)(2,1)S(1)} %get-tuple-element.36), channel_id=1, source_target_pairs={{0,6},{2,0},{4,2},{6,4},{1,7},{3,1},{5,3},{7,5},{8,14},{10,8},{12,... | collective-permute-start | bytes 884744 | tf_op jit(solution)/shard_map/ppermute | solution.py:398
  71.3 1.5 %collective-permute-start.9 = (bf16[1152,128]{1,0:T(8,128)(2,1)S(1)}, bf16[1152,128]{1,0:T(8,128)(2,1)S(1)}, u32[]{:S(2)}, u32[]{:S(2)}) collective-permute-start(bf16[1152,128]{1,0:T(8,128)(2,1)S(1)} %get-tuple-element.35), channel_id=1, source_target_pairs={{0,4},{2,6},{4,0},{6,2},{1,5},{3,7},{5,1},{7,3},{8,12},{10,14},{12... | collective-permute-start | bytes 884744 | tf_op jit(solution)/shard_map/ppermute | solution.py:398
  72.8 7.5 %all-to-all-done.1.q_ref = bf16[16,4,16,128]{3,2,1,0:T(8,128)(2,1)S(1)} async-done(((bf16[16,4,16,128]{3,2,1,0:T(8,128)(2,1)}), bf16[16,4,16,128]{3,2,1,0:T(8,128)(2,1)S(1)}, u32[]{:S(2)}, u32[]{:S(2)}) %all-to-all-start.1) | async-done | bytes 262176 | tf_op jit(solution)/shard_map/all_to_all | solution.py:438
  80.4 2.7 %collective-permute-done.10.refs_3_ = bf16[1152,128]{1,0:T(8,128)(2,1)S(1)} collective-permute-done((bf16[1152,128]{1,0:T(8,128)(2,1)S(1)}, bf16[1152,128]{1,0:T(8,128)(2,1)S(1)}, u32[]{:S(2)}, u32[]{:S(2)}) %collective-permute-start.10) | collective-permute-done | bytes 294944 | tf_op jit(solution)/shard_map/ppermute | solution.py:398
  83.1 2.4 %collective-permute-done.9.refs_2_ = bf16[1152,128]{1,0:T(8,128)(2,1)S(1)} collective-permute-done((bf16[1152,128]{1,0:T(8,128)(2,1)S(1)}, bf16[1152,128]{1,0:T(8,128)(2,1)S(1)}, u32[]{:S(2)}, u32[]{:S(2)}) %collective-permute-start.9) | collective-permute-done | bytes 294944 | tf_op jit(solution)/shard_map/ppermute | solution.py:398
  85.5 1.2 %partial_ratings.1 = f32[128,128]{1,0:T(8,128)S(1)} custom-call(bf16[128,128]{1,0:T(8,128)(2,1)S(1)} %summed_queries.1.q_ref, bf16[1152,128]{1,0:T(8,128)(2,1)S(1)} %get-tuple-element.30.refs_6_.refs_0_, bf16[1152,128]{1,0:T(8,128)(2,1)S(1)} %collective-permute-done.8.refs_1_, bf16[1152,128]{1,0:T(8,128)(2,1)S(1)} %collective-permute-done.9.refs_2_, ...), custom_call_target="tpu_custom_call" | custom-call | flops 33554432 | bytes 2097152 | tf_op jit(solution)/shard_map/partial_ratings/pallas_call | solution.py:355
  86.7 31.1 %all_to_all.21 = f32[128,1,128]{2,1,0:T(1,128)S(1)} all-to-all(f32[128,1,128]{2,1,0:T(1,128)S(1)} %bitcast.7), channel_id=1, replica_groups=mesh['groups'=2,'dp'=16,'tensor'=4,'seq'=2] {'dp','tensor','seq'}, dimensions={0} | all-to-all | bytes 131072 | tf_op jit(solution)/shard_map/all_to_all | solution.py:441
  117.9 0.9 shares.1
  (27 shorter events, 0.6 us)
Async XLA Ops:
  0.0 27.6 %copy-start = (bf16[128,4096]{1,0:T(8,128)(2,1)S(1)}, bf16[128,4096]{1,0:T(8,128)(2,1)}, u32[]{:S(2)}) copy-start(bf16[128,4096]{1,0:T(8,128)(2,1)} %weight_ref.1) | copy-start | bytes 3145732
  0.0 37.2 %copy-start.4 = (f32[4096]{0:T(1024)S(1)}, f32[4096]{0:T(1024)}, u32[]{:S(2)}) copy-start(f32[4096]{0:T(1024)} %param.15) | copy-start | bytes 49156
  3.1 42.9 %all-to-all-start = ((bf16[16,16,256]{2,1,0:T(8,128)(2,1)}), bf16[16,16,256]{2,1,0:T(8,128)(2,1)S(1)}, u32[]{:S(2)}, u32[]{:S(2)}) async-start(bf16[16,16,256]{2,1,0:T(8,128)(2,1)} %scoring_rows.1), calls=%async_computation | async-start | bytes 262144 | tf_op jit(solution)/shard_map/all_to_all | solution.py:414
  27.7 18.0 %collective-permute-start.3 = (bf16[128,512]{1,0:T(8,128)(2,1)S(1)}, bf16[128,512]{1,0:T(8,128)(2,1)S(1)}, u32[]{:S(2)}, u32[]{:S(2)}) collective-permute-start(bf16[128,512]{1,0:T(8,128)(2,1)S(1)} %get-tuple-element.21.after_ref.own_ref), channel_id=1, source_target_pairs={{1,9},{3,11},{5,13},{7,15},{9,1},{11,3},{13,5},{15,7},{17,25},{19,... | collective-permute-start | bytes 393224 | tf_op jit(solution)/shard_map/ppermute | solution.py:411
  30.8 14.9 %collective-permute-start.4 = (bf16[128,512]{1,0:T(8,128)(2,1)S(1)}, bf16[128,512]{1,0:T(8,128)(2,1)S(1)}, u32[]{:S(2)}, u32[]{:S(2)}) collective-permute-start(bf16[128,512]{1,0:T(8,128)(2,1)S(1)} %get-tuple-element.27), channel_id=1, source_target_pairs={{0,2},{1,11},{2,4},{3,13},{4,6},{5,15},{6,0},{7,9},{8,10},{9,3},{1... | collective-permute-start | bytes 393224 | tf_op jit(solution)/shard_map/ppermute | solution.py:411
  32.3 13.5 %collective-permute-start.5 = (bf16[128,512]{1,0:T(8,128)(2,1)S(1)}, bf16[128,512]{1,0:T(8,128)(2,1)S(1)}, u32[]{:S(2)}, u32[]{:S(2)}) collective-permute-start(bf16[128,512]{1,0:T(8,128)(2,1)S(1)} %get-tuple-element.28), channel_id=1, source_target_pairs={{0,4},{1,13},{2,6},{3,15},{4,0},{5,9},{6,2},{7,11},{8,12},{9,5},{1... | collective-permute-start | bytes 393224 | tf_op jit(solution)/shard_map/ppermute | solution.py:411
  35.9 9.9 %collective-permute-start.6 = (bf16[128,512]{1,0:T(8,128)(2,1)S(1)}, bf16[128,512]{1,0:T(8,128)(2,1)S(1)}, u32[]{:S(2)}, u32[]{:S(2)}) collective-permute-start(bf16[128,512]{1,0:T(8,128)(2,1)S(1)} %get-tuple-element.29), channel_id=1, source_target_pairs={{0,6},{1,15},{2,0},{3,9},{4,2},{5,11},{6,4},{7,13},{8,14},{9,7},{1... | collective-permute-start | bytes 393224 | tf_op jit(solution)/shard_map/ppermute | solution.py:411
  37.2 8.8 %copy-start.1 = (s32[16]{0:T(128)S(1)}, s32[16]{0:T(128)}, u32[]{:S(2)}) copy-start(s32[16]{0:T(128)} %refs_4_.1) | copy-start | bytes 196
  45.7 39.8 %copy-start.2 = (s32[16]{0:T(128)S(1)}, s32[16]{0:T(128)}, u32[]{:S(2)}) copy-start(s32[16]{0:T(128)} %refs_5_.1) | copy-start | bytes 196
  45.7 39.8 %copy-start.3 = (s32[16]{0:T(128)S(1)}, s32[16]{0:T(128)}, u32[]{:S(2)}) copy-start(s32[16]{0:T(128)} %refs_6_.1) | copy-start | bytes 196
  45.9 9.3 %collective-permute-start.7 = (bf16[4,128,512]{2,1,0:T(8,128)(2,1)S(1)}, bf16[4,128,512]{2,1,0:T(8,128)(2,1)S(1)}, u32[]{:S(2)}, u32[]{:S(2)}) collective-permute-start(bf16[4,128,512]{2,1,0:T(8,128)(2,1)S(1)} %stacked_weight.1.refs_4_), channel_id=1, source_target_pairs={{0,1},{1,0},{2,3},{3,2},{4,5},{5,4},{6,7},{7,6},{8,9},{9,8},{10,11... | collective-permute-start | bytes 1572872 | tf_op jit(solution)/shard_map/ppermute | solution.py:433
  46.0 8.8 %collective-permute-start = (bf16[16,16,256]{2,1,0:T(8,128)(2,1)S(1)}, bf16[16,16,256]{2,1,0:T(8,128)(2,1)S(1)}, u32[]{:S(2)}, u32[]{:S(2)}) collective-permute-start(bf16[16,16,256]{2,1,0:T(8,128)(2,1)S(1)} %all-to-all-done.refs_0_), channel_id=1, source_target_pairs={{0,2},{2,4},{4,6},{6,0},{1,3},{3,5},{5,7},{7,1},{8,10},{10,12},{12... | collective-permute-start | bytes 393224 | tf_op jit(solution)/shard_map/ppermute | solution.py:398
  46.6 8.2 %collective-permute-start.1 = (bf16[16,16,256]{2,1,0:T(8,128)(2,1)S(1)}, bf16[16,16,256]{2,1,0:T(8,128)(2,1)S(1)}, u32[]{:S(2)}, u32[]{:S(2)}) collective-permute-start(bf16[16,16,256]{2,1,0:T(8,128)(2,1)S(1)} %all-to-all-done.refs_0_), channel_id=1, source_target_pairs={{0,4},{2,6},{4,0},{6,2},{1,5},{3,7},{5,1},{7,3},{8,12},{10,14},{12... | collective-permute-start | bytes 393224 | tf_op jit(solution)/shard_map/ppermute | solution.py:398
  47.3 7.8 %collective-permute-start.2 = (bf16[16,16,256]{2,1,0:T(8,128)(2,1)S(1)}, bf16[16,16,256]{2,1,0:T(8,128)(2,1)S(1)}, u32[]{:S(2)}, u32[]{:S(2)}) collective-permute-start(bf16[16,16,256]{2,1,0:T(8,128)(2,1)S(1)} %all-to-all-done.refs_0_), channel_id=1, source_target_pairs={{0,6},{2,0},{4,2},{6,4},{1,7},{3,1},{5,3},{7,5},{8,14},{10,8},{12,... | collective-permute-start | bytes 393224 | tf_op jit(solution)/shard_map/ppermute | solution.py:398
  56.3 24.0 %all-to-all-start.1 = ((bf16[16,4,16,128]{3,2,1,0:T(8,128)(2,1)}), bf16[16,4,16,128]{3,2,1,0:T(8,128)(2,1)S(1)}, u32[]{:S(2)}, u32[]{:S(2)}) async-start(bf16[16,4,16,128]{3,2,1,0:T(8,128)(2,1)} %partial_queries.1), calls=%async_computation.1 | async-start | bytes 524288 | tf_op jit(solution)/shard_map/all_to_all | solution.py:438
  67.8 15.3 %collective-permute-start.10 = (bf16[1152,128]{1,0:T(8,128)(2,1)S(1)}, bf16[1152,128]{1,0:T(8,128)(2,1)S(1)}, u32[]{:S(2)}, u32[]{:S(2)}) collective-permute-start(bf16[1152,128]{1,0:T(8,128)(2,1)S(1)} %get-tuple-element.36), channel_id=1, source_target_pairs={{0,6},{2,0},{4,2},{6,4},{1,7},{3,1},{5,3},{7,5},{8,14},{10,8},{12,... | collective-permute-start | bytes 884744 | tf_op jit(solution)/shard_map/ppermute | solution.py:398
  71.3 11.8 %collective-permute-start.8 = (bf16[1152,128]{1,0:T(8,128)(2,1)S(1)}, bf16[1152,128]{1,0:T(8,128)(2,1)S(1)}, u32[]{:S(2)}, u32[]{:S(2)}) collective-permute-start(bf16[1152,128]{1,0:T(8,128)(2,1)S(1)} %get-tuple-element.34), channel_id=1, source_target_pairs={{0,2},{2,4},{4,6},{6,0},{1,3},{3,5},{5,7},{7,1},{8,10},{10,12},{12... | collective-permute-start | bytes 884744 | tf_op jit(solution)/shard_map/ppermute | solution.py:398
  71.3 14.2 %collective-permute-start.9 = (bf16[1152,128]{1,0:T(8,128)(2,1)S(1)}, bf16[1152,128]{1,0:T(8,128)(2,1)S(1)}, u32[]{:S(2)}, u32[]{:S(2)}) collective-permute-start(bf16[1152,128]{1,0:T(8,128)(2,1)S(1)} %get-tuple-element.35), channel_id=1, source_target_pairs={{0,4},{2,6},{4,0},{6,2},{1,5},{3,7},{5,1},{7,3},{8,12},{10,14},{12... | collective-permute-start | bytes 884744 | tf_op jit(solution)/shard_map/ppermute | solution.py:398

commit v5 on v4

--- a/solution.py
+++ b/solution.py
@@ -78,7 +78,7 @@
         in_specs=[SMEM, HBM],
         out_specs=VMEM,
         scratch_shapes=[
-            pltpu.VMEM((samples, 16, features), BF),
+            pltpu.VMEM((samples, 8, features), BF),
             pltpu.SemaphoreType.DMA((samples,)),
         ],
         cost_estimate=cost(2 * samples * 256 * features, samples * 16 * features * 2),
@@ -156,7 +156,8 @@
                 h_ref.at[pl.ds(i * rows, rows), :], x_ref.at[i], x_sems.at[i]
             )
         )
-    for copy in copies:
+    first = 1 + n_tensor
+    for copy in copies[:first]:
         copy.start()
 
     head = lax.broadcasted_iota(jnp.int32, (heads, KEY_VALUE_HEADS * HEAD_SIZE), 0)
@@ -170,10 +171,13 @@
     sine = jnp.concatenate([sin_ref[...]] * (rows // sin_ref.shape[0]), axis=0)
 
     for i in range(steps):
-        copies[0 if i == 0 else n_tensor + 1 + i].wait()
+        copies[0 if i == 0 else first + i].wait()
         if i == 0:
+            value_copy.start()
             for s in range(n_tensor):
                 copies[1 + s].wait()
+            copies[first + 1].start()
+            copies[first + 2].start()
         x = x_ref[i]
         keys = jnp.dot(x, w_ref[...], preferred_element_type=F32)
         for s in range(n_tensor):
@@ -182,6 +186,8 @@
             out_refs[s][i * rows : (i + 1) * rows, :] = rotated.astype(BF)
         if i == 0:
             value_copy.wait()
+            for copy in copies[first + 3 :]:
+                copy.start()
             z = lax.dot_general(
                 both, wv_ref[...], (((1,), (1,)), ((), ())), preferred_element_type=F32
             )

time: 119 us -> 119 us (level)
  no operation moved by 1% of the time
where the time goes in v5:
time: 119 us; the launch traced here: 118 us
  starting transfers between devices  53.5 us (45%)
  blocking collectives  31.1 us (26%)
  waiting for transfers between devices  18.4 us (15%)
  Pallas kernels  14.5 us (12%)
    all_to_all x1, blocking collectives, shards(): gathered = lax.all_to_all(rated, ('dp', 'tensor', 'seq'), 0, 0, tiled=True)  31.1 us
    all_to_all x1, starting transfers between devices, shards(): moved = lax.all_to_all(rows, 'dp', 0, 0, tiled=True)  24.5 us
    all_to_all x1, starting transfers between devices, shards(): arrived = lax.all_to_all(queries, 'dp', 0, 0, tiled=True)  11.5 us
    ppermute x6, waiting for transfers between devices, over_tensor(): lax.ppermute(value, 'tensor', [(i, (i + s) % n_tensor) for i in range(n_t...  10.9 us
    ppermute x4, starting transfers between devices, weight_piece(): return lax.ppermute(value, ('dp', 'tensor', 'seq'), pairs)  9.22 us
    pallas_call x1, Pallas kernels, keys_and_values(): pl.pallas_call(functools.partial(kv_kernel, n_tensor), in_specs=[HBM, HBM...  8.21 us
    ppermute x6, starting transfers between devices, over_tensor(): lax.ppermute(value, 'tensor', [(i, (i + s) % n_tensor) for i in range(n_t...  8.14 us
    all_to_all x1, waiting for transfers between devices, shards(): arrived = lax.all_to_all(queries, 'dp', 0, 0, tiled=True)  7.49 us
  transfers between devices with their start and end apart: 13, of which 5 were waited for; matrix products, arithmetic and copies ran while one was open for 0% of the time, Pallas kernels for 7%

profile of v5, /device:TPU:33, one launch (start us, length us, event | category | flops | bytes accessed | tf_op | source)
XLA Modules:
  0.0 118.2 jit_solution(7538757308743353693)
XLA Ops:
  0.0 2.8 %scoring_rows.1 = bf16[16,16,256]{2,1,0:T(8,128)(2,1)} custom-call(s32[16]{0:T(128)} %refs_4_.1, bf16[16,64,2048]{2,1,0:T(8,128)(2,1)} %hidden_ref.1), custom_call_target="tpu_custom_call" | custom-call | flops 16777216 | bytes 1048576 | tf_op jit(solution)/shard_map/scoring_rows/pallas_call | solution.py:75
  2.8 24.5 %all-to-all-start = ((bf16[16,16,256]{2,1,0:T(8,128)(2,1)}), bf16[16,16,256]{2,1,0:T(8,128)(2,1)S(1)}, u32[]{:S(2)}, u32[]{:S(2)}) async-start(bf16[16,16,256]{2,1,0:T(8,128)(2,1)} %scoring_rows.1), calls=%async_computation | async-start | bytes 262144 | tf_op jit(solution)/shard_map/all_to_all | solution.py:420
  27.4 3.1 %collective-permute-start.3 = (bf16[128,512]{1,0:T(8,128)(2,1)S(1)}, bf16[128,512]{1,0:T(8,128)(2,1)S(1)}, u32[]{:S(2)}, u32[]{:S(2)}) collective-permute-start(bf16[128,512]{1,0:T(8,128)(2,1)S(1)} %get-tuple-element.21.after_ref.own_ref), channel_id=1, source_target_pairs={{1,9},{3,11},{5,13},{7,15},{9,1},{11,3},{13,5},{15,7},{17,25},{19,... | collective-permute-start | bytes 393224 | tf_op jit(solution)/shard_map/ppermute | solution.py:417
  30.5 1.5 %collective-permute-start.4 = (bf16[128,512]{1,0:T(8,128)(2,1)S(1)}, bf16[128,512]{1,0:T(8,128)(2,1)S(1)}, u32[]{:S(2)}, u32[]{:S(2)}) collective-permute-start(bf16[128,512]{1,0:T(8,128)(2,1)S(1)} %get-tuple-element.27), channel_id=1, source_target_pairs={{0,2},{1,11},{2,4},{3,13},{4,6},{5,15},{6,0},{7,9},{8,10},{9,3},{1... | collective-permute-start | bytes 393224 | tf_op jit(solution)/shard_map/ppermute | solution.py:417
  32.0 3.6 %collective-permute-start.5 = (bf16[128,512]{1,0:T(8,128)(2,1)S(1)}, bf16[128,512]{1,0:T(8,128)(2,1)S(1)}, u32[]{:S(2)}, u32[]{:S(2)}) collective-permute-start(bf16[128,512]{1,0:T(8,128)(2,1)S(1)} %get-tuple-element.28), channel_id=1, source_target_pairs={{0,4},{1,13},{2,6},{3,15},{4,0},{5,9},{6,2},{7,11},{8,12},{9,5},{1... | collective-permute-start | bytes 393224 | tf_op jit(solution)/shard_map/ppermute | solution.py:417
  35.6 1.0 collective-permute-start.6
  36.7 0.1 fusion.2
  36.9 8.2 %keys_and_values.1 = (bf16[1152,128]{1,0:T(8,128)(2,1)S(1)}, bf16[1152,128]{1,0:T(8,128)(2,1)S(1)}, bf16[1152,128]{1,0:T(8,128)(2,1)S(1)}, bf16[1152,128]{1,0:T(8,128)(2,1)S(1)}) custom-call(bf16[1024,2048]{1,0:T(8,128)(2,1)} %bitcast.9, bf16[2048,512]{1,0:T(8,128)(2,1)} %k_ref.1, bf16[2048,512]{1,0:T(8,128)(2,1)} %v_ref.1, f32[32,128]{1,0:T(8,128)S(1)} %bitcast.8, ...), custom_call_target="tpu_custom_call" | custom-call | flops 2684354560 | bytes 9437184 | tf_op jit(solution)/shard_map/keys_and_values/pallas_call | solution.py:222
  45.3 0.1 collective-permute-start.7
  45.4 0.6 collective-permute-start
  46.0 0.7 collective-permute-start.1
  46.8 1.8 %collective-permute-start.2 = (bf16[16,16,256]{2,1,0:T(8,128)(2,1)S(1)}, bf16[16,16,256]{2,1,0:T(8,128)(2,1)S(1)}, u32[]{:S(2)}, u32[]{:S(2)}) collective-permute-start(bf16[16,16,256]{2,1,0:T(8,128)(2,1)S(1)} %all-to-all-done.refs_0_), channel_id=1, source_target_pairs={{0,6},{2,0},{4,2},{6,4},{1,7},{3,1},{5,3},{7,5},{8,14},{10,8},{12,... | collective-permute-start | bytes 393224 | tf_op jit(solution)/shard_map/ppermute | solution.py:404
  48.8 5.5 %collective-permute-done.refs_1_ = bf16[16,16,256]{2,1,0:T(8,128)(2,1)S(1)} collective-permute-done((bf16[16,16,256]{2,1,0:T(8,128)(2,1)S(1)}, bf16[16,16,256]{2,1,0:T(8,128)(2,1)S(1)}, u32[]{:S(2)}, u32[]{:S(2)}) %collective-permute-start) | collective-permute-done | bytes 131104 | tf_op jit(solution)/shard_map/ppermute | solution.py:404
  54.3 0.3 collective-permute-done.2.refs_3_
  54.6 1.1 partial_queries.1
  55.7 11.5 %all-to-all-start.1 = ((bf16[16,4,16,128]{3,2,1,0:T(8,128)(2,1)}), bf16[16,4,16,128]{3,2,1,0:T(8,128)(2,1)S(1)}, u32[]{:S(2)}, u32[]{:S(2)}) async-start(bf16[16,4,16,128]{3,2,1,0:T(8,128)(2,1)} %partial_queries.1), calls=%async_computation.1 | async-start | bytes 524288 | tf_op jit(solution)/shard_map/all_to_all | solution.py:444
  67.2 3.5 %collective-permute-start.10 = (bf16[1152,128]{1,0:T(8,128)(2,1)S(1)}, bf16[1152,128]{1,0:T(8,128)(2,1)S(1)}, u32[]{:S(2)}, u32[]{:S(2)}) collective-permute-start(bf16[1152,128]{1,0:T(8,128)(2,1)S(1)} %get-tuple-element.36), channel_id=1, source_target_pairs={{0,6},{2,0},{4,2},{6,4},{1,7},{3,1},{5,3},{7,5},{8,14},{10,8},{12,... | collective-permute-start | bytes 884744 | tf_op jit(solution)/shard_map/ppermute | solution.py:404
  70.7 1.5 %collective-permute-start.9 = (bf16[1152,128]{1,0:T(8,128)(2,1)S(1)}, bf16[1152,128]{1,0:T(8,128)(2,1)S(1)}, u32[]{:S(2)}, u32[]{:S(2)}) collective-permute-start(bf16[1152,128]{1,0:T(8,128)(2,1)S(1)} %get-tuple-element.35), channel_id=1, source_target_pairs={{0,4},{2,6},{4,0},{6,2},{1,5},{3,7},{5,1},{7,3},{8,12},{10,14},{12... | collective-permute-start | bytes 884744 | tf_op jit(solution)/shard_map/ppermute | solution.py:404
  72.2 7.5 %all-to-all-done.1.q_ref = bf16[16,4,16,128]{3,2,1,0:T(8,128)(2,1)S(1)} async-done(((bf16[16,4,16,128]{3,2,1,0:T(8,128)(2,1)}), bf16[16,4,16,128]{3,2,1,0:T(8,128)(2,1)S(1)}, u32[]{:S(2)}, u32[]{:S(2)}) %all-to-all-start.1) | async-done | bytes 262176 | tf_op jit(solution)/shard_map/all_to_all | solution.py:444
  79.8 2.7 %collective-permute-done.10.refs_3_ = bf16[1152,128]{1,0:T(8,128)(2,1)S(1)} collective-permute-done((bf16[1152,128]{1,0:T(8,128)(2,1)S(1)}, bf16[1152,128]{1,0:T(8,128)(2,1)S(1)}, u32[]{:S(2)}, u32[]{:S(2)}) %collective-permute-start.10) | collective-permute-done | bytes 294944 | tf_op jit(solution)/shard_map/ppermute | solution.py:404
  82.5 2.4 %collective-permute-done.9.refs_2_ = bf16[1152,128]{1,0:T(8,128)(2,1)S(1)} collective-permute-done((bf16[1152,128]{1,0:T(8,128)(2,1)S(1)}, bf16[1152,128]{1,0:T(8,128)(2,1)S(1)}, u32[]{:S(2)}, u32[]{:S(2)}) %collective-permute-start.9) | collective-permute-done | bytes 294944 | tf_op jit(solution)/shard_map/ppermute | solution.py:404
  84.9 1.2 %partial_ratings.1 = f32[128,128]{1,0:T(8,128)S(1)} custom-call(bf16[128,128]{1,0:T(8,128)(2,1)S(1)} %summed_queries.1.q_ref, bf16[1152,128]{1,0:T(8,128)(2,1)S(1)} %get-tuple-element.30.refs_6_.refs_0_, bf16[1152,128]{1,0:T(8,128)(2,1)S(1)} %collective-permute-done.8.refs_1_, bf16[1152,128]{1,0:T(8,128)(2,1)S(1)} %collective-permute-done.9.refs_2_, ...), custom_call_target="tpu_custom_call" | custom-call | flops 33554432 | bytes 2097152 | tf_op jit(solution)/shard_map/partial_ratings/pallas_call | solution.py:361
  86.2 31.1 %all_to_all.21 = f32[128,1,128]{2,1,0:T(1,128)S(1)} all-to-all(f32[128,1,128]{2,1,0:T(1,128)S(1)} %bitcast.7), channel_id=1, replica_groups=mesh['groups'=2,'dp'=16,'tensor'=4,'seq'=2] {'dp','tensor','seq'}, dimensions={0} | all-to-all | bytes 131072 | tf_op jit(solution)/shard_map/all_to_all | solution.py:447
  117.3 0.9 shares.1
  (27 shorter events, 0.6 us)
Async XLA Ops:
  0.0 27.3 %copy-start = (bf16[128,4096]{1,0:T(8,128)(2,1)S(1)}, bf16[128,4096]{1,0:T(8,128)(2,1)}, u32[]{:S(2)}) copy-start(bf16[128,4096]{1,0:T(8,128)(2,1)} %weight_ref.1) | copy-start | bytes 3145732
  0.0 36.9 %copy-start.4 = (f32[4096]{0:T(1024)S(1)}, f32[4096]{0:T(1024)}, u32[]{:S(2)}) copy-start(f32[4096]{0:T(1024)} %param.15) | copy-start | bytes 49156
  2.8 42.6 %all-to-all-start = ((bf16[16,16,256]{2,1,0:T(8,128)(2,1)}), bf16[16,16,256]{2,1,0:T(8,128)(2,1)S(1)}, u32[]{:S(2)}, u32[]{:S(2)}) async-start(bf16[16,16,256]{2,1,0:T(8,128)(2,1)} %scoring_rows.1), calls=%async_computation | async-start | bytes 262144 | tf_op jit(solution)/shard_map/all_to_all | solution.py:420
  27.4 17.8 %collective-permute-start.3 = (bf16[128,512]{1,0:T(8,128)(2,1)S(1)}, bf16[128,512]{1,0:T(8,128)(2,1)S(1)}, u32[]{:S(2)}, u32[]{:S(2)}) collective-permute-start(bf16[128,512]{1,0:T(8,128)(2,1)S(1)} %get-tuple-element.21.after_ref.own_ref), channel_id=1, source_target_pairs={{1,9},{3,11},{5,13},{7,15},{9,1},{11,3},{13,5},{15,7},{17,25},{19,... | collective-permute-start | bytes 393224 | tf_op jit(solution)/shard_map/ppermute | solution.py:417
  30.5 14.7 %collective-permute-start.4 = (bf16[128,512]{1,0:T(8,128)(2,1)S(1)}, bf16[128,512]{1,0:T(8,128)(2,1)S(1)}, u32[]{:S(2)}, u32[]{:S(2)}) collective-permute-start(bf16[128,512]{1,0:T(8,128)(2,1)S(1)} %get-tuple-element.27), channel_id=1, source_target_pairs={{0,2},{1,11},{2,4},{3,13},{4,6},{5,15},{6,0},{7,9},{8,10},{9,3},{1... | collective-permute-start | bytes 393224 | tf_op jit(solution)/shard_map/ppermute | solution.py:417
  32.0 13.2 %collective-permute-start.5 = (bf16[128,512]{1,0:T(8,128)(2,1)S(1)}, bf16[128,512]{1,0:T(8,128)(2,1)S(1)}, u32[]{:S(2)}, u32[]{:S(2)}) collective-permute-start(bf16[128,512]{1,0:T(8,128)(2,1)S(1)} %get-tuple-element.28), channel_id=1, source_target_pairs={{0,4},{1,13},{2,6},{3,15},{4,0},{5,9},{6,2},{7,11},{8,12},{9,5},{1... | collective-permute-start | bytes 393224 | tf_op jit(solution)/shard_map/ppermute | solution.py:417
  35.6 9.6 %collective-permute-start.6 = (bf16[128,512]{1,0:T(8,128)(2,1)S(1)}, bf16[128,512]{1,0:T(8,128)(2,1)S(1)}, u32[]{:S(2)}, u32[]{:S(2)}) collective-permute-start(bf16[128,512]{1,0:T(8,128)(2,1)S(1)} %get-tuple-element.29), channel_id=1, source_target_pairs={{0,6},{1,15},{2,0},{3,9},{4,2},{5,11},{6,4},{7,13},{8,14},{9,7},{1... | collective-permute-start | bytes 393224 | tf_op jit(solution)/shard_map/ppermute | solution.py:417
  36.9 8.5 %copy-start.1 = (s32[16]{0:T(128)S(1)}, s32[16]{0:T(128)}, u32[]{:S(2)}) copy-start(s32[16]{0:T(128)} %refs_4_.1) | copy-start | bytes 196
  45.1 39.8 %copy-start.2 = (s32[16]{0:T(128)S(1)}, s32[16]{0:T(128)}, u32[]{:S(2)}) copy-start(s32[16]{0:T(128)} %refs_5_.1) | copy-start | bytes 196
  45.2 39.8 %copy-start.3 = (s32[16]{0:T(128)S(1)}, s32[16]{0:T(128)}, u32[]{:S(2)}) copy-start(s32[16]{0:T(128)} %refs_6_.1) | copy-start | bytes 196
  45.3 9.3 %collective-permute-start.7 = (bf16[4,128,512]{2,1,0:T(8,128)(2,1)S(1)}, bf16[4,128,512]{2,1,0:T(8,128)(2,1)S(1)}, u32[]{:S(2)}, u32[]{:S(2)}) collective-permute-start(bf16[4,128,512]{2,1,0:T(8,128)(2,1)S(1)} %stacked_weight.1.refs_4_), channel_id=1, source_target_pairs={{0,1},{1,0},{2,3},{3,2},{4,5},{5,4},{6,7},{7,6},{8,9},{9,8},{10,11... | collective-permute-start | bytes 1572872 | tf_op jit(solution)/shard_map/ppermute | solution.py:439
  45.4 8.8 %collective-permute-start = (bf16[16,16,256]{2,1,0:T(8,128)(2,1)S(1)}, bf16[16,16,256]{2,1,0:T(8,128)(2,1)S(1)}, u32[]{:S(2)}, u32[]{:S(2)}) collective-permute-start(bf16[16,16,256]{2,1,0:T(8,128)(2,1)S(1)} %all-to-all-done.refs_0_), channel_id=1, source_target_pairs={{0,2},{2,4},{4,6},{6,0},{1,3},{3,5},{5,7},{7,1},{8,10},{10,12},{12... | collective-permute-start | bytes 393224 | tf_op jit(solution)/shard_map/ppermute | solution.py:404
  46.0 8.2 %collective-permute-start.1 = (bf16[16,16,256]{2,1,0:T(8,128)(2,1)S(1)}, bf16[16,16,256]{2,1,0:T(8,128)(2,1)S(1)}, u32[]{:S(2)}, u32[]{:S(2)}) collective-permute-start(bf16[16,16,256]{2,1,0:T(8,128)(2,1)S(1)} %all-to-all-done.refs_0_), channel_id=1, source_target_pairs={{0,4},{2,6},{4,0},{6,2},{1,5},{3,7},{5,1},{7,3},{8,12},{10,14},{12... | collective-permute-start | bytes 393224 | tf_op jit(solution)/shard_map/ppermute | solution.py:404
  46.8 7.8 %collective-permute-start.2 = (bf16[16,16,256]{2,1,0:T(8,128)(2,1)S(1)}, bf16[16,16,256]{2,1,0:T(8,128)(2,1)S(1)}, u32[]{:S(2)}, u32[]{:S(2)}) collective-permute-start(bf16[16,16,256]{2,1,0:T(8,128)(2,1)S(1)} %all-to-all-done.refs_0_), channel_id=1, source_target_pairs={{0,6},{2,0},{4,2},{6,4},{1,7},{3,1},{5,3},{7,5},{8,14},{10,8},{12,... | collective-permute-start | bytes 393224 | tf_op jit(solution)/shard_map/ppermute | solution.py:404
  55.7 24.0 %all-to-all-start.1 = ((bf16[16,4,16,128]{3,2,1,0:T(8,128)(2,1)}), bf16[16,4,16,128]{3,2,1,0:T(8,128)(2,1)S(1)}, u32[]{:S(2)}, u32[]{:S(2)}) async-start(bf16[16,4,16,128]{3,2,1,0:T(8,128)(2,1)} %partial_queries.1), calls=%async_computation.1 | async-start | bytes 524288 | tf_op jit(solution)/shard_map/all_to_all | solution.py:444
  67.2 15.3 %collective-permute-start.10 = (bf16[1152,128]{1,0:T(8,128)(2,1)S(1)}, bf16[1152,128]{1,0:T(8,128)(2,1)S(1)}, u32[]{:S(2)}, u32[]{:S(2)}) collective-permute-start(bf16[1152,128]{1,0:T(8,128)(2,1)S(1)} %get-tuple-element.36), channel_id=1, source_target_pairs={{0,6},{2,0},{4,2},{6,4},{1,7},{3,1},{5,3},{7,5},{8,14},{10,8},{12,... | collective-permute-start | bytes 884744 | tf_op jit(solution)/shard_map/ppermute | solution.py:404
  70.7 11.8 %collective-permute-start.8 = (bf16[1152,128]{1,0:T(8,128)(2,1)S(1)}, bf16[1152,128]{1,0:T(8,128)(2,1)S(1)}, u32[]{:S(2)}, u32[]{:S(2)}) collective-permute-start(bf16[1152,128]{1,0:T(8,128)(2,1)S(1)} %get-tuple-element.34), channel_id=1, source_target_pairs={{0,2},{2,4},{4,6},{6,0},{1,3},{3,5},{5,7},{7,1},{8,10},{10,12},{12... | collective-permute-start | bytes 884744 | tf_op jit(solution)/shard_map/ppermute | solution.py:404
  70.7 14.2 %collective-permute-start.9 = (bf16[1152,128]{1,0:T(8,128)(2,1)S(1)}, bf16[1152,128]{1,0:T(8,128)(2,1)S(1)}, u32[]{:S(2)}, u32[]{:S(2)}) collective-permute-start(bf16[1152,128]{1,0:T(8,128)(2,1)S(1)} %get-tuple-element.35), channel_id=1, source_target_pairs={{0,4},{2,6},{4,0},{6,2},{1,5},{3,7},{5,1},{7,3},{8,12},{10,14},{12... | collective-permute-start | bytes 884744 | tf_op jit(solution)/shard_map/ppermute | solution.py:404

commit v6 on v5

--- a/solution.py
+++ b/solution.py
@@ -149,7 +149,6 @@
             )
         )
     value_copy = pltpu.make_async_copy(v_ref, wv_ref, w_sems.at[n_tensor])
-    copies.append(value_copy)
     for i in range(1, steps):
         copies.append(
             pltpu.make_async_copy(
@@ -157,6 +156,7 @@
             )
         )
     first = 1 + n_tensor
+    value_copy.start()
     for copy in copies[:first]:
         copy.start()
 
@@ -171,30 +171,28 @@
     sine = jnp.concatenate([sin_ref[...]] * (rows // sin_ref.shape[0]), axis=0)
 
     for i in range(steps):
-        copies[0 if i == 0 else first + i].wait()
         if i == 0:
-            value_copy.start()
-            for s in range(n_tensor):
-                copies[1 + s].wait()
-            copies[first + 1].start()
-            copies[first + 2].start()
+            value_copy.wait()
+            copies[first].start()
+            z = lax.dot_general(
+                both, wv_ref[...], (((1,), (1,)), ((), ())), preferred_element_type=F32
+            )
+            z = z[:heads] + z[heads:]
+            z_high = z.astype(BF)
+            z_low = (z - z_high.astype(F32)).astype(BF)
+            z = jnp.concatenate([z_high, z_low], axis=0)
+            for copy in copies[:first]:
+                copy.wait()
+            for copy in copies[first + 1 :]:
+                copy.start()
+        else:
+            copies[first + i - 1].wait()
         x = x_ref[i]
         keys = jnp.dot(x, w_ref[...], preferred_element_type=F32)
         for s in range(n_tensor):
             k = keys[:, s * HEAD_SIZE : (s + 1) * HEAD_SIZE]
             rotated = k * cosine + pltpu.roll(k, HEAD_SIZE // 2, 1) * sine
             out_refs[s][i * rows : (i + 1) * rows, :] = rotated.astype(BF)
-        if i == 0:
-            value_copy.wait()
-            for copy in copies[first + 3 :]:
-                copy.start()
-            z = lax.dot_general(
-                both, wv_ref[...], (((1,), (1,)), ((), ())), preferred_element_type=F32
-            )
-            z = z[:heads] + z[heads:]
-            z_high = z.astype(BF)
-            z_low = (z - z_high.astype(F32)).astype(BF)
-            z = jnp.concatenate([z_high, z_low], axis=0)
         u = lax.dot_general(z, x, (((1,), (1,)), ((), ())), preferred_element_type=F32)
         u = u[:heads] + u[heads:]
         u_high = u.astype(BF)
@@ -237,9 +235,10 @@
     )(flat, key_weight, value_weight, score_rows, cosine, sine, after)
 
 
-def query_kernel(n_tensor, *refs):
-    x_refs = refs[:n_tensor]
-    here_ref, there_ref, _, out_ref = refs[n_tensor:]
+def query_kernel(owner, *refs):
+    n_tensor = len(owner) - 1
+    x_refs = refs[:-4]
+    here_ref, there_ref, _, out_ref = refs[-4:]
     n_dp, heads, samples, _ = out_ref.shape
     depth = here_ref.shape[1]
     seq = lax.axis_index("seq")
@@ -247,7 +246,11 @@
     for s in range(n_tensor):
         for side, w_ref in ((seq, here_ref), (1 - seq, there_ref)):
             at = pl.multiple_of(side * depth, depth)
-            columns.append(x_refs[s][:, :, pl.ds(at, depth)].reshape(n_dp * samples, depth))
+            parts = [
+                x_ref[:, :, pl.ds(at, depth)].reshape(-1, depth)
+                for x_ref in x_refs[owner[s] : owner[s + 1]]
+            ]
+            columns.append(parts[0] if len(parts) == 1 else jnp.concatenate(parts, axis=0))
             weights.append(w_ref[s])
     x = jnp.concatenate(columns, axis=1)
     w = jnp.concatenate(weights, axis=0)
@@ -259,17 +262,19 @@
 
 
 def partial_queries(pieces, here, there, after):
-    n_dp, samples, width = pieces[0].shape
+    n_dp, samples, width = pieces[0][0].shape
     heads = here.shape[2] // HEAD_SIZE
-    return pl.pallas_call(
-        functools.partial(query_kernel, len(pieces)),
+    owner = [sum(len(parts) for parts in pieces[:s]) for s in range(len(pieces) + 1)]
+    flat = [part for parts in pieces for part in parts]
+    return pl.pallas_call(
+        functools.partial(query_kernel, owner),
         out_shape=jax.ShapeDtypeStruct((n_dp, heads, samples, HEAD_SIZE), BF),
-        in_specs=[VMEM] * (len(pieces) + 2) + [ANY],
+        in_specs=[VMEM] * (len(flat) + 2) + [ANY],
         out_specs=VMEM,
         cost_estimate=cost(2 * n_dp * samples * width * 4 * heads * HEAD_SIZE, 2 * 2**20),
         compiler_params=limit(8),
         name="partial_queries",
-    )(*pieces, here, there, after)
+    )(*flat, here, there, after)
 
 
 def sum_kernel(q_ref, cos_ref, sin_ref, out_ref):
@@ -434,7 +439,10 @@
         n_tensor,
     )
     moved, *kv = lax.optimization_barrier((moved, *kv))
-    pieces = [moved] + [over_tensor(moved, s) for s in range(1, n_tensor)]
+    pieces = [[moved]]
+    for s in range(1, n_tensor):
+        parts = jnp.split(moved, 2) if 2 * s == n_tensor else [moved]
+        pieces.append([over_tensor(part, s) for part in parts])
     here = stacked_weight(cut[0], arrived_weight)
     there = lax.ppermute(here, "seq", [(i, (i + 1) % n_seq) for i in range(n_seq)])
     queries = partial_queries(pieces, here, there, kv[0])

time: 119 us -> 117 us (0.983)
  waiting for transfers between devices: 18.4 us -> 14.9 us
  starting transfers between devices: 53.5 us -> 55.1 us
    ppermute x6 -> x7, waiting for transfers between devices: 10.9 us -> 6.29 us  [over_tensor(): lax.ppermute(value, 'tensor', [(i, (i + s) % n_tensor) for i in range(n_t...]
    ppermute x6 -> x7, starting transfers between devices: 8.14 us -> 9.76 us  [over_tensor(): lax.ppermute(value, 'tensor', [(i, (i + s) % n_tensor) for i in range(n_t...]
  transfers between devices with their start and end apart: 13 -> 14, of which waited for: 5 -> 4; matrix products, arithmetic and copies ran while one was open for 0% -> 0% of each run, Pallas kernels for 7% -> 7%
where the time goes in v6:
time: 117 us
  starting transfers between devices  55.1 us (47%)
  blocking collectives  32 us (27%)
  waiting for transfers between devices  14.9 us (13%)
  Pallas kernels  14 us (12%)
    all_to_all x1, blocking collectives, shards(): gathered = lax.all_to_all(rated, ('dp', 'tensor', 'seq'), 0, 0, tiled=True)  32 us
    all_to_all x1, starting transfers between devices, shards(): moved = lax.all_to_all(rows, 'dp', 0, 0, tiled=True)  24.5 us
    all_to_all x1, starting transfers between devices, shards(): arrived = lax.all_to_all(queries, 'dp', 0, 0, tiled=True)  11.5 us
    ppermute x7, starting transfers between devices, over_tensor(): lax.ppermute(value, 'tensor', [(i, (i + s) % n_tensor) for i in range(n_t...  9.76 us
    ppermute x4, starting transfers between devices, weight_piece(): return lax.ppermute(value, ('dp', 'tensor', 'seq'), pairs)  9.22 us
    all_to_all x1, waiting for transfers between devices, shards(): arrived = lax.all_to_all(queries, 'dp', 0, 0, tiled=True)  8.64 us
    pallas_call x1, Pallas kernels, keys_and_values(): pl.pallas_call(functools.partial(kv_kernel, n_tensor), in_specs=[HBM, HBM...  7.66 us
    ppermute x7, waiting for transfers between devices, over_tensor(): lax.ppermute(value, 'tensor', [(i, (i + s) % n_tensor) for i in range(n_t...  6.29 us
  transfers between devices with their start and end apart: 14, of which 4 were waited for; matrix products, arithmetic and copies ran while one was open for 0% of the time, Pallas kernels for 7%

profile of v6, /device:TPU:33, one launch (start us, length us, event | category | flops | bytes accessed | tf_op | source)
XLA Modules:
  0.0 116.7 jit_solution(16898785978605623688)
XLA Ops:
  0.0 2.8 %scoring_rows.1 = bf16[16,16,256]{2,1,0:T(8,128)(2,1)} custom-call(s32[16]{0:T(128)} %refs_4_.1, bf16[16,64,2048]{2,1,0:T(8,128)(2,1)} %hidden_ref.1), custom_call_target="tpu_custom_call" | custom-call | flops 16777216 | bytes 1048576 | tf_op jit(solution)/shard_map/scoring_rows/pallas_call | solution.py:75
  2.8 24.5 %all-to-all-start = ((bf16[16,16,256]{2,1,0:T(8,128)(2,1)}), bf16[16,16,256]{2,1,0:T(8,128)(2,1)S(1)}, u32[]{:S(2)}, u32[]{:S(2)}) async-start(bf16[16,16,256]{2,1,0:T(8,128)(2,1)} %scoring_rows.1), calls=%async_computation | async-start | bytes 262144 | tf_op jit(solution)/shard_map/all_to_all | solution.py:425
  27.4 3.1 %collective-permute-start.4 = (bf16[128,512]{1,0:T(8,128)(2,1)S(1)}, bf16[128,512]{1,0:T(8,128)(2,1)S(1)}, u32[]{:S(2)}, u32[]{:S(2)}) collective-permute-start(bf16[128,512]{1,0:T(8,128)(2,1)S(1)} %get-tuple-element.21.after_ref.own_ref), channel_id=1, source_target_pairs={{1,9},{3,11},{5,13},{7,15},{9,1},{11,3},{13,5},{15,7},{17,25},{19,... | collective-permute-start | bytes 393224 | tf_op jit(solution)/shard_map/ppermute | solution.py:422
  30.5 1.5 %collective-permute-start.5 = (bf16[128,512]{1,0:T(8,128)(2,1)S(1)}, bf16[128,512]{1,0:T(8,128)(2,1)S(1)}, u32[]{:S(2)}, u32[]{:S(2)}) collective-permute-start(bf16[128,512]{1,0:T(8,128)(2,1)S(1)} %get-tuple-element.27), channel_id=1, source_target_pairs={{0,2},{1,11},{2,4},{3,13},{4,6},{5,15},{6,0},{7,9},{8,10},{9,3},{1... | collective-permute-start | bytes 393224 | tf_op jit(solution)/shard_map/ppermute | solution.py:422
  32.0 3.6 %collective-permute-start.6 = (bf16[128,512]{1,0:T(8,128)(2,1)S(1)}, bf16[128,512]{1,0:T(8,128)(2,1)S(1)}, u32[]{:S(2)}, u32[]{:S(2)}) collective-permute-start(bf16[128,512]{1,0:T(8,128)(2,1)S(1)} %get-tuple-element.28), channel_id=1, source_target_pairs={{0,4},{1,13},{2,6},{3,15},{4,0},{5,9},{6,2},{7,11},{8,12},{9,5},{1... | collective-permute-start | bytes 393224 | tf_op jit(solution)/shard_map/ppermute | solution.py:422
  35.6 1.0 collective-permute-start.7
  36.7 0.1 fusion.2
  36.9 7.7 %keys_and_values.1 = (bf16[1152,128]{1,0:T(8,128)(2,1)S(1)}, bf16[1152,128]{1,0:T(8,128)(2,1)S(1)}, bf16[1152,128]{1,0:T(8,128)(2,1)S(1)}, bf16[1152,128]{1,0:T(8,128)(2,1)S(1)}) custom-call(bf16[1024,2048]{1,0:T(8,128)(2,1)} %bitcast.9, bf16[2048,512]{1,0:T(8,128)(2,1)} %k_ref.1, bf16[2048,512]{1,0:T(8,128)(2,1)} %v_ref.1, f32[32,128]{1,0:T(8,128)S(1)} %bitcast.8, ...), custom_call_target="tpu_custom_call" | custom-call | flops 2684354560 | bytes 9437184 | tf_op jit(solution)/shard_map/keys_and_values/pallas_call | solution.py:220
  44.7 0.1 collective-permute-start.8
  45.0 0.6 collective-permute-start
  45.6 2.2 %collective-permute-start.3 = (bf16[16,16,256]{2,1,0:T(8,128)(2,1)S(1)}, bf16[16,16,256]{2,1,0:T(8,128)(2,1)S(1)}, u32[]{:S(2)}, u32[]{:S(2)}) collective-permute-start(bf16[16,16,256]{2,1,0:T(8,128)(2,1)S(1)} %all-to-all-done.refs_0_), channel_id=1, source_target_pairs={{0,6},{2,0},{4,2},{6,4},{1,7},{3,1},{5,3},{7,5},{8,14},{10,8},{12,... | collective-permute-start | bytes 393224 | tf_op jit(solution)/shard_map/ppermute | solution.py:409
  48.0 2.9 %collective-permute-start.2 = (bf16[8,16,256]{2,1,0:T(8,128)(2,1)S(1)}, bf16[8,16,256]{2,1,0:T(8,128)(2,1)S(1)}, u32[]{:S(2)}, u32[]{:S(2)}) collective-permute-start(bf16[8,16,256]{2,1,0:T(8,128)(2,1)S(1)} %get-tuple-element.37), channel_id=1, source_target_pairs={{0,4},{2,6},{4,0},{6,2},{1,5},{3,7},{5,1},{7,3},{8,12},{10,14},{12... | collective-permute-start | bytes 196616 | tf_op jit(solution)/shard_map/ppermute | solution.py:409
  51.0 1.6 %collective-permute-done.1.refs_2_ = bf16[8,16,256]{2,1,0:T(8,128)(2,1)S(1)} collective-permute-done((bf16[8,16,256]{2,1,0:T(8,128)(2,1)S(1)}, bf16[8,16,256]{2,1,0:T(8,128)(2,1)S(1)}, u32[]{:S(2)}, u32[]{:S(2)}) %collective-permute-start.1) | collective-permute-done | bytes 65568 | tf_op jit(solution)/shard_map/ppermute | solution.py:409
  52.6 0.7 collective-permute-done.2.refs_3_
  53.3 1.1 partial_queries.1
  54.4 11.5 %all-to-all-start.1 = ((bf16[16,4,16,128]{3,2,1,0:T(8,128)(2,1)}), bf16[16,4,16,128]{3,2,1,0:T(8,128)(2,1)S(1)}, u32[]{:S(2)}, u32[]{:S(2)}) async-start(bf16[16,4,16,128]{3,2,1,0:T(8,128)(2,1)} %partial_queries.1), calls=%async_computation.1 | async-start | bytes 524288 | tf_op jit(solution)/shard_map/all_to_all | solution.py:452
  65.9 2.4 %collective-permute-start.10 = (bf16[1152,128]{1,0:T(8,128)(2,1)S(1)}, bf16[1152,128]{1,0:T(8,128)(2,1)S(1)}, u32[]{:S(2)}, u32[]{:S(2)}) collective-permute-start(bf16[1152,128]{1,0:T(8,128)(2,1)S(1)} %get-tuple-element.35), channel_id=1, source_target_pairs={{0,4},{2,6},{4,0},{6,2},{1,5},{3,7},{5,1},{7,3},{8,12},{10,14},{12... | collective-permute-start | bytes 884744 | tf_op jit(solution)/shard_map/ppermute | solution.py:409
  68.3 1.2 %collective-permute-start.11 = (bf16[1152,128]{1,0:T(8,128)(2,1)S(1)}, bf16[1152,128]{1,0:T(8,128)(2,1)S(1)}, u32[]{:S(2)}, u32[]{:S(2)}) collective-permute-start(bf16[1152,128]{1,0:T(8,128)(2,1)S(1)} %get-tuple-element.36), channel_id=1, source_target_pairs={{0,6},{2,0},{4,2},{6,4},{1,7},{3,1},{5,3},{7,5},{8,14},{10,8},{12,... | collective-permute-start | bytes 884744 | tf_op jit(solution)/shard_map/ppermute | solution.py:409
  69.5 0.3 collective-permute-start.9
  69.8 8.6 %all-to-all-done.1.q_ref = bf16[16,4,16,128]{3,2,1,0:T(8,128)(2,1)S(1)} async-done(((bf16[16,4,16,128]{3,2,1,0:T(8,128)(2,1)}), bf16[16,4,16,128]{3,2,1,0:T(8,128)(2,1)S(1)}, u32[]{:S(2)}, u32[]{:S(2)}) %all-to-all-start.1) | async-done | bytes 262176 | tf_op jit(solution)/shard_map/all_to_all | solution.py:452
  78.5 4.0 %collective-permute-done.11.refs_3_ = bf16[1152,128]{1,0:T(8,128)(2,1)S(1)} collective-permute-done((bf16[1152,128]{1,0:T(8,128)(2,1)S(1)}, bf16[1152,128]{1,0:T(8,128)(2,1)S(1)}, u32[]{:S(2)}, u32[]{:S(2)}) %collective-permute-start.11) | collective-permute-done | bytes 294944 | tf_op jit(solution)/shard_map/ppermute | solution.py:409
  82.6 1.2 %partial_ratings.1 = f32[128,128]{1,0:T(8,128)S(1)} custom-call(bf16[128,128]{1,0:T(8,128)(2,1)S(1)} %summed_queries.1.q_ref, bf16[1152,128]{1,0:T(8,128)(2,1)S(1)} %get-tuple-element.30.refs_7_.refs_0_, bf16[1152,128]{1,0:T(8,128)(2,1)S(1)} %collective-permute-done.9.refs_1_, bf16[1152,128]{1,0:T(8,128)(2,1)S(1)} %collective-permute-done.10.refs_2_, ...), custom_call_target="tpu_custom_call" | custom-call | flops 33554432 | bytes 2097152 | tf_op jit(solution)/shard_map/partial_ratings/pallas_call | solution.py:366
  83.8 32.0 %all_to_all.21 = f32[128,1,128]{2,1,0:T(1,128)S(1)} all-to-all(f32[128,1,128]{2,1,0:T(1,128)S(1)} %bitcast.7), channel_id=1, replica_groups=mesh['groups'=2,'dp'=16,'tensor'=4,'seq'=2] {'dp','tensor','seq'}, dimensions={0} | all-to-all | bytes 131072 | tf_op jit(solution)/shard_map/all_to_all | solution.py:455
  115.8 0.9 shares.1
  (30 shorter events, 0.7 us)
Async XLA Ops:
  0.0 27.3 %copy-start = (bf16[128,4096]{1,0:T(8,128)(2,1)S(1)}, bf16[128,4096]{1,0:T(8,128)(2,1)}, u32[]{:S(2)}) copy-start(bf16[128,4096]{1,0:T(8,128)(2,1)} %weight_ref.1) | copy-start | bytes 3145732
  0.0 36.9 %copy-start.4 = (f32[4096]{0:T(1024)S(1)}, f32[4096]{0:T(1024)}, u32[]{:S(2)}) copy-start(f32[4096]{0:T(1024)} %param.15) | copy-start | bytes 49156
  2.8 42.2 %all-to-all-start = ((bf16[16,16,256]{2,1,0:T(8,128)(2,1)}), bf16[16,16,256]{2,1,0:T(8,128)(2,1)S(1)}, u32[]{:S(2)}, u32[]{:S(2)}) async-start(bf16[16,16,256]{2,1,0:T(8,128)(2,1)} %scoring_rows.1), calls=%async_computation | async-start | bytes 262144 | tf_op jit(solution)/shard_map/all_to_all | solution.py:425
  27.4 17.2 %collective-permute-start.4 = (bf16[128,512]{1,0:T(8,128)(2,1)S(1)}, bf16[128,512]{1,0:T(8,128)(2,1)S(1)}, u32[]{:S(2)}, u32[]{:S(2)}) collective-permute-start(bf16[128,512]{1,0:T(8,128)(2,1)S(1)} %get-tuple-element.21.after_ref.own_ref), channel_id=1, source_target_pairs={{1,9},{3,11},{5,13},{7,15},{9,1},{11,3},{13,5},{15,7},{17,25},{19,... | collective-permute-start | bytes 393224 | tf_op jit(solution)/shard_map/ppermute | solution.py:422
  30.5 14.1 %collective-permute-start.5 = (bf16[128,512]{1,0:T(8,128)(2,1)S(1)}, bf16[128,512]{1,0:T(8,128)(2,1)S(1)}, u32[]{:S(2)}, u32[]{:S(2)}) collective-permute-start(bf16[128,512]{1,0:T(8,128)(2,1)S(1)} %get-tuple-element.27), channel_id=1, source_target_pairs={{0,2},{1,11},{2,4},{3,13},{4,6},{5,15},{6,0},{7,9},{8,10},{9,3},{1... | collective-permute-start | bytes 393224 | tf_op jit(solution)/shard_map/ppermute | solution.py:422
  32.0 12.6 %collective-permute-start.6 = (bf16[128,512]{1,0:T(8,128)(2,1)S(1)}, bf16[128,512]{1,0:T(8,128)(2,1)S(1)}, u32[]{:S(2)}, u32[]{:S(2)}) collective-permute-start(bf16[128,512]{1,0:T(8,128)(2,1)S(1)} %get-tuple-element.28), channel_id=1, source_target_pairs={{0,4},{1,13},{2,6},{3,15},{4,0},{5,9},{6,2},{7,11},{8,12},{9,5},{1... | collective-permute-start | bytes 393224 | tf_op jit(solution)/shard_map/ppermute | solution.py:422
  35.6 9.1 %collective-permute-start.7 = (bf16[128,512]{1,0:T(8,128)(2,1)S(1)}, bf16[128,512]{1,0:T(8,128)(2,1)S(1)}, u32[]{:S(2)}, u32[]{:S(2)}) collective-permute-start(bf16[128,512]{1,0:T(8,128)(2,1)S(1)} %get-tuple-element.29), channel_id=1, source_target_pairs={{0,6},{1,15},{2,0},{3,9},{4,2},{5,11},{6,4},{7,13},{8,14},{9,7},{1... | collective-permute-start | bytes 393224 | tf_op jit(solution)/shard_map/ppermute | solution.py:422
  36.9 7.7 %copy-start.1 = (s32[16]{0:T(128)S(1)}, s32[16]{0:T(128)}, u32[]{:S(2)}) copy-start(s32[16]{0:T(128)} %refs_4_.1) | copy-start | bytes 196
  44.6 37.9 %copy-start.2 = (s32[16]{0:T(128)S(1)}, s32[16]{0:T(128)}, u32[]{:S(2)}) copy-start(s32[16]{0:T(128)} %refs_5_.1) | copy-start | bytes 196
  44.6 37.9 %copy-start.3 = (s32[16]{0:T(128)S(1)}, s32[16]{0:T(128)}, u32[]{:S(2)}) copy-start(s32[16]{0:T(128)} %refs_6_.1) | copy-start | bytes 196
  44.7 8.5 %collective-permute-start.8 = (bf16[4,128,512]{2,1,0:T(8,128)(2,1)S(1)}, bf16[4,128,512]{2,1,0:T(8,128)(2,1)S(1)}, u32[]{:S(2)}, u32[]{:S(2)}) collective-permute-start(bf16[4,128,512]{2,1,0:T(8,128)(2,1)S(1)} %stacked_weight.1.refs_5_), channel_id=1, source_target_pairs={{0,1},{1,0},{2,3},{3,2},{4,5},{5,4},{6,7},{7,6},{8,9},{9,8},{10,11... | collective-permute-start | bytes 1572872 | tf_op jit(solution)/shard_map/ppermute | solution.py:447
  45.0 8.3 %collective-permute-start = (bf16[16,16,256]{2,1,0:T(8,128)(2,1)S(1)}, bf16[16,16,256]{2,1,0:T(8,128)(2,1)S(1)}, u32[]{:S(2)}, u32[]{:S(2)}) collective-permute-start(bf16[16,16,256]{2,1,0:T(8,128)(2,1)S(1)} %all-to-all-done.refs_0_), channel_id=1, source_target_pairs={{0,2},{2,4},{4,6},{6,0},{1,3},{3,5},{5,7},{7,1},{8,10},{10,12},{12... | collective-permute-start | bytes 393224 | tf_op jit(solution)/shard_map/ppermute | solution.py:409
  45.6 7.7 %collective-permute-start.3 = (bf16[16,16,256]{2,1,0:T(8,128)(2,1)S(1)}, bf16[16,16,256]{2,1,0:T(8,128)(2,1)S(1)}, u32[]{:S(2)}, u32[]{:S(2)}) collective-permute-start(bf16[16,16,256]{2,1,0:T(8,128)(2,1)S(1)} %all-to-all-done.refs_0_), channel_id=1, source_target_pairs={{0,6},{2,0},{4,2},{6,4},{1,7},{3,1},{5,3},{7,5},{8,14},{10,8},{12,... | collective-permute-start | bytes 393224 | tf_op jit(solution)/shard_map/ppermute | solution.py:409
  47.8 4.7 %collective-permute-start.1 = (bf16[8,16,256]{2,1,0:T(8,128)(2,1)S(1)}, bf16[8,16,256]{2,1,0:T(8,128)(2,1)S(1)}, u32[]{:S(2)}, u32[]{:S(2)}) collective-permute-start(bf16[8,16,256]{2,1,0:T(8,128)(2,1)S(1)} %get-tuple-element.38), channel_id=1, source_target_pairs={{0,4},{2,6},{4,0},{6,2},{1,5},{3,7},{5,1},{7,3},{8,12},{10,14},{12... | collective-permute-start | bytes 196616 | tf_op jit(solution)/shard_map/ppermute | solution.py:409
  48.0 5.3 %collective-permute-start.2 = (bf16[8,16,256]{2,1,0:T(8,128)(2,1)S(1)}, bf16[8,16,256]{2,1,0:T(8,128)(2,1)S(1)}, u32[]{:S(2)}, u32[]{:S(2)}) collective-permute-start(bf16[8,16,256]{2,1,0:T(8,128)(2,1)S(1)} %get-tuple-element.37), channel_id=1, source_target_pairs={{0,4},{2,6},{4,0},{6,2},{1,5},{3,7},{5,1},{7,3},{8,12},{10,14},{12... | collective-permute-start | bytes 196616 | tf_op jit(solution)/shard_map/ppermute | solution.py:409
  54.4 24.0 %all-to-all-start.1 = ((bf16[16,4,16,128]{3,2,1,0:T(8,128)(2,1)}), bf16[16,4,16,128]{3,2,1,0:T(8,128)(2,1)S(1)}, u32[]{:S(2)}, u32[]{:S(2)}) async-start(bf16[16,4,16,128]{3,2,1,0:T(8,128)(2,1)} %partial_queries.1), calls=%async_computation.1 | async-start | bytes 524288 | tf_op jit(solution)/shard_map/all_to_all | solution.py:452
  65.9 12.6 %collective-permute-start.10 = (bf16[1152,128]{1,0:T(8,128)(2,1)S(1)}, bf16[1152,128]{1,0:T(8,128)(2,1)S(1)}, u32[]{:S(2)}, u32[]{:S(2)}) collective-permute-start(bf16[1152,128]{1,0:T(8,128)(2,1)S(1)} %get-tuple-element.35), channel_id=1, source_target_pairs={{0,4},{2,6},{4,0},{6,2},{1,5},{3,7},{5,1},{7,3},{8,12},{10,14},{12... | collective-permute-start | bytes 884744 | tf_op jit(solution)/shard_map/ppermute | solution.py:409
  68.3 14.3 %collective-permute-start.11 = (bf16[1152,128]{1,0:T(8,128)(2,1)S(1)}, bf16[1152,128]{1,0:T(8,128)(2,1)S(1)}, u32[]{:S(2)}, u32[]{:S(2)}) collective-permute-start(bf16[1152,128]{1,0:T(8,128)(2,1)S(1)} %get-tuple-element.36), channel_id=1, source_target_pairs={{0,6},{2,0},{4,2},{6,4},{1,7},{3,1},{5,3},{7,5},{8,14},{10,8},{12,... | collective-permute-start | bytes 884744 | tf_op jit(solution)/shard_map/ppermute | solution.py:409
  69.5 13.0 %collective-permute-start.9 = (bf16[1152,128]{1,0:T(8,128)(2,1)S(1)}, bf16[1152,128]{1,0:T(8,128)(2,1)S(1)}, u32[]{:S(2)}, u32[]{:S(2)}) collective-permute-start(bf16[1152,128]{1,0:T(8,128)(2,1)S(1)} %get-tuple-element.34), channel_id=1, source_target_pairs={{0,2},{2,4},{4,6},{6,0},{1,3},{3,5},{5,7},{7,1},{8,10},{10,12},{12... | collective-permute-start | bytes 884744 | tf_op jit(solution)/shard_map/ppermute | solution.py:409

commit v7 on v6

--- a/solution.py
+++ b/solution.py
@@ -89,7 +89,7 @@
 
 def cut_kernel(n_tensor, weight_ref, *out_refs):
     t, side = lax.axis_index("tensor"), lax.axis_index("dp") % 2
-    side = (side + lax.axis_index("seq")) % 2
+    side = (side + 1 - lax.axis_index("seq")) % 2
     part = out_refs[0].shape[1]
     for s in range(n_tensor):
         at = pl.multiple_of((2 * ((t + s) % n_tensor) + side) * part, part)
@@ -112,7 +112,7 @@
 
 def stack_kernel(own_ref, *refs):
     out_ref = refs[-1]
-    first = lax.axis_index("seq") == 0
+    first = lax.axis_index("seq") == 1
     out_ref[0] = jnp.where(first, own_ref[...].astype(F32), refs[0][...].astype(F32)).astype(BF)
     for s in range(1, len(refs) - 1):
         out_ref[s] = refs[s][...]
@@ -244,7 +244,7 @@
     seq = lax.axis_index("seq")
     columns, weights = [], []
     for s in range(n_tensor):
-        for side, w_ref in ((seq, here_ref), (1 - seq, there_ref)):
+        for side, w_ref in ((1 - seq, here_ref), (seq, there_ref)):
             at = pl.multiple_of(side * depth, depth)
             parts = [
                 x_ref[:, :, pl.ds(at, depth)].reshape(-1, depth)
@@ -412,12 +412,12 @@
         pairs = [
             (
                 (d * n_tensor + i) * n_seq + c,
-                ((d ^ c) * n_tensor + (i + s) % n_tensor) * n_seq + c,
+                ((d ^ (1 - c)) * n_tensor + (i + s) % n_tensor) * n_seq + c,
             )
             for d in range(n_dp)
             for i in range(n_tensor)
             for c in range(n_seq)
-            if s or c
+            if s or c == 0
         ]
         return lax.ppermute(value, ("dp", "tensor", "seq"), pairs)
 
@@ -441,8 +441,7 @@
     moved, *kv = lax.optimization_barrier((moved, *kv))
     pieces = [[moved]]
     for s in range(1, n_tensor):
-        parts = jnp.split(moved, 2) if 2 * s == n_tensor else [moved]
-        pieces.append([over_tensor(part, s) for part in parts])
+        pieces.append([over_tensor(moved, s)])
     here = stacked_weight(cut[0], arrived_weight)
     there = lax.ppermute(here, "seq", [(i, (i + 1) % n_seq) for i in range(n_seq)])
     queries = partial_queries(pieces, here, there, kv[0])

time: 117 us -> 120 us (1.026)
  waiting for transfers between devices: 14.9 us -> 18.8 us
    ppermute x1, starting transfers between devices: 0.14 us -> 5.48 us  [shards(): lax.ppermute(here, 'seq', [(i, (i + 1) % n_seq) for i in range(n_seq)])]
    ppermute x7 -> x6, waiting for transfers between devices: 6.29 us -> 10.9 us  [over_tensor(): lax.ppermute(value, 'tensor', [(i, (i + s) % n_tensor) for i in range(n_t...]
    ppermute x4, starting transfers between devices: 9.22 us -> 5.87 us  [weight_piece(): return lax.ppermute(value, ('dp', 'tensor', 'seq'), pairs)]
    ppermute x7 -> x6, starting transfers between devices: 9.76 us -> 7.79 us  [over_tensor(): lax.ppermute(value, 'tensor', [(i, (i + s) % n_tensor) for i in range(n_t...]
  transfers between devices with their start and end apart: 14 -> 13, of which waited for: 4 -> 5; matrix products, arithmetic and copies ran while one was open for 0% -> 0% of each run, Pallas kernels for 7% -> 7%
where the time goes in v7:
time: 120 us
  starting transfers between devices  55.4 us (46%)
  blocking collectives  31.1 us (26%)
  waiting for transfers between devices  18.8 us (16%)
  Pallas kernels  14 us (12%)
    all_to_all x1, blocking collectives, shards(): gathered = lax.all_to_all(rated, ('dp', 'tensor', 'seq'), 0, 0, tiled=True)  31.1 us
    all_to_all x1, starting transfers between devices, shards(): moved = lax.all_to_all(rows, 'dp', 0, 0, tiled=True)  24.5 us
    all_to_all x1, starting transfers between devices, shards(): arrived = lax.all_to_all(queries, 'dp', 0, 0, tiled=True)  11.8 us
    ppermute x6, waiting for transfers between devices, over_tensor(): lax.ppermute(value, 'tensor', [(i, (i + s) % n_tensor) for i in range(n_t...  10.9 us
    all_to_all x1, waiting for transfers between devices, shards(): arrived = lax.all_to_all(queries, 'dp', 0, 0, tiled=True)  7.84 us
    ppermute x6, starting transfers between devices, over_tensor(): lax.ppermute(value, 'tensor', [(i, (i + s) % n_tensor) for i in range(n_t...  7.79 us
    pallas_call x1, Pallas kernels, keys_and_values(): pl.pallas_call(functools.partial(kv_kernel, n_tensor), in_specs=[HBM, HBM...  7.66 us
    ppermute x4, starting transfers between devices, weight_piece(): return lax.ppermute(value, ('dp', 'tensor', 'seq'), pairs)  5.87 us
  transfers between devices with their start and end apart: 13, of which 5 were waited for; matrix products, arithmetic and copies ran while one was open for 0% of the time, Pallas kernels for 7%

profile of v7, /device:TPU:33, one launch (start us, length us, event | category | flops | bytes accessed | tf_op | source)
XLA Modules:
  0.0 119.9 jit_solution(15146872315963994536)
XLA Ops:
  0.0 2.8 %scoring_rows.1 = bf16[16,16,256]{2,1,0:T(8,128)(2,1)} custom-call(s32[16]{0:T(128)} %refs_4_.1, bf16[16,64,2048]{2,1,0:T(8,128)(2,1)} %hidden_ref.1), custom_call_target="tpu_custom_call" | custom-call | flops 16777216 | bytes 1048576 | tf_op jit(solution)/shard_map/scoring_rows/pallas_call | solution.py:75
  2.8 24.5 %all-to-all-start = ((bf16[16,16,256]{2,1,0:T(8,128)(2,1)}), bf16[16,16,256]{2,1,0:T(8,128)(2,1)S(1)}, u32[]{:S(2)}, u32[]{:S(2)}) async-start(bf16[16,16,256]{2,1,0:T(8,128)(2,1)} %scoring_rows.1), calls=%async_computation | async-start | bytes 262144 | tf_op jit(solution)/shard_map/all_to_all | solution.py:425
  27.4 0.7 collective-permute-start.3
  28.1 1.5 %collective-permute-start.4 = (bf16[128,512]{1,0:T(8,128)(2,1)S(1)}, bf16[128,512]{1,0:T(8,128)(2,1)S(1)}, u32[]{:S(2)}, u32[]{:S(2)}) collective-permute-start(bf16[128,512]{1,0:T(8,128)(2,1)S(1)} %get-tuple-element.27), channel_id=1, source_target_pairs={{0,10},{1,3},{2,12},{3,5},{4,14},{5,7},{6,8},{7,1},{8,2},{9,11},{1... | collective-permute-start | bytes 393224 | tf_op jit(solution)/shard_map/ppermute | solution.py:422
  29.6 2.7 %collective-permute-start.5 = (bf16[128,512]{1,0:T(8,128)(2,1)S(1)}, bf16[128,512]{1,0:T(8,128)(2,1)S(1)}, u32[]{:S(2)}, u32[]{:S(2)}) collective-permute-start(bf16[128,512]{1,0:T(8,128)(2,1)S(1)} %get-tuple-element.28), channel_id=1, source_target_pairs={{0,12},{1,5},{2,14},{3,7},{4,8},{5,1},{6,10},{7,3},{8,4},{9,13},{1... | collective-permute-start | bytes 393224 | tf_op jit(solution)/shard_map/ppermute | solution.py:422
  32.3 1.0 collective-permute-start.6
  33.3 0.1 fusion.2
  33.6 7.7 %keys_and_values.1 = (bf16[1152,128]{1,0:T(8,128)(2,1)S(1)}, bf16[1152,128]{1,0:T(8,128)(2,1)S(1)}, bf16[1152,128]{1,0:T(8,128)(2,1)S(1)}, bf16[1152,128]{1,0:T(8,128)(2,1)S(1)}) custom-call(bf16[1024,2048]{1,0:T(8,128)(2,1)} %bitcast.9, bf16[2048,512]{1,0:T(8,128)(2,1)} %k_ref.1, bf16[2048,512]{1,0:T(8,128)(2,1)} %v_ref.1, f32[32,128]{1,0:T(8,128)S(1)} %bitcast.8, ...), custom_call_target="tpu_custom_call" | custom-call | flops 2684354560 | bytes 9437184 | tf_op jit(solution)/shard_map/keys_and_values/pallas_call | solution.py:220
  41.4 5.5 %collective-permute-start.7 = (bf16[4,128,512]{2,1,0:T(8,128)(2,1)S(1)}, bf16[4,128,512]{2,1,0:T(8,128)(2,1)S(1)}, u32[]{:S(2)}, u32[]{:S(2)}) collective-permute-start(bf16[4,128,512]{2,1,0:T(8,128)(2,1)S(1)} %stacked_weight.1.refs_4_), channel_id=1, source_target_pairs={{0,1},{1,0},{2,3},{3,2},{4,5},{5,4},{6,7},{7,6},{8,9},{9,8},{10,11... | collective-permute-start | bytes 1572872 | tf_op jit(solution)/shard_map/ppermute | solution.py:446
  46.8 0.6 collective-permute-start
  47.4 0.7 collective-permute-start.1
  48.2 1.8 %collective-permute-start.2 = (bf16[16,16,256]{2,1,0:T(8,128)(2,1)S(1)}, bf16[16,16,256]{2,1,0:T(8,128)(2,1)S(1)}, u32[]{:S(2)}, u32[]{:S(2)}) collective-permute-start(bf16[16,16,256]{2,1,0:T(8,128)(2,1)S(1)} %all-to-all-done.refs_0_), channel_id=1, source_target_pairs={{0,6},{2,0},{4,2},{6,4},{1,7},{3,1},{5,3},{7,5},{8,14},{10,8},{12,... | collective-permute-start | bytes 393224 | tf_op jit(solution)/shard_map/ppermute | solution.py:409
  50.2 5.8 %collective-permute-done.refs_1_ = bf16[16,16,256]{2,1,0:T(8,128)(2,1)S(1)} collective-permute-done((bf16[16,16,256]{2,1,0:T(8,128)(2,1)S(1)}, bf16[16,16,256]{2,1,0:T(8,128)(2,1)S(1)}, u32[]{:S(2)}, u32[]{:S(2)}) %collective-permute-start) | collective-permute-done | bytes 131104 | tf_op jit(solution)/shard_map/ppermute | solution.py:409
  56.0 0.3 collective-permute-done.2.refs_3_
  56.3 1.2 partial_queries.1
  57.5 11.8 %all-to-all-start.1 = ((bf16[16,4,16,128]{3,2,1,0:T(8,128)(2,1)}), bf16[16,4,16,128]{3,2,1,0:T(8,128)(2,1)S(1)}, u32[]{:S(2)}, u32[]{:S(2)}) async-start(bf16[16,4,16,128]{3,2,1,0:T(8,128)(2,1)} %partial_queries.1), calls=%async_computation.1 | async-start | bytes 524288 | tf_op jit(solution)/shard_map/all_to_all | solution.py:451
  69.2 3.2 %collective-permute-start.10 = (bf16[1152,128]{1,0:T(8,128)(2,1)S(1)}, bf16[1152,128]{1,0:T(8,128)(2,1)S(1)}, u32[]{:S(2)}, u32[]{:S(2)}) collective-permute-start(bf16[1152,128]{1,0:T(8,128)(2,1)S(1)} %get-tuple-element.36), channel_id=1, source_target_pairs={{0,6},{2,0},{4,2},{6,4},{1,7},{3,1},{5,3},{7,5},{8,14},{10,8},{12,... | collective-permute-start | bytes 884744 | tf_op jit(solution)/shard_map/ppermute | solution.py:409
  72.4 1.5 %collective-permute-start.9 = (bf16[1152,128]{1,0:T(8,128)(2,1)S(1)}, bf16[1152,128]{1,0:T(8,128)(2,1)S(1)}, u32[]{:S(2)}, u32[]{:S(2)}) collective-permute-start(bf16[1152,128]{1,0:T(8,128)(2,1)S(1)} %get-tuple-element.35), channel_id=1, source_target_pairs={{0,4},{2,6},{4,0},{6,2},{1,5},{3,7},{5,1},{7,3},{8,12},{10,14},{12... | collective-permute-start | bytes 884744 | tf_op jit(solution)/shard_map/ppermute | solution.py:409
  73.9 7.8 %all-to-all-done.1.q_ref = bf16[16,4,16,128]{3,2,1,0:T(8,128)(2,1)S(1)} async-done(((bf16[16,4,16,128]{3,2,1,0:T(8,128)(2,1)}), bf16[16,4,16,128]{3,2,1,0:T(8,128)(2,1)S(1)}, u32[]{:S(2)}, u32[]{:S(2)}) %all-to-all-start.1) | async-done | bytes 262176 | tf_op jit(solution)/shard_map/all_to_all | solution.py:451
  81.9 2.3 %collective-permute-done.10.refs_3_ = bf16[1152,128]{1,0:T(8,128)(2,1)S(1)} collective-permute-done((bf16[1152,128]{1,0:T(8,128)(2,1)S(1)}, bf16[1152,128]{1,0:T(8,128)(2,1)S(1)}, u32[]{:S(2)}, u32[]{:S(2)}) %collective-permute-start.10) | collective-permute-done | bytes 294944 | tf_op jit(solution)/shard_map/ppermute | solution.py:409
  84.2 2.4 %collective-permute-done.9.refs_2_ = bf16[1152,128]{1,0:T(8,128)(2,1)S(1)} collective-permute-done((bf16[1152,128]{1,0:T(8,128)(2,1)S(1)}, bf16[1152,128]{1,0:T(8,128)(2,1)S(1)}, u32[]{:S(2)}, u32[]{:S(2)}) %collective-permute-start.9) | collective-permute-done | bytes 294944 | tf_op jit(solution)/shard_map/ppermute | solution.py:409
  86.6 1.2 %partial_ratings.1 = f32[128,128]{1,0:T(8,128)S(1)} custom-call(bf16[128,128]{1,0:T(8,128)(2,1)S(1)} %summed_queries.1.q_ref, bf16[1152,128]{1,0:T(8,128)(2,1)S(1)} %get-tuple-element.30.refs_6_.refs_0_, bf16[1152,128]{1,0:T(8,128)(2,1)S(1)} %collective-permute-done.8.refs_1_, bf16[1152,128]{1,0:T(8,128)(2,1)S(1)} %collective-permute-done.9.refs_2_, ...), custom_call_target="tpu_custom_call" | custom-call | flops 33554432 | bytes 2097152 | tf_op jit(solution)/shard_map/partial_ratings/pallas_call | solution.py:366
  87.9 31.1 %all_to_all.21 = f32[128,1,128]{2,1,0:T(1,128)S(1)} all-to-all(f32[128,1,128]{2,1,0:T(1,128)S(1)} %bitcast.7), channel_id=1, replica_groups=mesh['groups'=2,'dp'=16,'tensor'=4,'seq'=2] {'dp','tensor','seq'}, dimensions={0} | all-to-all | bytes 131072 | tf_op jit(solution)/shard_map/all_to_all | solution.py:454
  119.0 0.9 shares.1
  (27 shorter events, 0.6 us)
Async XLA Ops:
  0.0 27.3 %copy-start = (bf16[128,4096]{1,0:T(8,128)(2,1)S(1)}, bf16[128,4096]{1,0:T(8,128)(2,1)}, u32[]{:S(2)}) copy-start(bf16[128,4096]{1,0:T(8,128)(2,1)} %weight_ref.1) | copy-start | bytes 3145732
  0.0 33.5 %copy-start.4 = (f32[4096]{0:T(1024)S(1)}, f32[4096]{0:T(1024)}, u32[]{:S(2)}) copy-start(f32[4096]{0:T(1024)} %param.15) | copy-start | bytes 49156
  2.8 44.0 %all-to-all-start = ((bf16[16,16,256]{2,1,0:T(8,128)(2,1)}), bf16[16,16,256]{2,1,0:T(8,128)(2,1)S(1)}, u32[]{:S(2)}, u32[]{:S(2)}) async-start(bf16[16,16,256]{2,1,0:T(8,128)(2,1)} %scoring_rows.1), calls=%async_computation | async-start | bytes 262144 | tf_op jit(solution)/shard_map/all_to_all | solution.py:425
  27.4 13.8 %collective-permute-start.3 = (bf16[128,512]{1,0:T(8,128)(2,1)S(1)}, bf16[128,512]{1,0:T(8,128)(2,1)S(1)}, u32[]{:S(2)}, u32[]{:S(2)}) collective-permute-start(bf16[128,512]{1,0:T(8,128)(2,1)S(1)} %get-tuple-element.21.after_ref.own_ref), channel_id=1, source_target_pairs={{0,8},{2,10},{4,12},{6,14},{8,0},{10,2},{12,4},{14,6},{16,24},{18,... | collective-permute-start | bytes 393224 | tf_op jit(solution)/shard_map/ppermute | solution.py:422
  28.1 13.2 %collective-permute-start.4 = (bf16[128,512]{1,0:T(8,128)(2,1)S(1)}, bf16[128,512]{1,0:T(8,128)(2,1)S(1)}, u32[]{:S(2)}, u32[]{:S(2)}) collective-permute-start(bf16[128,512]{1,0:T(8,128)(2,1)S(1)} %get-tuple-element.27), channel_id=1, source_target_pairs={{0,10},{1,3},{2,12},{3,5},{4,14},{5,7},{6,8},{7,1},{8,2},{9,11},{1... | collective-permute-start | bytes 393224 | tf_op jit(solution)/shard_map/ppermute | solution.py:422
  29.6 11.7 %collective-permute-start.5 = (bf16[128,512]{1,0:T(8,128)(2,1)S(1)}, bf16[128,512]{1,0:T(8,128)(2,1)S(1)}, u32[]{:S(2)}, u32[]{:S(2)}) collective-permute-start(bf16[128,512]{1,0:T(8,128)(2,1)S(1)} %get-tuple-element.28), channel_id=1, source_target_pairs={{0,12},{1,5},{2,14},{3,7},{4,8},{5,1},{6,10},{7,3},{8,4},{9,13},{1... | collective-permute-start | bytes 393224 | tf_op jit(solution)/shard_map/ppermute | solution.py:422
  32.3 9.0 %collective-permute-start.6 = (bf16[128,512]{1,0:T(8,128)(2,1)S(1)}, bf16[128,512]{1,0:T(8,128)(2,1)S(1)}, u32[]{:S(2)}, u32[]{:S(2)}) collective-permute-start(bf16[128,512]{1,0:T(8,128)(2,1)S(1)} %get-tuple-element.29), channel_id=1, source_target_pairs={{0,14},{1,7},{2,8},{3,1},{4,10},{5,3},{6,12},{7,5},{8,6},{9,15},{1... | collective-permute-start | bytes 393224 | tf_op jit(solution)/shard_map/ppermute | solution.py:422
  33.6 13.3 %copy-start.1 = (s32[16]{0:T(128)S(1)}, s32[16]{0:T(128)}, u32[]{:S(2)}) copy-start(s32[16]{0:T(128)} %refs_4_.1) | copy-start | bytes 196
  41.2 45.4 %copy-start.2 = (s32[16]{0:T(128)S(1)}, s32[16]{0:T(128)}, u32[]{:S(2)}) copy-start(s32[16]{0:T(128)} %refs_5_.1) | copy-start | bytes 196
  41.2 45.4 %copy-start.3 = (s32[16]{0:T(128)S(1)}, s32[16]{0:T(128)}, u32[]{:S(2)}) copy-start(s32[16]{0:T(128)} %refs_6_.1) | copy-start | bytes 196
  41.4 15.0 %collective-permute-start.7 = (bf16[4,128,512]{2,1,0:T(8,128)(2,1)S(1)}, bf16[4,128,512]{2,1,0:T(8,128)(2,1)S(1)}, u32[]{:S(2)}, u32[]{:S(2)}) collective-permute-start(bf16[4,128,512]{2,1,0:T(8,128)(2,1)S(1)} %stacked_weight.1.refs_4_), channel_id=1, source_target_pairs={{0,1},{1,0},{2,3},{3,2},{4,5},{5,4},{6,7},{7,6},{8,9},{9,8},{10,11... | collective-permute-start | bytes 1572872 | tf_op jit(solution)/shard_map/ppermute | solution.py:446
  46.8 9.1 %collective-permute-start = (bf16[16,16,256]{2,1,0:T(8,128)(2,1)S(1)}, bf16[16,16,256]{2,1,0:T(8,128)(2,1)S(1)}, u32[]{:S(2)}, u32[]{:S(2)}) collective-permute-start(bf16[16,16,256]{2,1,0:T(8,128)(2,1)S(1)} %all-to-all-done.refs_0_), channel_id=1, source_target_pairs={{0,2},{2,4},{4,6},{6,0},{1,3},{3,5},{5,7},{7,1},{8,10},{10,12},{12... | collective-permute-start | bytes 393224 | tf_op jit(solution)/shard_map/ppermute | solution.py:409
  47.4 8.6 %collective-permute-start.1 = (bf16[16,16,256]{2,1,0:T(8,128)(2,1)S(1)}, bf16[16,16,256]{2,1,0:T(8,128)(2,1)S(1)}, u32[]{:S(2)}, u32[]{:S(2)}) collective-permute-start(bf16[16,16,256]{2,1,0:T(8,128)(2,1)S(1)} %all-to-all-done.refs_0_), channel_id=1, source_target_pairs={{0,4},{2,6},{4,0},{6,2},{1,5},{3,7},{5,1},{7,3},{8,12},{10,14},{12... | collective-permute-start | bytes 393224 | tf_op jit(solution)/shard_map/ppermute | solution.py:409
  48.2 8.2 %collective-permute-start.2 = (bf16[16,16,256]{2,1,0:T(8,128)(2,1)S(1)}, bf16[16,16,256]{2,1,0:T(8,128)(2,1)S(1)}, u32[]{:S(2)}, u32[]{:S(2)}) collective-permute-start(bf16[16,16,256]{2,1,0:T(8,128)(2,1)S(1)} %all-to-all-done.refs_0_), channel_id=1, source_target_pairs={{0,6},{2,0},{4,2},{6,4},{1,7},{3,1},{5,3},{7,5},{8,14},{10,8},{12,... | collective-permute-start | bytes 393224 | tf_op jit(solution)/shard_map/ppermute | solution.py:409
  57.5 24.3 %all-to-all-start.1 = ((bf16[16,4,16,128]{3,2,1,0:T(8,128)(2,1)}), bf16[16,4,16,128]{3,2,1,0:T(8,128)(2,1)S(1)}, u32[]{:S(2)}, u32[]{:S(2)}) async-start(bf16[16,4,16,128]{3,2,1,0:T(8,128)(2,1)} %partial_queries.1), calls=%async_computation.1 | async-start | bytes 524288 | tf_op jit(solution)/shard_map/all_to_all | solution.py:451
  69.2 15.0 %collective-permute-start.10 = (bf16[1152,128]{1,0:T(8,128)(2,1)S(1)}, bf16[1152,128]{1,0:T(8,128)(2,1)S(1)}, u32[]{:S(2)}, u32[]{:S(2)}) collective-permute-start(bf16[1152,128]{1,0:T(8,128)(2,1)S(1)} %get-tuple-element.36), channel_id=1, source_target_pairs={{0,6},{2,0},{4,2},{6,4},{1,7},{3,1},{5,3},{7,5},{8,14},{10,8},{12,... | collective-permute-start | bytes 884744 | tf_op jit(solution)/shard_map/ppermute | solution.py:409
  72.4 11.8 %collective-permute-start.8 = (bf16[1152,128]{1,0:T(8,128)(2,1)S(1)}, bf16[1152,128]{1,0:T(8,128)(2,1)S(1)}, u32[]{:S(2)}, u32[]{:S(2)}) collective-permute-start(bf16[1152,128]{1,0:T(8,128)(2,1)S(1)} %get-tuple-element.34), channel_id=1, source_target_pairs={{0,2},{2,4},{4,6},{6,0},{1,3},{3,5},{5,7},{7,1},{8,10},{10,12},{12... | collective-permute-start | bytes 884744 | tf_op jit(solution)/shard_map/ppermute | solution.py:409
  72.4 14.2 %collective-permute-start.9 = (bf16[1152,128]{1,0:T(8,128)(2,1)S(1)}, bf16[1152,128]{1,0:T(8,128)(2,1)S(1)}, u32[]{:S(2)}, u32[]{:S(2)}) collective-permute-start(bf16[1152,128]{1,0:T(8,128)(2,1)S(1)} %get-tuple-element.35), channel_id=1, source_target_pairs={{0,4},{2,6},{4,0},{6,2},{1,5},{3,7},{5,1},{7,3},{8,12},{10,14},{12... | collective-permute-start | bytes 884744 | tf_op jit(solution)/shard_map/ppermute | solution.py:409
